TPU v7x, 8 devices: a whole 2x2x1 slice. The times are simulated.
8 devices in a mesh: dp: 1 (over z), tp: 2 (over y), cp: 4 (over x, core).
Axes of the slice: x: 2, y: 2, z: 1, core: 2. Of those that a mesh axis runs over, the one named last changes fastest.
Arguments:
- x: bfloat16 [2048, 4096], P(('dp', 'cp'))
- attn_gain: bfloat16 [4096], replicated
- w_q: bfloat16 [4096, 4096], P(None, 'tp')
- w_k: bfloat16 [4096, 1024], P(None, 'tp')
- w_v: bfloat16 [4096, 1024], P(None, 'tp')
- w_o: bfloat16 [4096, 4096], P('tp')
- mlp_gain: bfloat16 [4096], replicated
- w_gate: bfloat16 [4096, 12288], P(None, 'tp')
- w_up: bfloat16 [4096, 12288], P(None, 'tp')
- w_down: bfloat16 [12288, 4096], P('tp')
Outputs:
- output 1: bfloat16 [2048, 4096], P(('dp', 'cp'))
- output 2: bfloat16 [2048, 8, 128], P(('dp', 'cp'), 'tp')
- output 3: bfloat16 [2048, 8, 128], P(('dp', 'cp'), 'tp')
All inputs are finite; a program needn't handle non-finite values.
Results may differ from a plain program's by a relative error of at most 0.0129251.
Values are sent between devices in bfloat16 or wider.
A program may use at most 1 GiB of HBM per device.

v0:
```python
import math
import jax
import jax.numpy as jnp
from jax import lax
from jax.sharding import PartitionSpec as P

HEAD_DIM = 128
ROPE_THETA = 1000000.0
NORM_EPS = 1e-5
MASK_VALUE = -1e30
TILE_CAP = 512


def rms_norm(rows, gain):
    wide = rows.astype(jnp.float32)
    inv_rms = lax.rsqrt(jnp.mean(wide * wide, axis=-1, keepdims=True) + NORM_EPS)
    return (wide * inv_rms * gain.astype(jnp.float32)).astype(jnp.bfloat16)


def rope_tables(positions):
    inv_freq = jnp.asarray(ROPE_THETA, jnp.float32) ** (-jnp.arange(0, HEAD_DIM, 2, dtype=jnp.float32) / HEAD_DIM)
    angles = positions.astype(jnp.float32)[:, None] * inv_freq[None, :]
    return jnp.cos(angles), jnp.sin(angles)


def apply_rope(heads, cos_b, sin_b):
    half = heads.shape[-1] // 2
    wide = heads.astype(jnp.float32)
    first = wide[..., :half]
    second = wide[..., half:]
    return jnp.concatenate([first * cos_b - second * sin_b, second * cos_b + first * sin_b], axis=-1).astype(jnp.bfloat16)


def attend_tiles(state, queries, key_rows, value_rows, key_start, q_pos, n_tiles, tile):
    def tile_step(tile_idx, carry):
        run_max, run_sum, weighted = carry
        k_tile = lax.dynamic_slice_in_dim(key_rows, tile_idx * tile, tile, axis=0)
        v_tile = lax.dynamic_slice_in_dim(value_rows, tile_idx * tile, tile, axis=0)
        k_pos = key_start + tile_idx * tile + jnp.arange(tile)
        scores = jnp.einsum('qkgd,skd->kgqs', queries, k_tile, preferred_element_type=jnp.float32) * (HEAD_DIM ** -0.5)
        scores = jnp.where(k_pos[None, :] <= q_pos[:, None], scores, MASK_VALUE)
        new_max = jnp.maximum(run_max, jnp.max(scores, axis=-1))
        rescale = jnp.exp(run_max - new_max)
        exp_scores = jnp.exp(scores - new_max[..., None])
        new_sum = run_sum * rescale + jnp.sum(exp_scores, axis=-1)
        new_weighted = weighted * rescale[..., None] + jnp.einsum('kgqs,skd->kgqd', exp_scores.astype(jnp.bfloat16), v_tile, preferred_element_type=jnp.float32)
        return new_max, new_sum, new_weighted
    return lax.fori_loop(0, n_tiles, tile_step, state)


def solution(mesh):
    cp_size = mesh.shape['cp']
    shift_pairs = [(source, (source + 1) % cp_size) for source in range(cp_size)]
    row_spec = P(('dp', 'cp'), None)
    cache_spec = P(('dp', 'cp'), 'tp', None)
    col_spec = P(None, 'tp')
    split_rows = P('tp', None)
    vec_spec = P(None)

    def local_layer(x, attn_gain, w_q, w_k, w_v, w_o, mlp_gain, w_gate, w_up, w_down):
        tok_dev = x.shape[0]
        kv_local = w_k.shape[1] // HEAD_DIM
        groups = w_q.shape[1] // w_k.shape[1]
        cp_index = lax.axis_index('cp')
        q_pos = cp_index * tok_dev + jnp.arange(tok_dev)
        cos_tab, sin_tab = rope_tables(q_pos)
        normed = rms_norm(x, attn_gain)
        queries = jnp.dot(normed, w_q, preferred_element_type=jnp.float32).astype(jnp.bfloat16).reshape(tok_dev, kv_local, groups, HEAD_DIM)
        keys = jnp.dot(normed, w_k, preferred_element_type=jnp.float32).astype(jnp.bfloat16).reshape(tok_dev, kv_local, HEAD_DIM)
        values = jnp.dot(normed, w_v, preferred_element_type=jnp.float32).astype(jnp.bfloat16).reshape(tok_dev, kv_local, HEAD_DIM)
        queries = apply_rope(queries, cos_tab[:, None, None, :], sin_tab[:, None, None, :])
        keys = apply_rope(keys, cos_tab[:, None, :], sin_tab[:, None, :])
        tile = math.gcd(tok_dev, TILE_CAP)
        n_tiles = tok_dev // tile
        stat_shape = (kv_local, groups, tok_dev)
        state = (jnp.full(stat_shape, MASK_VALUE, jnp.float32), jnp.zeros(stat_shape, jnp.float32), jnp.zeros(stat_shape + (HEAD_DIM,), jnp.float32))
        state = attend_tiles(state, queries, keys, values, cp_index * tok_dev, q_pos, n_tiles, tile)

        def shift_step(step, carry):
            held, state_in = carry
            held = lax.ppermute(held, 'cp', shift_pairs)
            source = cp_index - step

            def use_block(current):
                return attend_tiles(current, queries, held[0], held[1], source * tok_dev, q_pos, n_tiles, tile)

            def keep_state(current):
                return current

            state_out = lax.cond(step <= cp_index, use_block, keep_state, state_in)
            return held, state_out

        state = lax.fori_loop(1, cp_size, shift_step, ((keys, values), state))[1]
        attn_heads = (state[2] / state[1][..., None]).astype(jnp.bfloat16)
        attn_rows = jnp.transpose(attn_heads, (2, 0, 1, 3)).reshape(tok_dev, kv_local * groups * HEAD_DIM)
        attn_part = jnp.dot(attn_rows, w_o, preferred_element_type=jnp.float32).astype(jnp.bfloat16)
        attn_total = lax.psum(attn_part, 'tp')
        hidden = (x.astype(jnp.float32) + attn_total.astype(jnp.float32)).astype(jnp.bfloat16)
        normed_mlp = rms_norm(hidden, mlp_gain)
        gate_proj = jnp.dot(normed_mlp, w_gate, preferred_element_type=jnp.float32)
        up_proj = jnp.dot(normed_mlp, w_up, preferred_element_type=jnp.float32)
        activated = (jax.nn.silu(gate_proj) * up_proj).astype(jnp.bfloat16)
        down_part = jnp.dot(activated, w_down, preferred_element_type=jnp.float32).astype(jnp.bfloat16)
        down_total = lax.psum(down_part, 'tp')
        x_out = (hidden.astype(jnp.float32) + down_total.astype(jnp.float32)).astype(jnp.bfloat16)
        return x_out, keys, values

    return jax.shard_map(local_layer, mesh=mesh,
                         in_specs=(row_spec, vec_spec, col_spec, col_spec, col_spec, split_rows, vec_spec, col_spec, col_spec, split_rows),
                         out_specs=(row_spec, cache_spec, cache_spec), check_vma=False)
```

profile of v0, /device:TPU:3, one launch (start us, length us, event | category | flops | bytes accessed | tf_op | source)
XLA Modules:
  0.0 561.1 jit_solution(11988192790029674665)
XLA Ops:
  7.2 0.0 all-reduce.3.cloned.1.call-start
  7.2 0.7 convert_element_type.90
  7.9 3.1 fusion.18
  11.0 5.9 %convolution_convert_fusion.4 = bf16[512,512]{0,1:T(8,128)(2,1)S(1)} fusion(bf16[4096,512]{1,0:T(8,128)(2,1)} %param.17, bf16[512,4096]{1,0:T(8,128)(2,1)} %param.14, f32[4096]{0:T(1024)S(1)} %convert_element_type.90, f32[512]{0:T(512)S(1)} %add_rsqrt_fusion.1), kind=kOutput, calls=%fused_computation.51 | convolution fusion | flops 2156134400 | bytes 8931328 | tf_op jit(solution)/shard_map/dot_general | solution.py:69
  17.0 0.1 fusion.48
  17.1 0.3 copy.42
  17.4 0.3 copy.43
  17.8 15.0 %fusion.29 = f32[512,2048]{1,0:T(8,128)} fusion(bf16[4096,2048]{1,0:T(8,128)(2,1)} %param.16, bf16[512,4096]{1,0:T(8,128)(2,1)} %param.14, f32[4096]{0:T(1024)S(1)} %convert_element_type.90, f32[512]{0:T(512)S(1)} %add_rsqrt_fusion.1), kind=kOutput, calls=%fused_computation.47 | convolution fusion | flops 8600420352 | bytes 25184256 | tf_op jit(solution)/shard_map/dot_general | solution.py:68
  32.8 6.2 %reshape.166 = f32[512,4,4,128]{3,2,1,0:T(4,128)} reshape(f32[512,2048]{1,0:T(8,128)} %fusion.29) | data formatting | bytes 8388608 | tf_op jit(solution)/shard_map/convert_element_type | solution.py:28
  39.0 6.3 %fusion.47 = (f32[512,4,4,64]{3,2,1,0:T(4,128)S(1)}, f32[512,4,4,64]{3,2,1,0:T(4,128)S(1)}) fusion(f32[512,4,4,128]{3,2,1,0:T(4,128)} %reshape.166), kind=kLoop, calls=%fused_computation.72 | loop fusion | bytes 8388608 | tf_op jit(solution)/shard_map/slice | solution.py:29
  45.3 0.2 broadcast_compare_fusion.1
  45.6 1.0 multiply_cosine_fusion
  46.5 0.3 subtract_convert_fusion.1
  46.8 0.3 pad_maximum_fusion.1
  47.1 0.8 copy.57
  48.0 2.7 subtract_convert_fusion
  50.7 1.2 pad_maximum_fusion
  51.8 7.6 %fusion.17 = (f32[4,4,512]{2,1,0:T(4,128)S(1)}, f32[4,512,512,4]{2,1,3,0:T(8,128)}) fusion(pred[512,512]{0,1:T(8,128)(4,1)S(1)} %broadcast_compare_fusion.1, bf16[512,4,4,128]{3,0,2,1:T(8,128)(2,1)S(1)} %pad_maximum_fusion, bf16[512,4,128]{2,0,1:T(8,128)(2,1)S(1)} %pad_maximum_fusion.1), kind=kOutput, calls=%fused_computation.23 | convolution fusion | flops 1086316544 | bytes 19693568 | tf_op jit(solution)/shard_map/while/body/eval_jaxpr/qkgd,skd->kgqs/dot_general | solution.py:40
  59.5 9.2 %fusion.16 = f32[4,4,512]{2,1,0:T(4,128)S(1)} fusion(f32[4,512,512,4]{2,1,3,0:T(8,128)} %get-tuple-element.353, f32[4,4,512]{2,1,0:T(4,128)S(1)} %broadcast_maximum_fusion, pred[512,512]{0,1:T(8,128)(4,1)S(1)} %broadcast_compare_fusion.1), kind=kLoop, calls=%fused_computation.22 | loop fusion | flops 16769024 | bytes 17104896 | tf_op jit(solution)/shard_map/while/body/eval_jaxpr/reduce_sum | solution.py:45
  68.7 5.9 %convolution_convert_fusion.3 = bf16[512,512]{0,1:T(8,128)(2,1)S(1)} fusion(bf16[4096,512]{1,0:T(8,128)(2,1)} %param.18, bf16[512,4096]{1,0:T(8,128)(2,1)} %param.14, f32[4096]{0:T(1024)S(1)} %convert_element_type.90, f32[512]{0:T(512)S(1)} %add_rsqrt_fusion.1), kind=kOutput, calls=%fused_computation.50 | convolution fusion | flops 2156134400 | bytes 8931328 | tf_op jit(solution)/shard_map/dot_general | solution.py:70
  74.7 1.0 copy.30
  75.7 10.1 %broadcast_add_fusion.1 = f32[4,4,512,128]{3,2,1,0:T(8,128)} fusion(f32[4,4,512]{2,1,0:T(4,128)S(1)} %get-tuple-element.348, bf16[512,4,128,1]{0,2,3,1:T(8,128)(2,1)S(1)} %bitcast.78, f32[4,512,512,4]{2,1,3,0:T(8,128)} %get-tuple-element.353, f32[4,4,512]{2,1,0:T(4,128)S(1)} %broadcast_maximum_fusion, pred[512,512]{0,1:T(8,128)(4,1)S(1)} %broadcast_compare_fusion.1), kind=kOutput, calls=%fused_computation.49 | convolution fusion | flops 1091567616 | bytes 21823488 | tf_op jit(solution)/shard_map/while/body/eval_jaxpr/kgqs,skd->kgqd/dot_general | solution.py:46
  85.7 123.1 %while.7 = (s32[]{:T(128)}, bf16[512,4,128]{2,0,1:T(8,128)(2,1)}, bf16[512,4,128]{2,0,1:T(8,128)(2,1)}, f32[4,4,512]{2,1,0:T(4,128)S(1)}, f32[4,4,512]{2,1,0:T(4...) while((s32[]{:T(128)}, bf16[512,4,128]{2,0,1:T(8,128)(2,1)}, ...), condition=%wide.region_8.9_spmd.clone, body=%wide.region_3.8_spmd.clone.sunk | while | flops 2195997696 | bytes 69742952 | solution.py:93
  86.0 6.1 %collective-permute-done = bf16[512,4,128]{2,0,1:T(8,128)(2,1)S(1)} collective-permute-done((bf16[512,4,128]{2,0,1:T(8,128)(2,1)}, bf16[512,4,128]{2,0,1:T(8,128)(2,1)S(1)}, u32[]{:S(2)}, u32[]{:S(2)}) %collective-permute-start) | collective-permute-done | bytes 524320 | tf_op jit(solution)/shard_map/while/body/eval_jaxpr/ppermute | solution.py:81
  92.0 5.6 %collective-permute-done.1 = bf16[512,4,128]{2,0,1:T(8,128)(2,1)S(1)} collective-permute-done((bf16[512,4,128]{2,0,1:T(8,128)(2,1)}, bf16[512,4,128]{2,0,1:T(8,128)(2,1)S(1)}, u32[]{:S(2)}, u32[]{:S(2)}) %collective-permute-start.1) | collective-permute-done | bytes 524320 | tf_op jit(solution)/shard_map/while/body/eval_jaxpr/ppermute | solution.py:81
  97.6 27.6 %conditional.3 = ((f32[4,4,512]{2,1,0:T(4,128)S(1)}, f32[4,4,512]{2,1,0:T(4,128)S(1)}, f32[4,4,512,128]{3,2,1,0:T(8,128)})) conditional(s32[]{:T(128)} %convert_element_type.190, (f32[4,4,512]{2,1,0:T(4,128)S(1)}, f32[4,4,512]{2,1,0:T(4,128)S(1)}, f32[4,4,512,128]{3,2,1,0:T(8,128)}) %tuple.67, (s32[]{:T(128)}, s32[]{:T(128)}, s32[]{:T(128)}, ...), branch_computations={%region_4.4_spmd, %region_5.7_spmd} | conditional | flops 2195997696 | bytes 63449152 | solution.py:90
  97.7 0.2 broadcast_compare_fusion
  97.9 7.3 %fusion.4 = (f32[4,4,512]{2,1,0:T(4,128)S(1)}, f32[4,512,512,4]{2,1,3,0:T(8,128)}) fusion(pred[512,512]{0,1:T(8,128)(4,1)S(1)} %broadcast_compare_fusion, bf16[512,4,4,128]{3,0,2,1:T(8,128)(2,1)S(1)} %get-tuple-element.239, bf16[512,4,128]{2,0,1:T(8,128)(2,1)S(1)} %get-tuple-element.238), kind=kOutput, calls=%fused_computation.5 | convolution fusion | flops 1086316544 | bytes 19693568 | tf_op jit(solution)/shard_map/while/body/eval_jaxpr/cond/branch_1_fun/while/body/eval_jaxpr/qkgd,skd->kgqs/dot_general | solution.py:40
  105.2 9.2 %fusion.3 = f32[4,4,512]{2,1,0:T(4,128)S(1)} fusion(f32[4,512,512,4]{2,1,3,0:T(8,128)} %get-tuple-element.337, f32[4,4,512]{2,1,0:T(4,128)S(1)} %max.13, pred[512,512]{0,1:T(8,128)(4,1)S(1)} %broadcast_compare_fusion), kind=kLoop, calls=%fused_computation.4 | loop fusion | flops 16769024 | bytes 17104896 | tf_op jit(solution)/shard_map/while/body/eval_jaxpr/cond/branch_1_fun/while/body/eval_jaxpr/reduce_sum | solution.py:45
  114.4 10.9 %multiply_add_fusion = f32[4,4,512,128]{3,2,1,0:T(8,128)} fusion(f32[4,4,512,128]{3,2,1,0:T(8,128)} %get-tuple-element.241, f32[4,4,512]{2,1,0:T(4,128)S(1)} %bitcast.83, f32[4,512,512,4]{2,1,3,0:T(8,128)} %get-tuple-element.337, f32[4,4,512]{2,1,0:T(4,128)S(1)} %max.13, pred[512,512]{0,1:T(8,128)(4,1)S(1)} %broadcast_compare_fusion, ...), kind=kOutput, calls=%fused_computation.8 | convolution fusion | flops 1092616192 | bytes 26017792 | tf_op jit(solution)/shard_map/while/body/eval_jaxpr/cond/branch_1_fun/while/body/eval_jaxpr/kgqs,skd->kgqd/dot_general | solution.py:46
  125.3 0.8 copy.69
  126.1 0.8 copy.70
  126.9 2.4 collective-permute-start.1
  129.3 3.7 collective-permute-done
  133.0 5.6 %collective-permute-done.1 = bf16[512,4,128]{2,0,1:T(8,128)(2,1)S(1)} collective-permute-done((bf16[512,4,128]{2,0,1:T(8,128)(2,1)}, bf16[512,4,128]{2,0,1:T(8,128)(2,1)S(1)}, u32[]{:S(2)}, u32[]{:S(2)}) %collective-permute-start.1) | collective-permute-done | bytes 524320 | tf_op jit(solution)/shard_map/while/body/eval_jaxpr/ppermute | solution.py:81
  138.6 27.6 %conditional.3 = ((f32[4,4,512]{2,1,0:T(4,128)S(1)}, f32[4,4,512]{2,1,0:T(4,128)S(1)}, f32[4,4,512,128]{3,2,1,0:T(8,128)})) conditional(s32[]{:T(128)} %convert_element_type.190, (f32[4,4,512]{2,1,0:T(4,128)S(1)}, f32[4,4,512]{2,1,0:T(4,128)S(1)}, f32[4,4,512,128]{3,2,1,0:T(8,128)}) %tuple.67, (s32[]{:T(128)}, s32[]{:T(128)}, s32[]{:T(128)}, ...), branch_computations={%region_4.4_spmd, %region_5.7_spmd} | conditional | flops 2195997696 | bytes 63449152 | solution.py:90
  138.6 0.2 broadcast_compare_fusion
  138.8 7.3 %fusion.4 = (f32[4,4,512]{2,1,0:T(4,128)S(1)}, f32[4,512,512,4]{2,1,3,0:T(8,128)}) fusion(pred[512,512]{0,1:T(8,128)(4,1)S(1)} %broadcast_compare_fusion, bf16[512,4,4,128]{3,0,2,1:T(8,128)(2,1)S(1)} %get-tuple-element.239, bf16[512,4,128]{2,0,1:T(8,128)(2,1)S(1)} %get-tuple-element.238), kind=kOutput, calls=%fused_computation.5 | convolution fusion | flops 1086316544 | bytes 19693568 | tf_op jit(solution)/shard_map/while/body/eval_jaxpr/cond/branch_1_fun/while/body/eval_jaxpr/qkgd,skd->kgqs/dot_general | solution.py:40
  146.1 9.2 %fusion.3 = f32[4,4,512]{2,1,0:T(4,128)S(1)} fusion(f32[4,512,512,4]{2,1,3,0:T(8,128)} %get-tuple-element.337, f32[4,4,512]{2,1,0:T(4,128)S(1)} %max.13, pred[512,512]{0,1:T(8,128)(4,1)S(1)} %broadcast_compare_fusion), kind=kLoop, calls=%fused_computation.4 | loop fusion | flops 16769024 | bytes 17104896 | tf_op jit(solution)/shard_map/while/body/eval_jaxpr/cond/branch_1_fun/while/body/eval_jaxpr/reduce_sum | solution.py:45
  155.3 10.9 %multiply_add_fusion = f32[4,4,512,128]{3,2,1,0:T(8,128)} fusion(f32[4,4,512,128]{3,2,1,0:T(8,128)} %get-tuple-element.241, f32[4,4,512]{2,1,0:T(4,128)S(1)} %bitcast.83, f32[4,512,512,4]{2,1,3,0:T(8,128)} %get-tuple-element.337, f32[4,4,512]{2,1,0:T(4,128)S(1)} %max.13, pred[512,512]{0,1:T(8,128)(4,1)S(1)} %broadcast_compare_fusion, ...), kind=kOutput, calls=%fused_computation.8 | convolution fusion | flops 1092616192 | bytes 26017792 | tf_op jit(solution)/shard_map/while/body/eval_jaxpr/cond/branch_1_fun/while/body/eval_jaxpr/kgqs,skd->kgqd/dot_general | solution.py:46
  166.2 0.8 copy.69
  167.0 0.8 copy.70
  167.8 7.1 %collective-permute-done = bf16[512,4,128]{2,0,1:T(8,128)(2,1)S(1)} collective-permute-done((bf16[512,4,128]{2,0,1:T(8,128)(2,1)}, bf16[512,4,128]{2,0,1:T(8,128)(2,1)S(1)}, u32[]{:S(2)}, u32[]{:S(2)}) %collective-permute-start) | collective-permute-done | bytes 524320 | tf_op jit(solution)/shard_map/while/body/eval_jaxpr/ppermute | solution.py:81
  174.9 4.7 collective-permute-done.1
  179.6 27.6 %conditional.3 = ((f32[4,4,512]{2,1,0:T(4,128)S(1)}, f32[4,4,512]{2,1,0:T(4,128)S(1)}, f32[4,4,512,128]{3,2,1,0:T(8,128)})) conditional(s32[]{:T(128)} %convert_element_type.190, (f32[4,4,512]{2,1,0:T(4,128)S(1)}, f32[4,4,512]{2,1,0:T(4,128)S(1)}, f32[4,4,512,128]{3,2,1,0:T(8,128)}) %tuple.67, (s32[]{:T(128)}, s32[]{:T(128)}, s32[]{:T(128)}, ...), branch_computations={%region_4.4_spmd, %region_5.7_spmd} | conditional | flops 2195997696 | bytes 63449152 | solution.py:90
  179.6 0.2 broadcast_compare_fusion
  179.8 7.3 %fusion.4 = (f32[4,4,512]{2,1,0:T(4,128)S(1)}, f32[4,512,512,4]{2,1,3,0:T(8,128)}) fusion(pred[512,512]{0,1:T(8,128)(4,1)S(1)} %broadcast_compare_fusion, bf16[512,4,4,128]{3,0,2,1:T(8,128)(2,1)S(1)} %get-tuple-element.239, bf16[512,4,128]{2,0,1:T(8,128)(2,1)S(1)} %get-tuple-element.238), kind=kOutput, calls=%fused_computation.5 | convolution fusion | flops 1086316544 | bytes 19693568 | tf_op jit(solution)/shard_map/while/body/eval_jaxpr/cond/branch_1_fun/while/body/eval_jaxpr/qkgd,skd->kgqs/dot_general | solution.py:40
  187.1 9.2 %fusion.3 = f32[4,4,512]{2,1,0:T(4,128)S(1)} fusion(f32[4,512,512,4]{2,1,3,0:T(8,128)} %get-tuple-element.337, f32[4,4,512]{2,1,0:T(4,128)S(1)} %max.13, pred[512,512]{0,1:T(8,128)(4,1)S(1)} %broadcast_compare_fusion), kind=kLoop, calls=%fused_computation.4 | loop fusion | flops 16769024 | bytes 17104896 | tf_op jit(solution)/shard_map/while/body/eval_jaxpr/cond/branch_1_fun/while/body/eval_jaxpr/reduce_sum | solution.py:45
  196.3 10.9 %multiply_add_fusion = f32[4,4,512,128]{3,2,1,0:T(8,128)} fusion(f32[4,4,512,128]{3,2,1,0:T(8,128)} %get-tuple-element.241, f32[4,4,512]{2,1,0:T(4,128)S(1)} %bitcast.83, f32[4,512,512,4]{2,1,3,0:T(8,128)} %get-tuple-element.337, f32[4,4,512]{2,1,0:T(4,128)S(1)} %max.13, pred[512,512]{0,1:T(8,128)(4,1)S(1)} %broadcast_compare_fusion, ...), kind=kOutput, calls=%fused_computation.8 | convolution fusion | flops 1092616192 | bytes 26017792 | tf_op jit(solution)/shard_map/while/body/eval_jaxpr/cond/branch_1_fun/while/body/eval_jaxpr/kgqs,skd->kgqd/dot_general | solution.py:46
  207.2 0.8 copy.69
  208.0 0.8 copy.70
  208.8 5.2 copy.31
  214.0 2.8 divide_convert_fusion
  216.8 14.1 %convolution_convert_fusion.1 = bf16[512,4096]{1,0:T(8,128)(2,1)} fusion(bf16[512,2048]{0,1:T(8,128)(2,1)S(1)} %bitcast.76, bf16[2048,4096]{1,0:T(8,128)(2,1)} %param.19), kind=kOutput, calls=%fused_computation.42 | convolution fusion | flops 8592031744 | bytes 23068672 | tf_op jit(solution)/shard_map/dot_general | solution.py:96
  231.0 0.0 all-reduce.5.cloned.1.call-start
  231.0 103.1 %all-reduce.3.cloned.1.call-done = bf16[512,4096]{1,0:T(8,128)(2,1)} async-done(((bf16[512,4096]{1,0:T(8,128)(2,1)}), bf16[512,4096]{1,0:T(8,128)(2,1)}) %all-reduce.3.cloned.1.call-update) | async-done | bytes 4194320 | tf_op jit(solution)/shard_map/psum | solution.py:97
  334.2 5.4 fusion.22
  339.6 34.6 %fusion.34 = f32[512,6144]{1,0:T(8,128)} fusion(bf16[4096,6144]{1,0:T(8,128)(2,1)} %param.21, bf16[512,4096]{1,0:T(8,128)(2,1)S(1)} %get-tuple-element.335, f32[4096]{0:T(1024)S(1)} %convert_element_type.106, f32[512]{0:T(512)S(1)} %add_rsqrt_fusion), kind=kOutput, calls=%fused_computation.52 | convolution fusion | flops 25778192384 | bytes 67127296 | tf_op jit(solution)/shard_map/dot_general | solution.py:100
  374.2 35.8 %multiply_convert_fusion.clone.4 = bf16[512,6144]{1,0:T(8,128)(2,1)} fusion(f32[512,6144]{1,0:T(8,128)} %fusion.34, bf16[4096,6144]{1,0:T(8,128)(2,1)} %param.22, bf16[512,4096]{1,0:T(8,128)(2,1)S(1)} %get-tuple-element.335, f32[4096]{0:T(1024)S(1)} %convert_element_type.106, f32[512]{0:T(512)S(1)} %add_rsqrt_fusion), kind=kOutput, calls=%fused_computation.24.clone.clone.clone.1 | convolution fusion | flops 25797066752 | bytes 73418752 | tf_op jit(solution)/shard_map/dot_general | solution.py:101
  410.0 34.4 %convolution_convert_fusion = bf16[512,4096]{1,0:T(8,128)(2,1)} fusion(bf16[6144,4096]{1,0:T(8,128)(2,1)} %param.23, bf16[512,6144]{1,0:T(8,128)(2,1)} %multiply_convert_fusion.clone.4), kind=kOutput, calls=%fused_computation.41 | convolution fusion | flops 25771900928 | bytes 60817408 | tf_op jit(solution)/shard_map/dot_general | solution.py:103
  444.4 1.2 copy.32
  445.6 1.1 copy.33
  446.6 99.9 %all-reduce.5.cloned.1.call-done = bf16[512,4096]{1,0:T(8,128)(2,1)} async-done(((bf16[512,4096]{1,0:T(8,128)(2,1)}), bf16[512,4096]{1,0:T(8,128)(2,1)}) %all-reduce.5.cloned.1.call-update) | async-done | bytes 4194320 | tf_op jit(solution)/shard_map/psum | solution.py:104
  546.5 7.2 %fusion.25 = bf16[512,4096]{1,0:T(8,128)(2,1)} fusion(bf16[512,4096]{1,0:T(8,128)(2,1)} %copy-done, bf16[512,4096]{1,0:T(8,128)(2,1)} %all-reduce.5.cloned.1.call-done), kind=kLoop, calls=%fused_computation.38 | loop fusion | flops 8388608 | bytes 12582912 | tf_op jit(solution)/shard_map/convert_element_type | solution.py:105
  (41 shorter events, 0.3 us)
Async XLA Ops:
  7.2 327.0 %all-reduce.3.cloned.1.call-start = ((), (), s32[]{:S(2)}) async-start(), calls=%async_computation | async-start | bytes 8388608 | tf_op jit(solution)/shard_map/psum | solution.py:97
  47.1 12.4 %copy-start.1 = (bf16[512,4,128]{2,0,1:T(8,128)(2,1)}, bf16[512,4,128]{2,0,1:T(8,128)(2,1)S(1)}, u32[]{:S(2)}) copy-start(bf16[512,4,128]{2,0,1:T(8,128)(2,1)S(1)} %pad_maximum_fusion.1) | copy-start | bytes 1572868
  74.7 11.1 %copy-start.3 = (bf16[512,512]{0,1:T(8,128)(2,1)}, bf16[512,512]{0,1:T(8,128)(2,1)S(1)}, u32[]{:S(2)}) copy-start(bf16[512,512]{0,1:T(8,128)(2,1)S(1)} %convolution_convert_fusion.3) | copy-start | bytes 1572868
  85.9 6.1 %collective-permute-start = (bf16[512,4,128]{2,0,1:T(8,128)(2,1)}, bf16[512,4,128]{2,0,1:T(8,128)(2,1)S(1)}, u32[]{:S(2)}, u32[]{:S(2)}) collective-permute-start(bf16[512,4,128]{2,0,1:T(8,128)(2,1)} %get-tuple-element.436), channel_id=1, source_target_pairs={{0,1},{1,2},{2,3},{3,0},{4,5},{5,6},{6,7},{7,4}} | collective-permute-start | bytes 1572872 | tf_op jit(solution)/shard_map/while/body/eval_jaxpr/ppermute | solution.py:81
  85.9 11.7 %collective-permute-start.1 = (bf16[512,4,128]{2,0,1:T(8,128)(2,1)}, bf16[512,4,128]{2,0,1:T(8,128)(2,1)S(1)}, u32[]{:S(2)}, u32[]{:S(2)}) collective-permute-start(bf16[512,4,128]{2,0,1:T(8,128)(2,1)} %get-tuple-element.437), channel_id=1, source_target_pairs={{0,1},{1,2},{2,3},{3,0},{4,5},{5,6},{6,7},{7,4}} | collective-permute-start | bytes 1572872 | tf_op jit(solution)/shard_map/while/body/eval_jaxpr/ppermute | solution.py:81
  126.9 6.1 %collective-permute-start = (bf16[512,4,128]{2,0,1:T(8,128)(2,1)}, bf16[512,4,128]{2,0,1:T(8,128)(2,1)S(1)}, u32[]{:S(2)}, u32[]{:S(2)}) collective-permute-start(bf16[512,4,128]{2,0,1:T(8,128)(2,1)} %get-tuple-element.436), channel_id=1, source_target_pairs={{0,1},{1,2},{2,3},{3,0},{4,5},{5,6},{6,7},{7,4}} | collective-permute-start | bytes 1572872 | tf_op jit(solution)/shard_map/while/body/eval_jaxpr/ppermute | solution.py:81
  126.9 11.7 %collective-permute-start.1 = (bf16[512,4,128]{2,0,1:T(8,128)(2,1)}, bf16[512,4,128]{2,0,1:T(8,128)(2,1)S(1)}, u32[]{:S(2)}, u32[]{:S(2)}) collective-permute-start(bf16[512,4,128]{2,0,1:T(8,128)(2,1)} %get-tuple-element.437), channel_id=1, source_target_pairs={{0,1},{1,2},{2,3},{3,0},{4,5},{5,6},{6,7},{7,4}} | collective-permute-start | bytes 1572872 | tf_op jit(solution)/shard_map/while/body/eval_jaxpr/ppermute | solution.py:81
  167.8 7.1 %collective-permute-start = (bf16[512,4,128]{2,0,1:T(8,128)(2,1)}, bf16[512,4,128]{2,0,1:T(8,128)(2,1)S(1)}, u32[]{:S(2)}, u32[]{:S(2)}) collective-permute-start(bf16[512,4,128]{2,0,1:T(8,128)(2,1)} %get-tuple-element.436), channel_id=1, source_target_pairs={{0,1},{1,2},{2,3},{3,0},{4,5},{5,6},{6,7},{7,4}} | collective-permute-start | bytes 1572872 | tf_op jit(solution)/shard_map/while/body/eval_jaxpr/ppermute | solution.py:81
  167.8 11.7 %collective-permute-start.1 = (bf16[512,4,128]{2,0,1:T(8,128)(2,1)}, bf16[512,4,128]{2,0,1:T(8,128)(2,1)S(1)}, u32[]{:S(2)}, u32[]{:S(2)}) collective-permute-start(bf16[512,4,128]{2,0,1:T(8,128)(2,1)} %get-tuple-element.437), channel_id=1, source_target_pairs={{0,1},{1,2},{2,3},{3,0},{4,5},{5,6},{6,7},{7,4}} | collective-permute-start | bytes 1572872 | tf_op jit(solution)/shard_map/while/body/eval_jaxpr/ppermute | solution.py:81
  216.8 14.2 %copy-start.5 = (bf16[4096]{0:T(1024)(128)(2,1)S(1)}, bf16[4096]{0:T(1024)(128)(2,1)}, u32[]{:S(2)}) copy-start(bf16[4096]{0:T(1024)(128)(2,1)} %param.20) | copy-start | bytes 24580
  231.0 315.6 %all-reduce.5.cloned.1.call-start = ((), (), s32[]{:S(2)}) async-start(), calls=%async_computation.1 | async-start | bytes 8388608 | tf_op jit(solution)/shard_map/psum | solution.py:104
  339.6 34.6 %copy-start = (bf16[512,4096]{1,0:T(8,128)(2,1)}, bf16[512,4096]{1,0:T(8,128)(2,1)S(1)}, u32[]{:S(2)}) copy-start(bf16[512,4096]{1,0:T(8,128)(2,1)S(1)} %get-tuple-element.335) | copy-start | bytes 12582916
  410.0 34.4 %copy-start.2 = (bf16[512,4,128]{2,0,1:T(8,128)(2,1)S(1)}, bf16[512,4,128]{2,0,1:T(8,128)(2,1)}, u32[]{:S(2)}) copy-start(bf16[512,4,128]{2,0,1:T(8,128)(2,1)} %copy-done.1) | copy-start | bytes 1572868
  410.0 35.6 %copy-start.4 = (bf16[512,512]{0,1:T(8,128)(2,1)S(1)}, bf16[512,512]{0,1:T(8,128)(2,1)}, u32[]{:S(2)}) copy-start(bf16[512,512]{0,1:T(8,128)(2,1)} %copy-done.3) | copy-start | bytes 1572868
Sparse Core Ops, SparseCore 0:
  231.1 103.0 all-reduce.2
  444.5 102.0 all-reduce.4
where the time goes:
time: 570 us; the launch traced here: 561 us
  waiting for transfers between devices  236 us (41%)
  matrix products  218 us (38%)
  other arithmetic  62.4 us (11%)
  local copies, waits for them, and re-layouts  27.5 us (5%)
  between operations  14.8 us (3%)
    psum x1, waiting for transfers between devices, local_layer(): attn_total = lax.psum(attn_part, 'tp')  103 us
    psum x1, waiting for transfers between devices, local_layer(): down_total = lax.psum(down_part, 'tp')  99.9 us
    dot_general x4, matrix products, tile_step(): jnp.einsum('kgqs,skd->kgqd', exp_scores.astype(jnp.bfloat16), v_tile, pre...  42.8 us
    reduce_sum x4, other arithmetic, tile_step(): new_sum = run_sum * rescale + jnp.sum(exp_scores, axis=-1)  36.7 us
    dot_general x1, matrix products, local_layer(): up_proj = jnp.dot(normed_mlp, w_up, preferred_element_type=jnp.float32)  35.8 us
    dot_general x1, matrix products, local_layer(): gate_proj = jnp.dot(normed_mlp, w_gate, preferred_element_type=jnp.float32)  34.6 us
    dot_general x1, matrix products, local_layer(): jnp.dot(activated, w_down, preferred_element_type=jnp.float32)  34.4 us
    ppermute x6, waiting for transfers between devices, shift_step(): held = lax.ppermute(held, 'cp', shift_pairs)  32.7 us
  transfers between devices with their start and end apart: 8, of which 8 were waited for; matrix products, arithmetic and copies ran while one was open for 0% of the time, Pallas kernels for 0%

commit v1 on v0

v1 whole, which is shorter than its diff:
```python
import functools
import jax
import jax.numpy as jnp
from jax import lax
from jax.experimental import pallas as pl
from jax.experimental.pallas import tpu as pltpu
from jax.sharding import PartitionSpec as P

HEAD_DIM = 128
ROPE_THETA = 1000000.0
NORM_EPS = 1e-5
MASK_VALUE = -1e30
EXP2_SCALE = HEAD_DIM ** -0.5 * 1.4426950408889634
BF = jnp.bfloat16
F32 = jnp.float32
VMEM_BIG = 60 * 1024 * 1024
ANY = pl.BlockSpec(memory_space=pl.ANY)
SMEM = pl.BlockSpec(memory_space=pltpu.SMEM)


def cost(flops, nbytes):
    return pl.CostEstimate(flops=flops, bytes_accessed=nbytes, transcendentals=0)


def params():
    return pltpu.CompilerParams(vmem_limit_bytes=VMEM_BIG)


def rope_tables(positions):
    inv_freq = jnp.asarray(ROPE_THETA, F32) ** (-jnp.arange(0, HEAD_DIM, 2, dtype=F32) / HEAD_DIM)
    angles = positions.astype(F32)[:, None] * inv_freq[None, :]
    return jnp.cos(angles), jnp.sin(angles)


def norm_rows(rows, gain_row):
    inv_rms = lax.rsqrt(jnp.mean(rows * rows, axis=-1, keepdims=True) + NORM_EPS)
    return (rows * inv_rms * gain_row.astype(F32)).astype(BF)


def rope_block(prod, cos_full, sin_full):
    pieces = []
    for head in range(prod.shape[1] // HEAD_DIM):
        u = prod[:, head * HEAD_DIM:(head + 1) * HEAD_DIM].astype(BF).astype(F32)
        pieces.append((u * cos_full + pltpu.roll(u, HEAD_DIM // 2, 1) * sin_full).astype(BF))
    return jnp.concatenate(pieces, axis=1)


def kv_kernel(x_ref, gain_ref, wk_ref, wv_ref, cos_ref, sin_ref, n_ref, k_ref, v_ref):
    @pl.when(pl.program_id(0) == 0)
    def _():
        def chunk(i, c):
            rows = pl.ds(pl.multiple_of(i * 64, 64), 64)
            n_ref[rows, :] = norm_rows(x_ref[rows, :].astype(F32), gain_ref[...])
            return c
        lax.fori_loop(0, x_ref.shape[0] // 64, chunk, 0)
    n = n_ref[...]
    k = jnp.dot(n, wk_ref[...], preferred_element_type=F32)
    k_ref[...] = rope_block(k, cos_ref[...], sin_ref[...])
    v_ref[...] = jnp.dot(n, wv_ref[...], preferred_element_type=F32).astype(BF)


def kv_proj(x, gain, w_k, w_v, cos_full, sin_full):
    rows, width = x.shape
    cols = w_k.shape[1]
    bn = 256
    whole = lambda a: pl.BlockSpec(a.shape, lambda i: (0, 0))
    wspec = pl.BlockSpec((width, bn), lambda i: (0, i))
    ospec = pl.BlockSpec((rows, bn), lambda i: (0, i))
    return pl.pallas_call(
        kv_kernel, grid=(cols // bn,),
        in_specs=[whole(x), whole(gain), wspec, wspec, whole(cos_full), whole(sin_full)],
        out_specs=[pl.BlockSpec((rows, width), lambda i: (0, 0)), ospec, ospec],
        out_shape=[jax.ShapeDtypeStruct((rows, width), BF), jax.ShapeDtypeStruct((rows, cols), BF), jax.ShapeDtypeStruct((rows, cols), BF)],
        compiler_params=params(), name='kv_proj',
        cost_estimate=cost(4 * rows * width * cols, 2 * 2 * width * (rows + cols)),
    )(x, gain, w_k, w_v, cos_full, sin_full)


def q_kernel(n_ref, w_ref, cos_ref, sin_ref, q_ref):
    prod = jnp.dot(n_ref[...], w_ref[...], preferred_element_type=F32)
    q_ref[...] = rope_block(prod, cos_ref[...], sin_ref[...])


def q_proj(n, w_q, cos_full, sin_full):
    rows, width = n.shape
    cols = w_q.shape[1]
    bn = 512
    whole = lambda a: pl.BlockSpec(a.shape, lambda i: (0, 0))
    return pl.pallas_call(
        q_kernel, grid=(cols // bn,),
        in_specs=[whole(n), pl.BlockSpec((width, bn), lambda i: (0, i)), whole(cos_full), whole(sin_full)],
        out_specs=pl.BlockSpec((rows, bn), lambda i: (0, i)),
        out_shape=jax.ShapeDtypeStruct((rows, cols), BF),
        compiler_params=params(), name='q_proj',
        cost_estimate=cost(2 * rows * width * cols, 2 * width * (rows + cols)),
    )(n, w_q, cos_full, sin_full)


def attn_kernel(row0, chunk, bounds_ref, q_ref, k_ref, v_ref, ka, va, kb, vb, kc, vc, wo_ref, part_ref,
                wo_buf, k_buf, v_buf, o_buf, m_sc, l_sc, acc_sc, wo_sem, kv_sem):
    wo_copy = pltpu.make_async_copy(wo_ref, wo_buf, wo_sem)
    copies = []
    for slot, (ks, vs) in enumerate(((ka, va), (kb, vb), (kc, vc))):
        copies.append(pltpu.make_async_copy(ks, k_buf.at[slot], kv_sem.at[2 * slot]))
        copies.append(pltpu.make_async_copy(vs, v_buf.at[slot], kv_sem.at[2 * slot + 1]))
    for c in copies:
        c.start()
    wo_copy.start()
    n_kv = k_ref.shape[1] // HEAD_DIM
    groups = q_ref.shape[1] // k_ref.shape[1]
    stacked = groups * chunk
    n_keys = row0 + chunk
    for c in copies:
        c.wait()

    def head_step(g, carry):
        kcol = pl.ds(pl.multiple_of(g * HEAD_DIM, HEAD_DIM), HEAD_DIM)
        heads = [q_ref[:, pl.ds(pl.multiple_of((g * groups + j) * HEAD_DIM, HEAD_DIM), HEAD_DIM)] for j in range(groups)]
        q = jnp.concatenate(heads, axis=0)
        s = lax.dot_general(q, k_ref[:n_keys, kcol], (((1,), (1,)), ((), ())), preferred_element_type=F32)
        qpos = row0 + lax.rem(lax.broadcasted_iota(jnp.int32, (stacked, n_keys), 0), chunk)
        kpos = lax.broadcasted_iota(jnp.int32, (stacked, n_keys), 1)
        s = jnp.where(kpos <= qpos, s, MASK_VALUE)
        m0 = jnp.max(s, axis=-1, keepdims=True)
        p = jnp.exp2(s * EXP2_SCALE - m0 * EXP2_SCALE)
        m_sc[...] = jnp.broadcast_to(m0, m_sc.shape)
        l_sc[...] = jnp.broadcast_to(jnp.sum(p, axis=-1, keepdims=True), l_sc.shape)
        acc_sc[...] = jnp.dot(p.astype(BF), v_ref[:n_keys, kcol], preferred_element_type=F32)

        def block_step(b, carry2):
            s = lax.dot_general(q, k_buf[b, :, kcol], (((1,), (1,)), ((), ())), preferred_element_type=F32)
            m_old = m_sc[...]
            m_new = jnp.maximum(m_old, jnp.max(s, axis=-1, keepdims=True))
            alpha = jnp.exp2((m_old - m_new) * EXP2_SCALE)
            p = jnp.exp2(s * EXP2_SCALE - m_new[:, :1] * EXP2_SCALE)
            l_sc[...] = l_sc[...] * alpha + jnp.sum(p, axis=-1, keepdims=True)
            acc_sc[...] = acc_sc[...] * alpha + jnp.dot(p.astype(BF), v_buf[b, :, kcol], preferred_element_type=F32)
            m_sc[...] = m_new
            return carry2
        lax.fori_loop(bounds_ref[0], bounds_ref[1], block_step, 0)
        out = (acc_sc[...] / l_sc[...]).astype(BF)
        for j in range(groups):
            o_buf[:, pl.ds(pl.multiple_of((g * groups + j) * HEAD_DIM, HEAD_DIM), HEAD_DIM)] = out[j * chunk:(j + 1) * chunk]
        return carry
    lax.fori_loop(0, n_kv, head_step, 0)
    wo_copy.wait()

    def col_step(i, carry):
        cols = pl.ds(pl.multiple_of(i * 512, 512), 512)
        part_ref[:, cols] = jnp.dot(o_buf[...], wo_buf[:, cols], preferred_element_type=F32).astype(BF)
        return carry
    lax.fori_loop(0, part_ref.shape[1] // 512, col_step, 0)


def attn_chunk(row0, chunk, bounds, q, k, v, others, w_o):
    rows, qcols = q.shape
    kcols = k.shape[1]
    width = w_o.shape[1]
    stacked = chunk * (qcols // kcols)
    vmem = lambda a: pl.BlockSpec(a.shape, lambda i: (0, 0))
    return pl.pallas_call(
        functools.partial(attn_kernel, row0, chunk), grid=(1,),
        in_specs=[SMEM, pl.BlockSpec((chunk, qcols), lambda i: (row0 // chunk, 0)), vmem(k), vmem(v)] + [ANY] * 7,
        out_specs=pl.BlockSpec((chunk, width), lambda i: (0, 0)),
        out_shape=jax.ShapeDtypeStruct((chunk, width), BF),
        scratch_shapes=[pltpu.VMEM(w_o.shape, BF), pltpu.VMEM((3, rows, kcols), BF), pltpu.VMEM((3, rows, kcols), BF),
                        pltpu.VMEM((chunk, qcols), BF), pltpu.VMEM((stacked, HEAD_DIM), F32), pltpu.VMEM((stacked, HEAD_DIM), F32),
                        pltpu.VMEM((stacked, HEAD_DIM), F32), pltpu.SemaphoreType.DMA, pltpu.SemaphoreType.DMA((6,))],
        compiler_params=params(), name='attn_%d' % row0,
        cost_estimate=cost(2 * chunk * qcols * width + 8 * chunk * rows * qcols, 2 * qcols * width),
    )(bounds, q, k, v, *others, w_o)


def gate_up_kernel(n_parts, *refs):
    x_ref, gain_ref = refs[0], refs[1]
    parts = refs[2:2 + 2 * n_parts]
    wg_ref, wu_ref, h_ref, act_ref, m_buf = refs[2 + 2 * n_parts:]

    @pl.when(pl.program_id(0) == 0)
    def _():
        sub = x_ref.shape[0] // n_parts
        for i in range(n_parts):
            mine, other = parts[2 * i], parts[2 * i + 1]

            def chunk(j, c, i=i, mine=mine, other=other):
                src = pl.ds(pl.multiple_of(j * 32, 32), 32)
                dst = pl.ds(pl.multiple_of(i * sub + j * 32, 32), 32)
                total = mine[src, :].astype(F32) + other[src, :].astype(F32)
                h = (x_ref[dst, :].astype(F32) + total).astype(BF)
                h_ref[dst, :] = h
                m_buf[dst, :] = norm_rows(h.astype(F32), gain_ref[...])
                return c
            lax.fori_loop(0, sub // 32, chunk, 0)
    m = m_buf[...]
    gate = jnp.dot(m, wg_ref[...], preferred_element_type=F32)
    up = jnp.dot(m, wu_ref[...], preferred_element_type=F32)
    act_ref[...] = (gate / (1.0 + jnp.exp(-gate)) * up).astype(BF)


def gate_up(x, row0, rows, gain, parts, w_gate, w_up):
    width = x.shape[1]
    cols = w_gate.shape[1]
    bn = 512
    whole = lambda a: pl.BlockSpec(a.shape, lambda i: (0, 0))
    wspec = pl.BlockSpec((width, bn), lambda i: (0, i))
    n_parts = len(parts) // 2
    return pl.pallas_call(
        functools.partial(gate_up_kernel, n_parts), grid=(cols // bn,),
        in_specs=[pl.BlockSpec((rows, width), lambda i: (row0 // rows, 0)), whole(gain)] + [whole(p) for p in parts] + [wspec, wspec],
        out_specs=[pl.BlockSpec((rows, width), lambda i: (0, 0)), pl.BlockSpec((rows, bn), lambda i: (0, i))],
        out_shape=[jax.ShapeDtypeStruct((rows, width), BF), jax.ShapeDtypeStruct((rows, cols), BF)],
        scratch_shapes=[pltpu.VMEM((rows, width), BF)],
        compiler_params=params(), name='gate_up_%d' % row0,
        cost_estimate=cost(4 * rows * width * cols, 4 * width * cols),
    )(x, gain, *parts, w_gate, w_up)


def down_kernel(act_ref, w_ref, out_ref):
    out_ref[...] = jnp.dot(act_ref[...], w_ref[...], preferred_element_type=F32).astype(BF)


def down(act, w_down, col0, cols, tag):
    rows, depth = act.shape
    bn = 512
    return pl.pallas_call(
        down_kernel, grid=(cols // bn,),
        in_specs=[pl.BlockSpec((rows, depth), lambda i: (0, 0)), pl.BlockSpec((depth, bn), lambda i: (0, i + col0 // bn))],
        out_specs=pl.BlockSpec((rows, bn), lambda i: (0, i)),
        out_shape=jax.ShapeDtypeStruct((rows, cols), BF),
        compiler_params=params(), name='down_%s_%d' % (tag, col0),
        cost_estimate=cost(2 * rows * depth * cols, 2 * depth * cols),
    )(act, w_down)


def solution(mesh):
    row_spec = P(('dp', 'cp'), None)
    cache_spec = P(('dp', 'cp'), 'tp', None)
    col_spec = P(None, 'tp')
    split_rows = P('tp', None)
    vec_spec = P(None)
    swap = [(0, 1), (1, 0)]

    def local_layer(x, attn_gain, w_q, w_k, w_v, w_o, mlp_gain, w_gate, w_up, w_down):
        tok = x.shape[0]
        kv_local = w_k.shape[1] // HEAD_DIM
        cp_index = lax.axis_index('cp')
        cos_tab, sin_tab = rope_tables(cp_index * tok + jnp.arange(tok))
        cos_full = jnp.concatenate([cos_tab, cos_tab], axis=1)
        sin_full = jnp.concatenate([-sin_tab, sin_tab], axis=1)
        n, k, v = kv_proj(x, attn_gain[None, :], w_k, w_v, cos_full, sin_full)
        kb = lax.ppermute(k, 'cp', [(0, 2), (1, 3)])
        vb = lax.ppermute(v, 'cp', [(0, 2), (1, 3)])
        ka = lax.ppermute(k, 'cp', [(0, 1), (2, 3)])
        va = lax.ppermute(v, 'cp', [(0, 1), (2, 3)])
        kc = lax.ppermute(kb, 'cp', [(2, 3), (3, 2)])
        vc = lax.ppermute(vb, 'cp', [(2, 3), (3, 2)])
        q = q_proj(n, w_q, cos_full, sin_full)
        lo = jnp.where(cp_index == 2, 1, 0)
        hi = jnp.where(cp_index == 0, 0, jnp.where(cp_index == 1, 1, 3))
        bounds = jnp.stack([lo, hi]).astype(jnp.int32)
        others = (ka, va, kb, vb, kc, vc)
        chunk = 128
        mine, theirs = [], []
        for i in range(tok // chunk):
            part = attn_chunk(i * chunk, chunk, bounds, q, k, v, others, w_o)
            mine.append(part)
            theirs.append(lax.ppermute(part, 'tp', swap))
        half = tok // 2
        per = half // chunk
        outs = []
        pieces = (1024, 1024, 2048)
        for s in range(2):
            parts = []
            for i in range(s * per, (s + 1) * per):
                parts += [mine[i], theirs[i]]
            h, act = gate_up(x, s * half, half, mlp_gain[None, :], parts, w_gate, w_up)
            col = 0
            row_out = []
            for wdt in pieces:
                d = down(act, w_down, col, wdt, 'ab'[s])
                r = lax.ppermute(d, 'tp', swap)
                row_out.append((h[:, col:col + wdt].astype(F32) + (d.astype(F32) + r.astype(F32))).astype(BF))
                col += wdt
            outs.append(jnp.concatenate(row_out, axis=1))
        x_out = jnp.concatenate(outs, axis=0)
        return x_out, k.reshape(tok, kv_local, HEAD_DIM), v.reshape(tok, kv_local, HEAD_DIM)

    return jax.shard_map(local_layer, mesh=mesh,
                         in_specs=(row_spec, vec_spec, col_spec, col_spec, col_spec, split_rows, vec_spec, col_spec, col_spec, split_rows),
                         out_specs=(row_spec, cache_spec, cache_spec), check_vma=False)
```

time: 570 us -> 392 us (0.69)
  Pallas kernels: 0 us -> 253 us
  matrix products: 218 us -> 0 us
  waiting for transfers between devices: 236 us -> 73.8 us
  other arithmetic: 62.4 us -> 30.5 us
  local copies, waits for them, and re-layouts: 27.5 us -> 8.72 us
  starting transfers between devices: 2.55 us -> 20.8 us
  between operations: 14.8 us -> 1.36 us
    pallas_call x0 -> x14, Pallas kernels: none -> 253 us  [the longest x2 87.3 us: gate_up(): pl.pallas_call(functools.partial(gate_up_kernel, n_parts), grid=(cols //...]
    dot_general x15 -> x0, matrix products: 218 us -> none  [the longest x4 42.8 us: tile_step(): jnp.einsum('kgqs,skd->kgqd', exp_scores.astype(jnp.bfloat16), v_tile, pre...]
    psum x2 -> x0, waiting for transfers between devices: 203 us -> none  [the longest x1 103 us: local_layer(): attn_total = lax.psum(attn_part, 'tp')]
    reduce_sum x6 -> x0, other arithmetic: 45.2 us -> none  [the longest x4 36.7 us: tile_step(): new_sum = run_sum * rescale + jnp.sum(exp_scores, axis=-1)]
    ppermute x6 -> x16, waiting for transfers between devices: 32.7 us -> 73.8 us  [the longest x6 58.2 us: local_layer(): r = lax.ppermute(d, 'tp', swap)]
    concatenate x2, other arithmetic: 1.44 us -> 23.6 us  [the longest x1 22.6 us: local_layer(): x_out = jnp.concatenate(outs, axis=0)]
    ppermute x6 -> x16, starting transfers between devices: 2.47 us -> 20.8 us  [the longest x1 4.56 us: local_layer(): kc = lax.ppermute(kb, 'cp', [(2, 3), (3, 2)])]
    while x7 -> x0, local copies, waits for them, and re-layouts: 10 us -> none  [the longest x1 5.24 us: local_layer(): state = lax.fori_loop(1, cp_size, shift_step, ((keys, values), state))[1]]
  transfers between devices with their start and end apart: 8 -> 16, of which waited for: 8 -> 6; matrix products, arithmetic and copies ran while one was open for 0% -> 2% of each run, Pallas kernels for 0% -> 42%
where the time goes in v1:
time: 392 us; the launch traced here: 388 us
  Pallas kernels  253 us (65%)
  waiting for transfers between devices  73.8 us (19%)
  other arithmetic  30.5 us (8%)
  starting transfers between devices  20.8 us (5%)
  local copies, waits for them, and re-layouts  8.72 us (2%)
    pallas_call x2, Pallas kernels, gate_up(): pl.pallas_call(functools.partial(gate_up_kernel, n_parts), grid=(cols //...  87.3 us
    pallas_call x4, Pallas kernels, attn_chunk(): pl.pallas_call(functools.partial(attn_kernel, row0, chunk), grid=(1,), in...  81.1 us
    pallas_call x6, Pallas kernels, down(): pl.pallas_call(down_kernel, grid=(cols // bn,), in_specs=[pl.BlockSpec((r...  58.8 us
    ppermute x6, waiting for transfers between devices, local_layer(): r = lax.ppermute(d, 'tp', swap)  58.2 us
    concatenate x1, other arithmetic, local_layer(): x_out = jnp.concatenate(outs, axis=0)  22.6 us
    pallas_call x1, Pallas kernels, q_proj(): pl.pallas_call(q_kernel, grid=(cols // bn,), in_specs=[whole(n), pl.Block...  14.3 us
    pallas_call x1, Pallas kernels, kv_proj(): pl.pallas_call(kv_kernel, grid=(cols // bn,), in_specs=[whole(x), whole(g...  11.5 us
    ppermute x1, waiting for transfers between devices, local_layer(): kb = lax.ppermute(k, 'cp', [(0, 2), (1, 3)])  8.89 us
  transfers between devices with their start and end apart: 16, of which 6 were waited for; matrix products, arithmetic and copies ran while one was open for 2% of the time, Pallas kernels for 42%

profile of v1, /device:TPU:3, one launch (start us, length us, event | category | flops | bytes accessed | tf_op | source)
XLA Modules:
  0.0 388.2 jit_solution(13247714154281162697)
XLA Ops:
  0.7 1.3 broadcast_in_dim.10.gain_ref
  2.0 1.0 fusion
  3.0 1.0 pad_maximum_fusion
  4.0 11.5 %kv_proj.1 = (bf16[512,4096]{1,0:T(8,128)(2,1)}, bf16[512,512]{1,0:T(8,128)(2,1)}, bf16[512,512]{1,0:T(8,128)(2,1)}) custom-call(bf16[512,4096]{1,0:T(8,128)(2,1)} %refs_0_.3, bf16[1,4096]{1,0:T(2,128)(2,1)} %broadcast_in_dim.10.gain_ref, bf16[4096,512]{1,0:T(8,128)(2,1)} %wk_ref.1, bf16[4096,512]{1,0:T(8,128)(2,1)} %wv_ref.1, ...), custom_call_target="tpu_custom_call" | custom-call | flops 4294967296 | bytes 16777216 | tf_op jit(solution)/shard_map/kv_proj/pallas_call | solution.py:69
  15.4 1.3 collective-permute-start.2
  16.7 1.3 collective-permute-start.3
  18.0 1.3 collective-permute-start
  19.3 1.3 collective-permute-start.1
  20.6 0.6 pad_add_fusion.bounds_ref
  21.2 8.9 %collective-permute-done.2.kb = bf16[512,512]{1,0:T(8,128)(2,1)S(1)} collective-permute-done((bf16[512,512]{1,0:T(8,128)(2,1)}, bf16[512,512]{1,0:T(8,128)(2,1)S(1)}, u32[]{:S(2)}, u32[]{:S(2)}) %collective-permute-start.2) | collective-permute-done | bytes 524320 | tf_op jit(solution)/shard_map/ppermute | solution.py:251
  30.1 4.6 %collective-permute-start.4 = (bf16[512,512]{1,0:T(8,128)(2,1)S(1)}, bf16[512,512]{1,0:T(8,128)(2,1)S(1)}, u32[]{:S(2)}, u32[]{:S(2)}) collective-permute-start(bf16[512,512]{1,0:T(8,128)(2,1)S(1)} %collective-permute-done.2.kb), channel_id=1, source_target_pairs={{2,3},{3,2},{6,7},{7,6}} | collective-permute-start | bytes 1572872 | tf_op jit(solution)/shard_map/ppermute | solution.py:255
  34.7 6.7 %collective-permute-done.3.vb = bf16[512,512]{1,0:T(8,128)(2,1)S(1)} collective-permute-done((bf16[512,512]{1,0:T(8,128)(2,1)}, bf16[512,512]{1,0:T(8,128)(2,1)S(1)}, u32[]{:S(2)}, u32[]{:S(2)}) %collective-permute-start.3) | collective-permute-done | bytes 524320 | tf_op jit(solution)/shard_map/ppermute | solution.py:252
  41.4 3.6 collective-permute-start.5
  45.0 14.3 %q_proj.1.q_ref = bf16[512,2048]{1,0:T(8,128)(2,1)} custom-call(bf16[512,4096]{1,0:T(8,128)(2,1)} %get-tuple-element.10.n_ref, bf16[4096,2048]{1,0:T(8,128)(2,1)} %w_ref.7, f32[512,128]{1,0:T(8,128)} %get-tuple-element.24.cos_ref, f32[512,128]{1,0:T(8,128)} %get-tuple-element.25.sin_ref), custom_call_target="tpu_custom_call" | custom-call | flops 8589934592 | bytes 20971520 | tf_op jit(solution)/shard_map/q_proj/pallas_call | solution.py:89
  59.3 0.0 collective-permute-done.ka
  59.3 0.0 copy-start.4
  59.4 0.0 collective-permute-done.5.vc
  59.4 0.7 copy-done.4
  60.1 0.2 copy-done.5
  60.4 0.1 copy-done.6
  60.5 0.8 copy-done.7
  61.3 19.5 %attn_0.1.refs_2_ = bf16[128,4096]{1,0:T(8,128)(2,1)} custom-call(s32[2]{0:T(128)} %pad_add_fusion.bounds_ref, bf16[512,2048]{1,0:T(8,128)(2,1)} %q_proj.1.q_ref, bf16[512,512]{1,0:T(8,128)(2,1)} %get-tuple-element.11.k_ref, bf16[512,512]{1,0:T(8,128)(2,1)} %get-tuple-element.12.v_ref, bf16[512,512]{1,0:T(8,128)(2,1)} %copy-done.4, ...), custom_call_target="tpu_custom_call" | custom-call | flops 3221225472 | bytes 16777216 | tf_op jit(solution)/shard_map/attn_0/pallas_call | solution.py:161
  80.8 0.0 copy-start.19
  80.8 1.3 collective-permute-start.6
  82.1 20.2 %attn_128.1.refs_4_ = bf16[128,4096]{1,0:T(8,128)(2,1)} custom-call(s32[2]{0:T(128)} %pad_add_fusion.bounds_ref, bf16[512,2048]{1,0:T(8,128)(2,1)} %q_proj.1.q_ref, bf16[512,512]{1,0:T(8,128)(2,1)} %get-tuple-element.11.k_ref, bf16[512,512]{1,0:T(8,128)(2,1)} %get-tuple-element.12.v_ref, bf16[512,512]{1,0:T(8,128)(2,1)} %copy-done.4, ...), custom_call_target="tpu_custom_call" | custom-call | flops 3221225472 | bytes 16777216 | tf_op jit(solution)/shard_map/attn_128/pallas_call | solution.py:161
  102.3 0.3 collective-permute-start.7
  102.6 0.9 reshape.24
  103.5 0.9 reshape.25
  104.4 0.6 broadcast_in_dim.4.refs_1_
  105.0 20.0 %attn_256.1.refs_2_ = bf16[128,4096]{1,0:T(8,128)(2,1)} custom-call(s32[2]{0:T(128)} %pad_add_fusion.bounds_ref, bf16[512,2048]{1,0:T(8,128)(2,1)} %q_proj.1.q_ref, bf16[512,512]{1,0:T(8,128)(2,1)} %get-tuple-element.11.k_ref, bf16[512,512]{1,0:T(8,128)(2,1)} %get-tuple-element.12.v_ref, bf16[512,512]{1,0:T(8,128)(2,1)} %copy-done.4, ...), custom_call_target="tpu_custom_call" | custom-call | flops 3221225472 | bytes 16777216 | tf_op jit(solution)/shard_map/attn_256/pallas_call | solution.py:161
  125.0 1.2 collective-permute-start.11
  126.2 21.5 %attn_384.1.refs_4_ = bf16[128,4096]{1,0:T(8,128)(2,1)} custom-call(s32[2]{0:T(128)} %pad_add_fusion.bounds_ref, bf16[512,2048]{1,0:T(8,128)(2,1)} %q_proj.1.q_ref, bf16[512,512]{1,0:T(8,128)(2,1)} %get-tuple-element.11.k_ref, bf16[512,512]{1,0:T(8,128)(2,1)} %get-tuple-element.12.v_ref, bf16[512,512]{1,0:T(8,128)(2,1)} %copy-done.4, ...), custom_call_target="tpu_custom_call" | custom-call | flops 3221225472 | bytes 16777216 | tf_op jit(solution)/shard_map/attn_384/pallas_call | solution.py:161
  147.7 0.3 collective-permute-start.12
  148.0 0.0 collective-permute-done.6.refs_3_
  148.0 0.0 collective-permute-done.7.refs_5_
  148.0 1.1 copy-done.17
  149.1 1.0 copy-done.18
  150.1 43.7 %gate_up_0.1 = (bf16[256,4096]{1,0:T(8,128)(2,1)}, bf16[256,6144]{1,0:T(8,128)(2,1)}) custom-call(bf16[512,4096]{1,0:T(8,128)(2,1)} %refs_0_.3, bf16[1,4096]{1,0:T(2,128)(2,1)} %broadcast_in_dim.4.refs_1_, bf16[128,4096]{1,0:T(8,128)(2,1)} %attn_0.1.refs_2_, bf16[128,4096]{1,0:T(8,128)(2,1)} %copy-done.17, bf16[128,4096]{1,0:T(8,128)(2,1)} %attn_128.1.refs_4_, ...), custom_call_target="tpu_custom_call" | custom-call | flops 25769803776 | bytes 100663296 | tf_op jit(solution)/shard_map/gate_up_0/pallas_call | solution.py:207
  193.8 8.0 %down_a_1024.1 = bf16[256,1024]{1,0:T(8,128)(2,1)} custom-call(bf16[256,6144]{1,0:T(8,128)(2,1)} %get-tuple-element.14.act_ref, bf16[6144,4096]{1,0:T(8,128)(2,1)} %w_ref.13), custom_call_target="tpu_custom_call" | custom-call | flops 3221225472 | bytes 12582912 | tf_op jit(solution)/shard_map/down_a_1024/pallas_call | solution.py:225
  201.8 8.2 %down_a_0.1 = bf16[256,1024]{1,0:T(8,128)(2,1)} custom-call(bf16[256,6144]{1,0:T(8,128)(2,1)} %get-tuple-element.14.act_ref, bf16[6144,4096]{1,0:T(8,128)(2,1)} %w_ref.13), custom_call_target="tpu_custom_call" | custom-call | flops 3221225472 | bytes 12582912 | tf_op jit(solution)/shard_map/down_a_0/pallas_call | solution.py:225
  210.1 13.1 %down_a_2048.1 = bf16[256,2048]{1,0:T(8,128)(2,1)} custom-call(bf16[256,6144]{1,0:T(8,128)(2,1)} %get-tuple-element.14.act_ref, bf16[6144,4096]{1,0:T(8,128)(2,1)} %w_ref.13), custom_call_target="tpu_custom_call" | custom-call | flops 6442450944 | bytes 25165824 | tf_op jit(solution)/shard_map/down_a_2048/pallas_call | solution.py:225
  223.2 0.0 collective-permute-done.11.refs_3_
  223.2 0.0 collective-permute-done.12.refs_5_
  223.2 1.0 copy-done.16
  224.2 43.6 %gate_up_256.1 = (bf16[256,4096]{1,0:T(8,128)(2,1)}, bf16[256,6144]{1,0:T(8,128)(2,1)}) custom-call(bf16[512,4096]{1,0:T(8,128)(2,1)} %refs_0_.3, bf16[1,4096]{1,0:T(2,128)(2,1)} %broadcast_in_dim.4.refs_1_, bf16[128,4096]{1,0:T(8,128)(2,1)} %attn_256.1.refs_2_, bf16[128,4096]{1,0:T(8,128)(2,1)} %copy-done.16, bf16[128,4096]{1,0:T(8,128)(2,1)} %attn_384.1.refs_4_, ...), custom_call_target="tpu_custom_call" | custom-call | flops 25769803776 | bytes 100663296 | tf_op jit(solution)/shard_map/gate_up_256/pallas_call | solution.py:207
  267.8 8.1 %down_b_1024.1 = bf16[256,1024]{1,0:T(8,128)(2,1)} custom-call(bf16[256,6144]{1,0:T(8,128)(2,1)} %get-tuple-element.16.act_ref, bf16[6144,4096]{1,0:T(8,128)(2,1)} %w_ref.13), custom_call_target="tpu_custom_call" | custom-call | flops 3221225472 | bytes 12582912 | tf_op jit(solution)/shard_map/down_b_1024/pallas_call | solution.py:225
  275.9 8.2 %down_b_0.1 = bf16[256,1024]{1,0:T(8,128)(2,1)} custom-call(bf16[256,6144]{1,0:T(8,128)(2,1)} %get-tuple-element.16.act_ref, bf16[6144,4096]{1,0:T(8,128)(2,1)} %w_ref.13), custom_call_target="tpu_custom_call" | custom-call | flops 3221225472 | bytes 12582912 | tf_op jit(solution)/shard_map/down_b_0/pallas_call | solution.py:225
  284.1 1.2 collective-permute-start.8
  285.3 0.3 collective-permute-start.9
  285.6 1.2 collective-permute-start.10
  286.8 0.3 collective-permute-start.13
  287.0 1.2 collective-permute-start.14
  288.2 13.1 %down_b_2048.1 = bf16[256,2048]{1,0:T(8,128)(2,1)} custom-call(bf16[256,6144]{1,0:T(8,128)(2,1)} %get-tuple-element.16.act_ref, bf16[6144,4096]{1,0:T(8,128)(2,1)} %w_ref.13), custom_call_target="tpu_custom_call" | custom-call | flops 6442450944 | bytes 25165824 | tf_op jit(solution)/shard_map/down_b_2048/pallas_call | solution.py:225
  301.3 0.0 collective-permute-done.8
  301.3 0.3 collective-permute-start.15
  301.6 7.7 %collective-permute-done.9 = bf16[256,1024]{1,0:T(8,128)(2,1)} collective-permute-done((bf16[256,1024]{1,0:T(8,128)(2,1)S(1)}, bf16[256,1024]{1,0:T(8,128)(2,1)}, u32[]{:S(2)}, u32[]{:S(2)}) %collective-permute-start.9) | collective-permute-done | bytes 524320 | tf_op jit(solution)/shard_map/ppermute | solution.py:281
  309.4 2.3 add_convert_fusion.5
  311.7 31.3 %collective-permute-done.13 = bf16[256,1024]{1,0:T(8,128)(2,1)} collective-permute-done((bf16[256,1024]{1,0:T(8,128)(2,1)}, bf16[256,1024]{1,0:T(8,128)(2,1)}, u32[]{:S(2)}, u32[]{:S(2)}) %collective-permute-start.13) | collective-permute-done | bytes 524320 | tf_op jit(solution)/shard_map/ppermute | solution.py:281
  343.0 10.4 %collective-permute-done.14 = bf16[256,1024]{1,0:T(8,128)(2,1)} collective-permute-done((bf16[256,1024]{1,0:T(8,128)(2,1)S(1)}, bf16[256,1024]{1,0:T(8,128)(2,1)}, u32[]{:S(2)}, u32[]{:S(2)}) %collective-permute-start.14) | collective-permute-done | bytes 524320 | tf_op jit(solution)/shard_map/ppermute | solution.py:281
  353.4 1.9 add_convert_fusion.3
  355.3 0.5 add_convert_fusion.1
  355.9 8.8 %collective-permute-done.15 = bf16[256,2048]{1,0:T(8,128)(2,1)S(1)} collective-permute-done((bf16[256,2048]{1,0:T(8,128)(2,1)}, bf16[256,2048]{1,0:T(8,128)(2,1)S(1)}, u32[]{:S(2)}, u32[]{:S(2)}) %collective-permute-start.15) | collective-permute-done | bytes 1048608 | tf_op jit(solution)/shard_map/ppermute | solution.py:281
  364.6 0.5 add_convert_fusion
  365.2 22.6 %maximum_maximum_fusion = bf16[512,4096]{1,0:T(8,128)(2,1)} fusion(bf16[256,2048]{1,0:T(8,128)(2,1)S(1)} %add_convert_fusion, bf16[256,1024]{1,0:T(8,128)(2,1)S(1)} %get-tuple-element.20, bf16[256,1024]{1,0:T(8,128)(2,1)S(1)} %get-tuple-element.19, bf16[256,2048]{1,0:T(8,128)(2,1)S(1)} %add_convert_fusion.1, bf16[256,1024]{1,0:T(8,128)(2,1)S(1)} %get-tuple-element.18, ...), kind=kLoop, calls=%fused_computation | loop fusion | flops 25165824 | bytes 8388608 | tf_op jit(solution)/shard_map/concatenate | solution.py:285
  (36 shorter events, 0.1 us)
Async XLA Ops:
  15.4 14.7 %collective-permute-start.2 = (bf16[512,512]{1,0:T(8,128)(2,1)}, bf16[512,512]{1,0:T(8,128)(2,1)S(1)}, u32[]{:S(2)}, u32[]{:S(2)}) collective-permute-start(bf16[512,512]{1,0:T(8,128)(2,1)} %get-tuple-element.11.k_ref), channel_id=1, source_target_pairs={{0,2},{1,3},{4,6},{5,7}} | collective-permute-start | bytes 1572872 | tf_op jit(solution)/shard_map/ppermute | solution.py:251
  16.7 24.6 %collective-permute-start.3 = (bf16[512,512]{1,0:T(8,128)(2,1)}, bf16[512,512]{1,0:T(8,128)(2,1)S(1)}, u32[]{:S(2)}, u32[]{:S(2)}) collective-permute-start(bf16[512,512]{1,0:T(8,128)(2,1)} %get-tuple-element.12.v_ref), channel_id=1, source_target_pairs={{0,2},{1,3},{4,6},{5,7}} | collective-permute-start | bytes 1572872 | tf_op jit(solution)/shard_map/ppermute | solution.py:252
  18.0 41.3 %collective-permute-start = (bf16[512,512]{1,0:T(8,128)(2,1)}, bf16[512,512]{1,0:T(8,128)(2,1)S(1)}, u32[]{:S(2)}, u32[]{:S(2)}) collective-permute-start(bf16[512,512]{1,0:T(8,128)(2,1)} %get-tuple-element.11.k_ref), channel_id=1, source_target_pairs={{0,1},{2,3},{4,5},{6,7}} | collective-permute-start | bytes 1572872 | tf_op jit(solution)/shard_map/ppermute | solution.py:253
  19.3 40.0 %collective-permute-start.1 = (bf16[512,512]{1,0:T(8,128)(2,1)}, bf16[512,512]{1,0:T(8,128)(2,1)S(1)}, u32[]{:S(2)}, u32[]{:S(2)}) collective-permute-start(bf16[512,512]{1,0:T(8,128)(2,1)} %get-tuple-element.12.v_ref), channel_id=1, source_target_pairs={{0,1},{2,3},{4,5},{6,7}} | collective-permute-start | bytes 1572872 | tf_op jit(solution)/shard_map/ppermute | solution.py:254
  30.1 29.2 %copy-start.2 = (bf16[512,512]{1,0:T(8,128)(2,1)}, bf16[512,512]{1,0:T(8,128)(2,1)S(1)}, u32[]{:S(2)}) copy-start(bf16[512,512]{1,0:T(8,128)(2,1)S(1)} %collective-permute-done.2.kb) | copy-start | bytes 1572868
  30.1 29.2 %collective-permute-start.4 = (bf16[512,512]{1,0:T(8,128)(2,1)S(1)}, bf16[512,512]{1,0:T(8,128)(2,1)S(1)}, u32[]{:S(2)}, u32[]{:S(2)}) collective-permute-start(bf16[512,512]{1,0:T(8,128)(2,1)S(1)} %collective-permute-done.2.kb), channel_id=1, source_target_pairs={{2,3},{3,2},{6,7},{7,6}} | collective-permute-start | bytes 1572872 | tf_op jit(solution)/shard_map/ppermute | solution.py:255
  41.4 18.0 %copy-start.3 = (bf16[512,512]{1,0:T(8,128)(2,1)}, bf16[512,512]{1,0:T(8,128)(2,1)S(1)}, u32[]{:S(2)}) copy-start(bf16[512,512]{1,0:T(8,128)(2,1)S(1)} %collective-permute-done.3.vb) | copy-start | bytes 1572868
  41.4 18.0 %collective-permute-start.5 = (bf16[512,512]{1,0:T(8,128)(2,1)S(1)}, bf16[512,512]{1,0:T(8,128)(2,1)S(1)}, u32[]{:S(2)}, u32[]{:S(2)}) collective-permute-start(bf16[512,512]{1,0:T(8,128)(2,1)S(1)} %collective-permute-done.3.vb), channel_id=1, source_target_pairs={{2,3},{3,2},{6,7},{7,6}} | collective-permute-start | bytes 1572872 | tf_op jit(solution)/shard_map/ppermute | solution.py:256
  59.3 0.8 copy-start.4
  59.4 1.0 copy-start.5
  59.4 1.1 copy-start.6
  60.5 0.8 copy-start.7
  80.8 21.8 %copy-start = (bf16[512,512]{1,0:T(8,128)(2,1)S(1)}, bf16[512,512]{1,0:T(8,128)(2,1)}, u32[]{:S(2)}) copy-start(bf16[512,512]{1,0:T(8,128)(2,1)} %get-tuple-element.11.k_ref) | copy-start | bytes 1572868
  80.8 22.7 %copy-start.1 = (bf16[512,512]{1,0:T(8,128)(2,1)S(1)}, bf16[512,512]{1,0:T(8,128)(2,1)}, u32[]{:S(2)}) copy-start(bf16[512,512]{1,0:T(8,128)(2,1)} %get-tuple-element.12.v_ref) | copy-start | bytes 1572868
  80.8 23.6 %copy-start.19 = (bf16[4096]{0:T(1024)(128)(2,1)S(1)}, bf16[4096]{0:T(1024)(128)(2,1)}, u32[]{:S(2)}) copy-start(bf16[4096]{0:T(1024)(128)(2,1)} %param.16) | copy-start | bytes 24580
  80.8 67.2 %collective-permute-start.6 = (bf16[128,4096]{1,0:T(8,128)(2,1)}, bf16[128,4096]{1,0:T(8,128)(2,1)S(1)}, u32[]{:S(2)}, u32[]{:S(2)}) collective-permute-start(bf16[128,4096]{1,0:T(8,128)(2,1)} %attn_0.1.refs_2_), channel_id=1, source_target_pairs={{0,4},{4,0},{1,5},{5,1},{2,6},{6,2},{3,7},{7,3}} | collective-permute-start | bytes 3145736 | tf_op jit(solution)/shard_map/ppermute | solution.py:267
  102.3 45.7 %collective-permute-start.7 = (bf16[128,4096]{1,0:T(8,128)(2,1)}, bf16[128,4096]{1,0:T(8,128)(2,1)S(1)}, u32[]{:S(2)}, u32[]{:S(2)}) collective-permute-start(bf16[128,4096]{1,0:T(8,128)(2,1)} %attn_128.1.refs_4_), channel_id=1, source_target_pairs={{0,4},{4,0},{1,5},{5,1},{2,6},{6,2},{3,7},{7,3}} | collective-permute-start | bytes 3145736 | tf_op jit(solution)/shard_map/ppermute | solution.py:267
  125.0 98.2 %collective-permute-start.11 = (bf16[128,4096]{1,0:T(8,128)(2,1)}, bf16[128,4096]{1,0:T(8,128)(2,1)S(1)}, u32[]{:S(2)}, u32[]{:S(2)}) collective-permute-start(bf16[128,4096]{1,0:T(8,128)(2,1)} %attn_256.1.refs_2_), channel_id=1, source_target_pairs={{0,4},{4,0},{1,5},{5,1},{2,6},{6,2},{3,7},{7,3}} | collective-permute-start | bytes 3145736 | tf_op jit(solution)/shard_map/ppermute | solution.py:267
  147.7 75.5 %collective-permute-start.12 = (bf16[128,4096]{1,0:T(8,128)(2,1)}, bf16[128,4096]{1,0:T(8,128)(2,1)}, u32[]{:S(2)}, u32[]{:S(2)}) collective-permute-start(bf16[128,4096]{1,0:T(8,128)(2,1)} %attn_384.1.refs_4_), channel_id=1, source_target_pairs={{0,4},{4,0},{1,5},{5,1},{2,6},{6,2},{3,7},{7,3}} | collective-permute-start | bytes 3145736 | tf_op jit(solution)/shard_map/ppermute | solution.py:267
  148.0 1.1 copy-start.17
  149.1 1.0 copy-start.18
  223.2 1.0 copy-start.16
  275.9 8.2 %copy-start.11 = (bf16[256,1024]{1,0:T(8,128)(2,1)S(1)}, bf16[256,1024]{1,0:T(8,128)(2,1)}, u32[]{:S(2)}) copy-start(bf16[256,1024]{1,0:T(8,128)(2,1)} %down_a_0.1) | copy-start | bytes 1572868
  275.9 9.4 %copy-start.10 = (bf16[256,1024]{1,0:T(8,128)(2,1)S(1)}, bf16[256,1024]{1,0:T(8,128)(2,1)}, u32[]{:S(2)}) copy-start(bf16[256,1024]{1,0:T(8,128)(2,1)} %down_a_1024.1) | copy-start | bytes 1572868
  275.9 9.7 %copy-start.8 = (bf16[256,2048]{1,0:T(8,128)(2,1)S(1)}, bf16[256,2048]{1,0:T(8,128)(2,1)}, u32[]{:S(2)}) copy-start(bf16[256,2048]{1,0:T(8,128)(2,1)} %down_a_2048.1) | copy-start | bytes 3145732
  275.9 11.2 %copy-start.12 = (bf16[256,1024]{1,0:T(8,128)(2,1)S(1)}, bf16[256,1024]{1,0:T(8,128)(2,1)}, u32[]{:S(2)}) copy-start(bf16[256,1024]{1,0:T(8,128)(2,1)} %down_b_1024.1) | copy-start | bytes 1572868
  284.1 17.2 %collective-permute-start.8 = (bf16[256,1024]{1,0:T(8,128)(2,1)S(1)}, bf16[256,1024]{1,0:T(8,128)(2,1)}, u32[]{:S(2)}, u32[]{:S(2)}) collective-permute-start(bf16[256,1024]{1,0:T(8,128)(2,1)S(1)} %copy-done.11), channel_id=1, source_target_pairs={{0,4},{4,0},{1,5},{5,1},{2,6},{6,2},{3,7},{7,3}} | collective-permute-start | bytes 1572872 | tf_op jit(solution)/shard_map/ppermute | solution.py:281
  285.3 24.1 %collective-permute-start.9 = (bf16[256,1024]{1,0:T(8,128)(2,1)S(1)}, bf16[256,1024]{1,0:T(8,128)(2,1)}, u32[]{:S(2)}, u32[]{:S(2)}) collective-permute-start(bf16[256,1024]{1,0:T(8,128)(2,1)S(1)} %copy-done.10), channel_id=1, source_target_pairs={{0,4},{4,0},{1,5},{5,1},{2,6},{6,2},{3,7},{7,3}} | collective-permute-start | bytes 1572872 | tf_op jit(solution)/shard_map/ppermute | solution.py:281
  285.6 69.7 %collective-permute-start.10 = (bf16[256,2048]{1,0:T(8,128)(2,1)S(1)}, bf16[256,2048]{1,0:T(8,128)(2,1)S(1)}, u32[]{:S(2)}, u32[]{:S(2)}) collective-permute-start(bf16[256,2048]{1,0:T(8,128)(2,1)S(1)} %copy-done.8), channel_id=1, source_target_pairs={{0,4},{4,0},{1,5},{5,1},{2,6},{6,2},{3,7},{7,3}} | collective-permute-start | bytes 3145736 | tf_op jit(solution)/shard_map/ppermute | solution.py:281
  286.8 56.2 %collective-permute-start.13 = (bf16[256,1024]{1,0:T(8,128)(2,1)}, bf16[256,1024]{1,0:T(8,128)(2,1)}, u32[]{:S(2)}, u32[]{:S(2)}) collective-permute-start(bf16[256,1024]{1,0:T(8,128)(2,1)} %down_b_0.1), channel_id=1, source_target_pairs={{0,4},{4,0},{1,5},{5,1},{2,6},{6,2},{3,7},{7,3}} | collective-permute-start | bytes 1572872 | tf_op jit(solution)/shard_map/ppermute | solution.py:281
  287.0 66.3 %collective-permute-start.14 = (bf16[256,1024]{1,0:T(8,128)(2,1)S(1)}, bf16[256,1024]{1,0:T(8,128)(2,1)}, u32[]{:S(2)}, u32[]{:S(2)}) collective-permute-start(bf16[256,1024]{1,0:T(8,128)(2,1)S(1)} %copy-done.12), channel_id=1, source_target_pairs={{0,4},{4,0},{1,5},{5,1},{2,6},{6,2},{3,7},{7,3}} | collective-permute-start | bytes 1572872 | tf_op jit(solution)/shard_map/ppermute | solution.py:281
  301.3 52.0 %copy-start.13 = (bf16[256,1024]{1,0:T(8,128)(2,1)S(1)}, bf16[256,1024]{1,0:T(8,128)(2,1)}, u32[]{:S(2)}) copy-start(bf16[256,1024]{1,0:T(8,128)(2,1)} %down_b_0.1) | copy-start | bytes 1572868
  301.3 52.0 %copy-start.15 = (bf16[256,4096]{1,0:T(8,128)(2,1)S(1)}, bf16[256,4096]{1,0:T(8,128)(2,1)}, u32[]{:S(2)}) copy-start(bf16[256,4096]{1,0:T(8,128)(2,1)} %get-tuple-element.15) | copy-start | bytes 6291460
  301.3 63.3 %collective-permute-start.15 = (bf16[256,2048]{1,0:T(8,128)(2,1)}, bf16[256,2048]{1,0:T(8,128)(2,1)S(1)}, u32[]{:S(2)}, u32[]{:S(2)}) collective-permute-start(bf16[256,2048]{1,0:T(8,128)(2,1)} %down_b_2048.1), channel_id=1, source_target_pairs={{0,4},{4,0},{1,5},{5,1},{2,6},{6,2},{3,7},{7,3}} | collective-permute-start | bytes 3145736 | tf_op jit(solution)/shard_map/ppermute | solution.py:281
  309.4 45.9 %copy-start.14 = (bf16[256,4096]{1,0:T(8,128)(2,1)S(1)}, bf16[256,4096]{1,0:T(8,128)(2,1)}, u32[]{:S(2)}) copy-start(bf16[256,4096]{1,0:T(8,128)(2,1)} %get-tuple-element.13) | copy-start | bytes 6291460
  353.4 11.2 %copy-start.9 = (bf16[256,2048]{1,0:T(8,128)(2,1)S(1)}, bf16[256,2048]{1,0:T(8,128)(2,1)}, u32[]{:S(2)}) copy-start(bf16[256,2048]{1,0:T(8,128)(2,1)} %down_b_2048.1) | copy-start | bytes 3145732

commit v2 on v0

v2 whole, which is shorter than its diff:
```python
import functools
import jax
import jax.numpy as jnp
from jax import lax
from jax.experimental import pallas as pl
from jax.experimental.pallas import tpu as pltpu
from jax.sharding import PartitionSpec as P

HEAD_DIM = 128
ROPE_THETA = 1000000.0
NORM_EPS = 1e-5
MASK_VALUE = -1e30
EXP2_SCALE = HEAD_DIM ** -0.5 * 1.4426950408889634
BF = jnp.bfloat16
F32 = jnp.float32
VMEM_BIG = 60 * 1024 * 1024
ANY = pl.BlockSpec(memory_space=pl.ANY)


def cost(flops, nbytes):
    return pl.CostEstimate(flops=flops, bytes_accessed=nbytes, transcendentals=0)


def params():
    return pltpu.CompilerParams(vmem_limit_bytes=VMEM_BIG)


def rope_tables(positions):
    inv_freq = jnp.asarray(ROPE_THETA, F32) ** (-jnp.arange(0, HEAD_DIM, 2, dtype=F32) / HEAD_DIM)
    angles = positions.astype(F32)[:, None] * inv_freq[None, :]
    return jnp.cos(angles), jnp.sin(angles)


def norm_rows(rows, gain_row):
    inv_rms = lax.rsqrt(jnp.mean(rows * rows, axis=-1, keepdims=True) + NORM_EPS)
    return (rows * inv_rms * gain_row.astype(F32)).astype(BF)


def rope_block(prod, cos_full, sin_full):
    pieces = []
    for head in range(prod.shape[1] // HEAD_DIM):
        u = prod[:, head * HEAD_DIM:(head + 1) * HEAD_DIM].astype(BF).astype(F32)
        pieces.append((u * cos_full + pltpu.roll(u, HEAD_DIM // 2, 1) * sin_full).astype(BF))
    return jnp.concatenate(pieces, axis=1)


def kv_kernel(x_ref, gain_ref, wk_ref, wv_ref, cos_ref, sin_ref, n_ref, kv_ref):
    step = pl.program_id(0)

    @pl.when(step == 0)
    def _():
        def chunk(i, c):
            rows = pl.ds(pl.multiple_of(i * 64, 64), 64)
            n_ref[rows, :] = norm_rows(x_ref[rows, :].astype(F32), gain_ref[...])
            return c
        lax.fori_loop(0, x_ref.shape[0] // 64, chunk, 0)
    n = n_ref[...]
    bn = wk_ref.shape[1]
    cols = kv_ref.shape[1] // 2
    k = jnp.dot(n, wk_ref[...], preferred_element_type=F32)
    kv_ref[:, pl.ds(pl.multiple_of(step * bn, bn), bn)] = rope_block(k, cos_ref[...], sin_ref[...])
    kv_ref[:, pl.ds(pl.multiple_of(cols + step * bn, bn), bn)] = jnp.dot(n, wv_ref[...], preferred_element_type=F32).astype(BF)


def kv_proj(x, gain, w_k, w_v, cos_full, sin_full):
    rows, width = x.shape
    cols = w_k.shape[1]
    bn = 256
    whole = lambda a: pl.BlockSpec(a.shape, lambda i: (0, 0))
    wspec = pl.BlockSpec((width, bn), lambda i: (0, i))
    return pl.pallas_call(
        kv_kernel, grid=(cols // bn,),
        in_specs=[whole(x), whole(gain), wspec, wspec, whole(cos_full), whole(sin_full)],
        out_specs=[pl.BlockSpec((rows, width), lambda i: (0, 0)), pl.BlockSpec((rows, 2 * cols), lambda i: (0, 0))],
        out_shape=[jax.ShapeDtypeStruct((rows, width), BF), jax.ShapeDtypeStruct((rows, 2 * cols), BF)],
        compiler_params=params(), name='kv_proj',
        cost_estimate=cost(4 * rows * width * cols, 2 * 2 * width * (rows + cols)),
    )(x, gain, w_k, w_v, cos_full, sin_full)


def q_kernel(n_ref, w_ref, cos_ref, sin_ref, q_ref):
    prod = jnp.dot(n_ref[...], w_ref[...], preferred_element_type=F32)
    q_ref[...] = rope_block(prod, cos_ref[...], sin_ref[...])


def q_proj(n, w_q, cos_full, sin_full):
    rows, width = n.shape
    cols = w_q.shape[1]
    bn = 512
    whole = lambda a: pl.BlockSpec(a.shape, lambda i: (0, 0))
    return pl.pallas_call(
        q_kernel, grid=(cols // bn,),
        in_specs=[whole(n), pl.BlockSpec((width, bn), lambda i: (0, i)), whole(cos_full), whole(sin_full)],
        out_specs=pl.BlockSpec((rows, bn), lambda i: (0, i)),
        out_shape=jax.ShapeDtypeStruct((rows, cols), BF),
        compiler_params=params(), name='q_proj',
        cost_estimate=cost(2 * rows * width * cols, 2 * width * (rows + cols)),
    )(n, w_q, cos_full, sin_full)


MESH = pl.DeviceIdType.MESH
CHUNK = 128
HALF = 256
BLK = 512


def at(i, size):
    return pl.ds(pl.multiple_of(i * size, size), size)


def layer_kernel(gain_ref, q_ref, kv_ref, x_ref, kva, kvb, kvc, wo_ref, wg_ref, wu_ref, wd_ref, out_ref,
                 send_buf, recv_buf, h_buf, m_buf, act_buf, g_buf, u_buf, d_buf, k_buf, o_buf, m_sc, l_sc, acc_sc,
                 kv_sem, x_sem, wo_sem, g_sem, u_sem, d_sem, ps_sem, pr_sem, ds_sem, dr_sem, out_sem, free_sem):
    cp = lax.axis_index('cp')
    peer = {'tp': 1 - lax.axis_index('tp')}
    tok, width = q_ref.shape[0], wo_ref.shape[1]
    n_blk = width // BLK
    n_gu = wg_ref.shape[1] // BLK
    kcols = kv_ref.shape[1] // 2
    n_kv = kcols // HEAD_DIM
    groups = q_ref.shape[1] // kcols
    n_chunk = tok // CHUNK
    depth_o = wo_ref.shape[0]
    ring = 2 * (d_buf.shape[1] // depth_o)
    stacked = groups * CHUNK

    def load_wo(t):
        slot = lax.rem(t, ring)
        dst = d_buf.at[slot // (ring // 2), at(lax.rem(slot, ring // 2), depth_o), :]
        return pltpu.make_async_copy(wo_ref.at[:, at(lax.rem(t, n_blk), BLK)], dst, wo_sem.at[slot])

    def load_gate(t):
        cols = at(lax.rem(t, n_gu), BLK)
        slot = lax.rem(t, 2)
        return (pltpu.make_async_copy(wg_ref.at[:, cols], g_buf.at[slot], g_sem.at[slot]),
                pltpu.make_async_copy(wu_ref.at[:, cols], u_buf.at[slot], u_sem.at[slot]))

    def load_down(t):
        slot = lax.rem(t, 2)
        return pltpu.make_async_copy(wd_ref.at[:, at(lax.rem(t, n_blk), BLK)], d_buf.at[slot], d_sem.at[slot])

    def load_x(j):
        return pltpu.make_async_copy(x_ref.at[:, at(j, BLK)], h_buf.at[j], x_sem.at[j])

    def part_copy(i, j):
        piece = (j, at(i, CHUNK), slice(None))
        return pltpu.make_async_remote_copy(send_buf.at[piece], recv_buf.at[piece], ps_sem.at[i, j], pr_sem.at[i, j],
                                            device_id=peer, device_id_type=MESH)

    def down_copy(s, j):
        piece = (j, at(s, HALF), slice(None))
        return pltpu.make_async_remote_copy(send_buf.at[piece], recv_buf.at[piece], ds_sem.at[s, j], dr_sem.at[s, j],
                                            device_id=peer, device_id_type=MESH)

    def out_copy(s, j):
        return pltpu.make_async_copy(h_buf.at[j, at(s, HALF), :], out_ref.at[at(s, HALF), at(j, BLK)], out_sem.at[s, j])

    def loop(n, body):
        def step(i, c):
            body(i)
            return c
        lax.fori_loop(0, n, step, 0)

    kv_copies = [pltpu.make_async_copy(src, k_buf.at[slot], kv_sem.at[slot]) for slot, src in enumerate((kva, kvb, kvc))]
    for c in kv_copies:
        c.start()
    loop(ring - 1, lambda t: load_wo(t).start())
    loop(n_blk, lambda j: load_x(j).start())
    for c in load_gate(0):
        c.start()

    barrier = pltpu.get_barrier_semaphore()
    pl.semaphore_signal(barrier, inc=1, device_id=peer, device_id_type=MESH)
    pl.semaphore_wait(barrier, 1)

    for c in kv_copies:
        c.wait()
    lo = jnp.where(cp == 2, 1, 0)
    hi = jnp.where(cp == 0, 0, jnp.where(cp == 1, 1, 3))

    for i in range(n_chunk):
        row0 = i * CHUNK
        n_keys = row0 + CHUNK

        def head_step(g):
            kcol = at(g, HEAD_DIM)
            vcol = pl.ds(pl.multiple_of(kcols + g * HEAD_DIM, HEAD_DIM), HEAD_DIM)
            q = jnp.concatenate([q_ref[row0:row0 + CHUNK, at(g * groups + j, HEAD_DIM)] for j in range(groups)], axis=0)
            s = lax.dot_general(q, kv_ref[:n_keys, kcol], (((1,), (1,)), ((), ())), preferred_element_type=F32)
            qpos = row0 + lax.rem(lax.broadcasted_iota(jnp.int32, (stacked, n_keys), 0), CHUNK)
            kpos = lax.broadcasted_iota(jnp.int32, (stacked, n_keys), 1)
            s = jnp.where(kpos <= qpos, s, MASK_VALUE)
            m0 = jnp.max(s, axis=-1, keepdims=True)
            p = jnp.exp2(s * EXP2_SCALE - m0 * EXP2_SCALE)
            m_sc[...] = jnp.broadcast_to(m0, m_sc.shape)
            l_sc[...] = jnp.broadcast_to(jnp.sum(p, axis=-1, keepdims=True), l_sc.shape)
            acc_sc[...] = jnp.dot(p.astype(BF), kv_ref[:n_keys, vcol], preferred_element_type=F32)

            def block_step(b, c):
                s = lax.dot_general(q, k_buf[b, :, kcol], (((1,), (1,)), ((), ())), preferred_element_type=F32)
                m_old = m_sc[...]
                m_new = jnp.maximum(m_old, jnp.max(s, axis=-1, keepdims=True))
                alpha = jnp.exp2((m_old - m_new) * EXP2_SCALE)
                p = jnp.exp2(s * EXP2_SCALE - m_new[:, :1] * EXP2_SCALE)
                l_sc[...] = l_sc[...] * alpha + jnp.sum(p, axis=-1, keepdims=True)
                acc_sc[...] = acc_sc[...] * alpha + jnp.dot(p.astype(BF), k_buf[b, :, vcol], preferred_element_type=F32)
                m_sc[...] = m_new
                return c
            lax.fori_loop(lo, hi, block_step, 0)
            out = (acc_sc[...] / l_sc[...]).astype(BF)
            for j in range(groups):
                o_buf[:, at(g * groups + j, HEAD_DIM)] = out[j * CHUNK:(j + 1) * CHUNK]
        loop(n_kv, head_step)

        def wo_step(j):
            t = i * n_blk + j

            @pl.when(t + ring - 1 < n_chunk * n_blk)
            def _():
                load_wo(t + ring - 1).start()
            load_wo(t).wait()
            slot = lax.rem(t, ring)
            w = d_buf[slot // (ring // 2), at(lax.rem(slot, ring // 2), depth_o), :]
            send_buf[j, row0:row0 + CHUNK, :] = jnp.dot(o_buf[...], w, preferred_element_type=F32).astype(BF)
            part_copy(i, j).start()
        loop(n_blk, wo_step)

    loop(n_blk, lambda j: load_x(j).wait())

    def half_step(s):
        def wait_part(r):
            c = part_copy(s * (HALF // CHUNK) + r // n_blk, lax.rem(r, n_blk))
            c.wait_recv()
            c.wait_send()
        loop(HALF // CHUNK * n_blk, wait_part)

        def h_step(r):
            rows = at(s * (HALF // 32) + r, 32)
            total = jnp.zeros((32, BLK), F32)
            for j in range(n_blk):
                add = send_buf[j, rows, :].astype(F32) + recv_buf[j, rows, :].astype(F32)
                h = (h_buf[j, rows, :].astype(F32) + add).astype(BF)
                h_buf[j, rows, :] = h
                wide = h.astype(F32)
                total += wide * wide
            inv = lax.rsqrt(jnp.sum(total, axis=-1, keepdims=True) / width + NORM_EPS)
            for j in range(n_blk):
                cols = slice(j * BLK, (j + 1) * BLK)
                m_buf[at(r, 32), cols] = (h_buf[j, rows, :].astype(F32) * inv * gain_ref[:, cols].astype(F32)).astype(BF)
        loop(HALF // 32, h_step)
        pl.semaphore_signal(free_sem.at[s], inc=1, device_id=peer, device_id_type=MESH)

        def gu_step(j):
            t = s * n_gu + j

            @pl.when(t + 1 < 2 * n_gu)
            def _():
                for c in load_gate(t + 1):
                    c.start()

            @pl.when(j == n_gu - 4)
            def _():
                load_down(s * n_blk).start()

            @pl.when(j == n_gu - 2)
            def _():
                load_down(s * n_blk + 1).start()
            for c in load_gate(t):
                c.wait()
            slot = lax.rem(t, 2)
            gate = jnp.dot(m_buf[...], g_buf[slot], preferred_element_type=F32)
            up = jnp.dot(m_buf[...], u_buf[slot], preferred_element_type=F32)
            act_buf[:, at(j, BLK)] = (gate / (1.0 + jnp.exp(-gate)) * up).astype(BF)
        loop(n_gu, gu_step)
        pl.semaphore_wait(free_sem.at[s], 1)

        def down_step(j):
            t = s * n_blk + j
            load_down(t).wait()
            send_buf[j, at(s, HALF), :] = jnp.dot(act_buf[...], d_buf[lax.rem(t, 2)], preferred_element_type=F32).astype(BF)

            @pl.when(j + 2 < n_blk)
            def _():
                load_down(t + 2).start()
            down_copy(s, j).start()
        loop(n_blk, down_step)
    loop(2, half_step)

    def final_step(t):
        s, j = t // n_blk, lax.rem(t, n_blk)
        c = down_copy(s, j)
        c.wait_recv()
        rows = at(s, HALF)
        add = send_buf[j, rows, :].astype(F32) + recv_buf[j, rows, :].astype(F32)
        h_buf[j, rows, :] = (h_buf[j, rows, :].astype(F32) + add).astype(BF)
        out_copy(s, j).start()
    loop(2 * n_blk, final_step)

    def drain(t):
        s, j = t // n_blk, lax.rem(t, n_blk)
        down_copy(s, j).wait_send()
        out_copy(s, j).wait()
    loop(2 * n_blk, drain)


def fused_layer(gain, q, kv, x, kva, kvb, kvc, w_o, w_gate, w_up, w_down):
    tok, width = x.shape
    qcols = q.shape[1]
    n_blk = width // BLK
    ff = w_gate.shape[1]
    n_chunk = tok // CHUNK
    stacked = CHUNK * (2 * qcols // kv.shape[1])
    vmem = pl.BlockSpec(memory_space=pltpu.VMEM)
    ring = 2 * (ff // qcols)
    dma = pltpu.SemaphoreType.DMA
    return pl.pallas_call(
        layer_kernel,
        in_specs=[vmem, vmem, vmem] + [ANY] * 8,
        out_specs=ANY,
        out_shape=jax.ShapeDtypeStruct((tok, width), BF),
        scratch_shapes=[
            pltpu.VMEM((n_blk, tok, BLK), BF), pltpu.VMEM((n_blk, tok, BLK), BF), pltpu.VMEM((n_blk, tok, BLK), BF),
            pltpu.VMEM((HALF, width), BF), pltpu.VMEM((HALF, ff), BF),
            pltpu.VMEM((2, width, BLK), BF), pltpu.VMEM((2, width, BLK), BF), pltpu.VMEM((2, ff, BLK), BF),
            pltpu.VMEM((3,) + kv.shape, BF), pltpu.VMEM((CHUNK, qcols), BF),
            pltpu.VMEM((stacked, HEAD_DIM), F32), pltpu.VMEM((stacked, HEAD_DIM), F32), pltpu.VMEM((stacked, HEAD_DIM), F32),
            dma((3,)), dma((n_blk,)), dma((ring,)), dma((2,)), dma((2,)), dma((2,)),
            dma((n_chunk, n_blk)), dma((n_chunk, n_blk)), dma((2, n_blk)), dma((2, n_blk)), dma((2, n_blk)),
            pltpu.SemaphoreType.REGULAR((2,))],
        compiler_params=pltpu.CompilerParams(vmem_limit_bytes=67043328, collective_id=0, has_side_effects=True),
        name='fused_layer',
        cost_estimate=cost(2 * tok * width * (qcols + 3 * ff), 2 * width * (qcols + 6 * ff)),
    )(gain, q, kv, x, kva, kvb, kvc, w_o, w_gate, w_up, w_down)


def solution(mesh):
    row_spec = P(('dp', 'cp'), None)
    cache_spec = P(('dp', 'cp'), 'tp', None)
    col_spec = P(None, 'tp')
    split_rows = P('tp', None)
    vec_spec = P(None)

    def local_layer(x, attn_gain, w_q, w_k, w_v, w_o, mlp_gain, w_gate, w_up, w_down):
        tok = x.shape[0]
        kv_local = w_k.shape[1] // HEAD_DIM
        cp_index = lax.axis_index('cp')
        cos_tab, sin_tab = rope_tables(cp_index * tok + jnp.arange(tok))
        cos_full = jnp.concatenate([cos_tab, cos_tab], axis=1)
        sin_full = jnp.concatenate([-sin_tab, sin_tab], axis=1)
        n, kv = kv_proj(x, attn_gain[None, :], w_k, w_v, cos_full, sin_full)
        kvb = lax.ppermute(kv, 'cp', [(0, 2), (1, 3)])
        kva = lax.ppermute(kv, 'cp', [(0, 1), (2, 3)])
        q = q_proj(n, w_q, cos_full, sin_full)
        kvc = lax.ppermute(kvb, 'cp', [(2, 3), (3, 2)])
        x_out = fused_layer(mlp_gain[None, :], q, kv, x, kva, kvb, kvc, w_o, w_gate, w_up, w_down)
        kcols = kv.shape[1] // 2
        k, v = kv[:, :kcols], kv[:, kcols:]
        return x_out, k.reshape(tok, kv_local, HEAD_DIM), v.reshape(tok, kv_local, HEAD_DIM)

    return jax.shard_map(local_layer, mesh=mesh,
                         in_specs=(row_spec, vec_spec, col_spec, col_spec, col_spec, split_rows, vec_spec, col_spec, col_spec, split_rows),
                         out_specs=(row_spec, cache_spec, cache_spec), check_vma=False)
```

time: 570 us -> 272 us (0.48); the launches traced: 561 us -> 271 us
  Pallas kernels: 0 us -> 229 us
  matrix products: 218 us -> 0 us
  waiting for transfers between devices: 236 us -> 22.7 us
  other arithmetic: 62.4 us -> 2.01 us
  local copies, waits for them, and re-layouts: 27.5 us -> 10.7 us
  between operations: 14.8 us -> 0.72 us
    pallas_call x0 -> x3, Pallas kernels: none -> 229 us  [the longest x1 203 us: fused_layer(): pl.pallas_call(layer_kernel, in_specs=[vmem, vmem, vmem] + [ANY] * 8, out...]
    dot_general x15 -> x0, matrix products: 218 us -> none  [the longest x4 42.8 us: tile_step(): jnp.einsum('kgqs,skd->kgqd', exp_scores.astype(jnp.bfloat16), v_tile, pre...]
    psum x2 -> x0, waiting for transfers between devices: 203 us -> none  [the longest x1 103 us: local_layer(): attn_total = lax.psum(attn_part, 'tp')]
    reduce_sum x6 -> x0, other arithmetic: 45.2 us -> none  [the longest x4 36.7 us: tile_step(): new_sum = run_sum * rescale + jnp.sum(exp_scores, axis=-1)]
    convert_element_type x4 -> x1, other arithmetic: 10.7 us -> 0.01 us  [rope_tables(): angles = positions.astype(F32)[:, None] * inv_freq[None, :]]
    while x7 -> x0, local copies, waits for them, and re-layouts: 10 us -> none  [the longest x1 5.24 us: local_layer(): state = lax.fori_loop(1, cp_size, shift_step, ((keys, values), state))[1]]
    ppermute x6 -> x3, waiting for transfers between devices: 32.7 us -> 22.7 us  [the longest x1 22.7 us: local_layer(): kvb = lax.ppermute(kv, 'cp', [(0, 2), (1, 3)])]
    convert_element_type x1 -> x0, local copies, waits for them, and re-layouts: 6.22 us -> none  [apply_rope(): wide = heads.astype(jnp.float32)]
  transfers between devices with their start and end apart: 8 -> 3, of which waited for: 8 -> 1; matrix products, arithmetic and copies ran while one was open for 0% -> 1% of each run, Pallas kernels for 0% -> 5%
where the time goes in v2:
time: 272 us; the launch traced here: 271 us
  Pallas kernels  229 us (84%)
  waiting for transfers between devices  22.7 us (8%)
  local copies, waits for them, and re-layouts  10.7 us (4%)
  starting transfers between devices  6.18 us (2%)
    pallas_call x1, Pallas kernels, fused_layer(): pl.pallas_call(layer_kernel, in_specs=[vmem, vmem, vmem] + [ANY] * 8, out...  203 us
    ppermute x1, waiting for transfers between devices, local_layer(): kvb = lax.ppermute(kv, 'cp', [(0, 2), (1, 3)])  22.7 us
    pallas_call x1, Pallas kernels, q_proj(): pl.pallas_call(q_kernel, grid=(cols // bn,), in_specs=[whole(n), pl.Block...  14.3 us
    pallas_call x1, Pallas kernels, kv_proj(): pl.pallas_call(kv_kernel, grid=(cols // bn,), in_specs=[whole(x), whole(g...  11.8 us
    unnamed x7, local copies, waits for them, and re-layouts  5.67 us
  transfers between devices with their start and end apart: 3, of which 1 were waited for; matrix products, arithmetic and copies ran while one was open for 1% of the time, Pallas kernels for 5%

profile of v2, /device:TPU:3, one launch (start us, length us, event | category | flops | bytes accessed | tf_op | source)
XLA Modules:
  0.0 271.2 jit_solution(6412345882444365518)
XLA Ops:
  0.7 1.3 broadcast_in_dim.9.gain_ref
  2.0 1.0 fusion
  3.0 1.0 pad_maximum_fusion
  4.0 0.0 copy-start
  4.0 11.8 %kv_proj.1 = (bf16[512,4096]{1,0:T(8,128)(2,1)}, bf16[512,1024]{1,0:T(8,128)(2,1)}) custom-call(bf16[512,4096]{1,0:T(8,128)(2,1)} %x_ref.3, bf16[1,4096]{1,0:T(2,128)(2,1)} %broadcast_in_dim.9.gain_ref, bf16[4096,512]{1,0:T(8,128)(2,1)} %wk_ref.1, bf16[4096,512]{1,0:T(8,128)(2,1)} %wv_ref.1, f32[512,128]{1,0:T(8,128)} %get-tuple-element.12.cos_ref, ...), custom_call_target="tpu_custom_call" | custom-call | flops 4294967296 | bytes 16777216 | tf_op jit(solution)/shard_map/kv_proj/pallas_call | solution.py:71
  15.7 1.3 collective-permute-start.1
  17.0 1.3 collective-permute-start
  18.3 0.0 copy-done
  18.3 0.6 broadcast_in_dim.8.gain_ref
  18.9 22.7 %collective-permute-done.1.kvb = bf16[512,1024]{1,0:T(8,128)(2,1)S(1)} collective-permute-done((bf16[512,1024]{1,0:T(8,128)(2,1)}, bf16[512,1024]{1,0:T(8,128)(2,1)S(1)}, u32[]{:S(2)}, u32[]{:S(2)}) %collective-permute-start.1) | collective-permute-done | bytes 1048608 | tf_op jit(solution)/shard_map/ppermute | solution.py:351
  41.7 0.0 copy-start.1
  41.7 3.6 %collective-permute-start.2 = (bf16[512,1024]{1,0:T(8,128)(2,1)S(1)}, bf16[512,1024]{1,0:T(8,128)(2,1)}, u32[]{:S(2)}, u32[]{:S(2)}) collective-permute-start(bf16[512,1024]{1,0:T(8,128)(2,1)S(1)} %collective-permute-done.1.kvb), channel_id=1, source_target_pairs={{2,3},{3,2},{6,7},{7,6}} | collective-permute-start | bytes 3145736 | tf_op jit(solution)/shard_map/ppermute | solution.py:354
  45.3 1.3 fusion.1
  46.6 0.9 reshape.24
  47.5 0.9 reshape.25
  48.4 14.3 %q_proj.1.q_ref = bf16[512,2048]{1,0:T(8,128)(2,1)} custom-call(bf16[512,4096]{1,0:T(8,128)(2,1)} %get-tuple-element.5.n_ref, bf16[4096,2048]{1,0:T(8,128)(2,1)} %w_ref.1, f32[512,128]{1,0:T(8,128)} %get-tuple-element.12.cos_ref, f32[512,128]{1,0:T(8,128)} %get-tuple-element.13.sin_ref), custom_call_target="tpu_custom_call" | custom-call | flops 8589934592 | bytes 20971520 | tf_op jit(solution)/shard_map/q_proj/pallas_call | solution.py:91
  62.7 0.0 copy-done.1
  62.7 0.0 collective-permute-done.kva
  62.7 0.0 copy-start.2
  62.7 1.0 copy-done.2
  63.7 0.0 collective-permute-done.2.kvc
  63.7 202.8 %fused_layer.1 = bf16[512,4096]{1,0:T(8,128)(2,1)} custom-call(bf16[1,4096]{1,0:T(2,128)(2,1)} %broadcast_in_dim.8.gain_ref, bf16[512,2048]{1,0:T(8,128)(2,1)} %q_proj.1.q_ref, bf16[512,1024]{1,0:T(8,128)(2,1)} %get-tuple-element.6.kv_ref, bf16[512,4096]{1,0:T(8,128)(2,1)} %x_ref.3, bf16[512,1024]{1,0:T(8,128)(2,1)} %copy-done.2, ...), custom_call_target="tpu_custom_call" | custom-call | flops 85899345920 | bytes 318767104 | tf_op jit(solution)/shard_map/fused_layer/pallas_call | solution.py:316
  266.5 4.7 %copy.14 = bf16[512,4096]{1,0:T(8,128)(2,1)} copy(bf16[512,4096]{1,0:T(8,128)(2,1)} %fused_layer.1) | data formatting | bytes 8388608
  (2 shorter events, 0.0 us)
Async XLA Ops:
  4.0 14.3 %copy-start = (bf16[4096]{0:T(1024)(128)(2,1)S(1)}, bf16[4096]{0:T(1024)(128)(2,1)}, u32[]{:S(2)}) copy-start(bf16[4096]{0:T(1024)(128)(2,1)} %param.16) | copy-start | bytes 24580
  15.7 25.9 %collective-permute-start.1 = (bf16[512,1024]{1,0:T(8,128)(2,1)}, bf16[512,1024]{1,0:T(8,128)(2,1)S(1)}, u32[]{:S(2)}, u32[]{:S(2)}) collective-permute-start(bf16[512,1024]{1,0:T(8,128)(2,1)} %get-tuple-element.6.kv_ref), channel_id=1, source_target_pairs={{0,2},{1,3},{4,6},{5,7}} | collective-permute-start | bytes 3145736 | tf_op jit(solution)/shard_map/ppermute | solution.py:351
  17.0 45.7 %collective-permute-start = (bf16[512,1024]{1,0:T(8,128)(2,1)}, bf16[512,1024]{1,0:T(8,128)(2,1)S(1)}, u32[]{:S(2)}, u32[]{:S(2)}) collective-permute-start(bf16[512,1024]{1,0:T(8,128)(2,1)} %get-tuple-element.6.kv_ref), channel_id=1, source_target_pairs={{0,1},{2,3},{4,5},{6,7}} | collective-permute-start | bytes 3145736 | tf_op jit(solution)/shard_map/ppermute | solution.py:352
  41.7 21.0 %copy-start.1 = (bf16[512,1024]{1,0:T(8,128)(2,1)}, bf16[512,1024]{1,0:T(8,128)(2,1)S(1)}, u32[]{:S(2)}) copy-start(bf16[512,1024]{1,0:T(8,128)(2,1)S(1)} %collective-permute-done.1.kvb) | copy-start | bytes 3145732
  41.7 22.0 %collective-permute-start.2 = (bf16[512,1024]{1,0:T(8,128)(2,1)S(1)}, bf16[512,1024]{1,0:T(8,128)(2,1)}, u32[]{:S(2)}, u32[]{:S(2)}) collective-permute-start(bf16[512,1024]{1,0:T(8,128)(2,1)S(1)} %collective-permute-done.1.kvb), channel_id=1, source_target_pairs={{2,3},{3,2},{6,7},{7,6}} | collective-permute-start | bytes 3145736 | tf_op jit(solution)/shard_map/ppermute | solution.py:354
  62.7 1.0 copy-start.2

commit v3 on v0

v3 whole, which is shorter than its diff:
```python
import jax
import jax.numpy as jnp
from jax import lax
from jax.experimental import pallas as pl
from jax.experimental.pallas import tpu as pltpu
from jax.sharding import PartitionSpec as P

HEAD_DIM = 128
ROPE_THETA = 1000000.0
NORM_EPS = 1e-5
MASK_VALUE = -1e30
EXP2_SCALE = HEAD_DIM ** -0.5 * 1.4426950408889634
BF = jnp.bfloat16
F32 = jnp.float32
ANY = pl.BlockSpec(memory_space=pl.ANY)
VMEM = pl.BlockSpec(memory_space=pltpu.VMEM)
MESH = pl.DeviceIdType.MESH
LANES = 128
CHUNK = 128
HALF = 256
BLK = 512
SLOT = 2048
N_SLOT = 12


def at(i, size):
    return pl.ds(pl.multiple_of(i * size, size), size)


def loop(n, body):
    def step(i, c):
        body(i)
        return c
    lax.fori_loop(0, n, step, 0)


def rope_tables(positions):
    inv_freq = jnp.asarray(ROPE_THETA, F32) ** (-jnp.arange(0, HEAD_DIM, 2, dtype=F32) / HEAD_DIM)
    angles = positions.astype(F32)[:, None] * inv_freq[None, :]
    return jnp.cos(angles), jnp.sin(angles)


def layer_kernel(cos_ref, sin_ref, again_ref, mgain_ref, x_ref, wq_ref, wk_ref, wv_ref, wo_ref, wg_ref, wu_ref, wd_ref,
                 out_ref, kv_out_ref,
                 ring, send_buf, recv_buf, h_buf, n_buf, act_buf, kv_buf, q_buf, o_buf, m_sc, l_sc, acc_sc,
                 x_sem, wkv_sem, w_sem, kvs_sem, kvr_sem, kvo_sem, ps_sem, pr_sem, ds_sem, dr_sem, out_sem, free_sem):
    cp = lax.axis_index('cp')
    peer = {'tp': 1 - lax.axis_index('tp')}
    pair = {'cp': cp + 1 - 2 * lax.rem(cp, 2)}
    across = {'cp': lax.rem(cp + 2, 4)}
    tok, width = n_buf.shape
    n_blk = width // BLK
    n_gu = wg_ref.shape[1] // BLK
    n_q = wq_ref.shape[1] // BLK
    n_kv = wk_ref.shape[1] // HEAD_DIM
    groups = wq_ref.shape[1] // wk_ref.shape[1]
    n_chunk = tok // CHUNK
    stacked = groups * CHUNK
    gu_slots, d_slots = width // SLOT, wd_ref.shape[0] // SLOT
    gu_deep, d_deep = N_SLOT // (2 * gu_slots), N_SLOT // d_slots
    kv_slots = n_kv // 2 * gu_slots

    def ring_rows(slot, n):
        return pl.ds(pl.multiple_of(slot * SLOT, SLOT), n * SLOT)

    def load(src, slot, n):
        return pltpu.make_async_copy(src, ring.at[ring_rows(slot, n), :], w_sem.at[slot])

    def load_q(u):
        return load(wq_ref.at[:, at(u, BLK)], kv_slots + gu_slots * u, gu_slots)

    def load_wo(t):
        return load(wo_ref.at[:, at(lax.rem(t, n_blk), BLK)], lax.rem(t, N_SLOT), 1)

    def gate_slot(j):
        return lax.rem(j, gu_deep) * 2 * gu_slots

    def load_gate(j):
        return load(wg_ref.at[:, at(j, BLK)], gate_slot(j), gu_slots)

    def load_up(j):
        return load(wu_ref.at[:, at(j, BLK)], gate_slot(j) + gu_slots, gu_slots)

    def load_down(j):
        return load(wd_ref.at[:, at(j, BLK)], lax.rem(j, d_deep) * d_slots, d_slots)

    def load_kv(g, which):
        src = (wk_ref, wv_ref)[which]
        rows = pl.ds(g // 2 * gu_slots * SLOT, width)
        cols = pl.ds((g % 2) * 2 * HEAD_DIM + which * HEAD_DIM, HEAD_DIM)
        return pltpu.make_async_copy(src.at[:, pl.ds(g * HEAD_DIM, HEAD_DIM)], ring.at[rows, cols], wkv_sem.at[g, which])

    def load_x(j):
        return pltpu.make_async_copy(x_ref.at[:, at(j, BLK)], h_buf.at[j], x_sem.at[j])

    def kv_copy(kind, g):
        src_block = 2 if kind == 2 else 0
        return pltpu.make_async_remote_copy(kv_buf.at[src_block, g], kv_buf.at[kind + 1, g], kvs_sem.at[kind, g], kvr_sem.at[kind, g],
                                            device_id=across if kind == 1 else pair, device_id_type=MESH)

    def kv_out(g):
        return pltpu.make_async_copy(kv_buf.at[0, g], kv_out_ref.at[g], kvo_sem.at[g])

    def part_copy(i, j):
        piece = (j, at(i, CHUNK), slice(None))
        return pltpu.make_async_remote_copy(send_buf.at[piece], recv_buf.at[piece], ps_sem.at[i, j], pr_sem.at[i, j],
                                            device_id=peer, device_id_type=MESH)

    def down_copy(s, j):
        piece = (j, at(s, HALF), slice(None))
        return pltpu.make_async_remote_copy(send_buf.at[piece], recv_buf.at[piece], ds_sem.at[s, j], dr_sem.at[s, j],
                                            device_id=peer, device_id_type=MESH)

    def out_copy(s, j):
        return pltpu.make_async_copy(h_buf.at[j, at(s, HALF), :], out_ref.at[at(s, HALF), at(j, BLK)], out_sem.at[s, j])

    def scale_rows(src_rows, dst_rows, total, gain_ref):
        inv = lax.rsqrt(jnp.sum(total, axis=-1, keepdims=True) / width + NORM_EPS)
        for r in range(width // LANES):
            j, c = r * LANES // BLK, r * LANES % BLK
            wide = h_buf[j, src_rows, c:c + LANES].astype(F32)
            n_buf[dst_rows, r * LANES:(r + 1) * LANES] = (wide * inv * gain_ref[r:r + 1, :].astype(F32)).astype(BF)

    def rope(prod):
        cos_full = jnp.concatenate([cos_ref[...], cos_ref[...]], axis=1)
        sin_full = jnp.concatenate([-sin_ref[...], sin_ref[...]], axis=1)
        u = prod.astype(BF).astype(F32)
        return (u * cos_full + pltpu.roll(u, HEAD_DIM // 2, 1) * sin_full).astype(BF)

    loop(n_blk, lambda j: load_x(j).start())
    for g in range(n_kv):
        for which in range(2):
            load_kv(g, which).start()
    for u in range(n_q):
        load_q(u).start()
    barrier = pltpu.get_barrier_semaphore()
    for other in (peer, pair, across):
        pl.semaphore_signal(barrier, inc=1, device_id=other, device_id_type=MESH)
    loop(n_blk, lambda j: load_x(j).wait())

    def norm_step(r):
        rows = at(r, 32)
        total = jnp.zeros((32, BLK), F32)
        for j in range(n_blk):
            wide = h_buf[j, rows, :].astype(F32)
            total += wide * wide
        scale_rows(rows, rows, total, again_ref)
    loop(tok // 32, norm_step)

    for g in range(n_kv):
        for which in range(2):
            load_kv(g, which).wait()
        w = ring[g // 2 * gu_slots * SLOT:g // 2 * gu_slots * SLOT + width, (g % 2) * 2 * HEAD_DIM:(g % 2 + 1) * 2 * HEAD_DIM]
        prod = jnp.dot(n_buf[...], w, preferred_element_type=F32)
        kv_buf[0, g, :, :HEAD_DIM] = rope(prod[:, :HEAD_DIM])
        kv_buf[0, g, :, HEAD_DIM:] = prod[:, HEAD_DIM:].astype(BF)
        if g == 0:
            pl.semaphore_wait(barrier, 3)

        @pl.when(cp < 2)
        def _():
            kv_copy(1, g).start()

        @pl.when(lax.rem(cp, 2) == 0)
        def _():
            kv_copy(0, g).start()
        kv_out(g).start()
    for t in range(kv_slots):
        load_wo(t).start()

    def q_step(u):
        load_q(u).wait()
        w = ring[ring_rows(kv_slots + gu_slots * u, gu_slots), :]
        prod = jnp.dot(n_buf[...], w, preferred_element_type=F32)
        for j in range(BLK // HEAD_DIM):
            q_buf[:, pl.ds(pl.multiple_of(u * BLK + j * HEAD_DIM, HEAD_DIM), HEAD_DIM)] = rope(prod[:, j * HEAD_DIM:(j + 1) * HEAD_DIM])
        for t in range(gu_slots):
            load_wo(kv_slots + gu_slots * u + t).start()
    loop(n_q, q_step)

    lo = jnp.where(cp == 2, 2, 1)
    hi = jnp.where(cp == 0, 1, jnp.where(cp == 1, 2, 4))
    for i in range(n_chunk):
        row0 = i * CHUNK
        n_keys = row0 + CHUNK

        def head_step(g):
            q = jnp.concatenate([q_buf[row0:row0 + CHUNK, at(g * groups + j, HEAD_DIM)] for j in range(groups)], axis=0)
            s = lax.dot_general(q, kv_buf[0, g, :n_keys, :HEAD_DIM], (((1,), (1,)), ((), ())), preferred_element_type=F32)
            qpos = row0 + lax.rem(lax.broadcasted_iota(jnp.int32, (stacked, n_keys), 0), CHUNK)
            kpos = lax.broadcasted_iota(jnp.int32, (stacked, n_keys), 1)
            s = jnp.where(kpos <= qpos, s, MASK_VALUE)
            m0 = jnp.max(s, axis=-1, keepdims=True)
            p = jnp.exp2(s * EXP2_SCALE - m0 * EXP2_SCALE)
            m_sc[...] = jnp.broadcast_to(m0, m_sc.shape)
            l_sc[...] = jnp.broadcast_to(jnp.sum(p, axis=-1, keepdims=True), l_sc.shape)
            acc_sc[...] = jnp.dot(p.astype(BF), kv_buf[0, g, :n_keys, HEAD_DIM:], preferred_element_type=F32)

            def block_step(b, c):
                if i == 0:
                    @pl.when(b == 1)
                    def _():
                        kv_copy(0, g).wait_recv()

                    @pl.when(b == 2)
                    def _():
                        kv_copy(1, g).wait_recv()
                        kv_copy(2, g).start()

                    @pl.when(b == 3)
                    def _():
                        kv_copy(2, g).wait_recv()
                s = lax.dot_general(q, kv_buf[b, g, :, :HEAD_DIM], (((1,), (1,)), ((), ())), preferred_element_type=F32)
                m_old = m_sc[...]
                m_new = jnp.maximum(m_old, jnp.max(s, axis=-1, keepdims=True))
                alpha = jnp.exp2((m_old - m_new) * EXP2_SCALE)
                p = jnp.exp2(s * EXP2_SCALE - m_new[:, :1] * EXP2_SCALE)
                l_sc[...] = l_sc[...] * alpha + jnp.sum(p, axis=-1, keepdims=True)
                acc_sc[...] = acc_sc[...] * alpha + jnp.dot(p.astype(BF), kv_buf[b, g, :, HEAD_DIM:], preferred_element_type=F32)
                m_sc[...] = m_new
                return c
            lax.fori_loop(lo, hi, block_step, 0)
            out = (acc_sc[...] / l_sc[...]).astype(BF)
            for j in range(groups):
                o_buf[:, at(g * groups + j, HEAD_DIM)] = out[j * CHUNK:(j + 1) * CHUNK]
        loop(n_kv, head_step)

        def wo_step(j):
            t = i * n_blk + j
            load_wo(t).wait()
            w = ring[ring_rows(lax.rem(t, N_SLOT), 1), :]
            send_buf[j, row0:row0 + CHUNK, :] = jnp.dot(o_buf[...], w, preferred_element_type=F32).astype(BF)
            part_copy(i, j).start()
            if (i + 1) * n_blk - 1 + N_SLOT < n_chunk * n_blk:
                load_wo(t + N_SLOT).start()
            else:
                @pl.when(t + N_SLOT < n_chunk * n_blk)
                def _():
                    load_wo(t + N_SLOT).start()

                first = n_chunk * n_blk - N_SLOT
                for b in range(gu_deep):
                    end = 2 * gu_slots * b
                    for which in range(2):
                        last_slot = end + which * gu_slots + gu_slots - 1
                        when = first + (last_slot - first) % N_SLOT

                        @pl.when(t == when)
                        def _():
                            (load_gate, load_up)[which](b).start()
        loop(n_blk, wo_step)

    def half_step(s):
        def wait_part(r):
            c = part_copy(s * (HALF // CHUNK) + r // n_blk, lax.rem(r, n_blk))
            c.wait_recv()
            c.wait_send()
        loop(HALF // CHUNK * n_blk, wait_part)

        def h_step(r):
            rows = at(s * (HALF // 32) + r, 32)
            total = jnp.zeros((32, BLK), F32)
            for j in range(n_blk):
                add = send_buf[j, rows, :].astype(F32) + recv_buf[j, rows, :].astype(F32)
                h = (h_buf[j, rows, :].astype(F32) + add).astype(BF)
                h_buf[j, rows, :] = h
                wide = h.astype(F32)
                total += wide * wide
            scale_rows(rows, at(r, 32), total, mgain_ref)
        loop(HALF // 32, h_step)
        pl.semaphore_signal(free_sem.at[s], inc=1, device_id=peer, device_id_type=MESH)

        def gu_step(j):
            slot = gate_slot(j)
            load_gate(j).wait()
            gate = jnp.dot(n_buf[:HALF, :], ring[ring_rows(slot, gu_slots), :], preferred_element_type=F32)
            load_up(j).wait()
            up = jnp.dot(n_buf[:HALF, :], ring[ring_rows(slot + gu_slots, gu_slots), :], preferred_element_type=F32)
            act_buf[:, at(j, BLK)] = (gate / (1.0 + jnp.exp(-gate)) * up).astype(BF)

            @pl.when(j + gu_deep < n_gu)
            def _():
                load_gate(j + gu_deep).start()
                load_up(j + gu_deep).start()
            freed = 0
            for back in range(gu_deep, 0, -1):
                now = (2 * gu_slots * (gu_deep - back + 1)) // d_slots

                @pl.when(j == n_gu - back)
                def _():
                    for d in range(freed, now):
                        load_down(d).start()
                freed = now
        loop(n_gu, gu_step)
        pl.semaphore_wait(free_sem.at[s], 1)

        def down_step(j):
            load_down(j).wait()
            w = ring[ring_rows(lax.rem(j, d_deep) * d_slots, d_slots), :]
            send_buf[j, at(s, HALF), :] = jnp.dot(act_buf[...], w, preferred_element_type=F32).astype(BF)
            down_copy(s, j).start()

            @pl.when(j + d_deep < n_blk)
            def _():
                load_down(j + d_deep).start()
            freed = 0
            for back in range(d_deep, 0, -1):
                now = d_slots * (d_deep - back + 1) // gu_slots

                @pl.when((j == n_blk - back) & (s == 0))
                def _():
                    for d in range(freed, now):
                        (load_gate, load_up)[d % 2](d // 2).start()
                freed = now
        loop(n_blk, down_step)
    loop(tok // HALF, half_step)

    def final_step(t):
        s, j = t // n_blk, lax.rem(t, n_blk)
        down_copy(s, j).wait_recv()
        rows = at(s, HALF)
        add = send_buf[j, rows, :].astype(F32) + recv_buf[j, rows, :].astype(F32)
        h_buf[j, rows, :] = (h_buf[j, rows, :].astype(F32) + add).astype(BF)
        out_copy(s, j).start()
    loop(tok // HALF * n_blk, final_step)

    def drain(t):
        s, j = t // n_blk, lax.rem(t, n_blk)
        down_copy(s, j).wait_send()
        out_copy(s, j).wait()
    loop(tok // HALF * n_blk, drain)
    for g in range(n_kv):
        kv_out(g).wait()

        @pl.when(cp < 2)
        def _():
            kv_copy(1, g).wait_send()

        @pl.when(lax.rem(cp, 2) == 0)
        def _():
            kv_copy(0, g).wait_send()

        @pl.when(cp >= 2)
        def _():
            kv_copy(2, g).wait_send()


def fused_layer(cos_tab, sin_tab, attn_gain, mlp_gain, x, w_q, w_k, w_v, w_o, w_gate, w_up, w_down):
    tok, width = x.shape
    qcols, kcols, ff = w_q.shape[1], w_k.shape[1], w_gate.shape[1]
    n_blk, n_chunk, n_kv, halves = width // BLK, tok // CHUNK, kcols // HEAD_DIM, tok // HALF
    stacked = CHUNK * (qcols // kcols)
    dma = pltpu.SemaphoreType.DMA
    return pl.pallas_call(
        layer_kernel,
        in_specs=[VMEM] * 4 + [ANY] * 8,
        out_specs=[ANY, ANY],
        out_shape=[jax.ShapeDtypeStruct((tok, width), BF), jax.ShapeDtypeStruct((n_kv, tok, 2 * HEAD_DIM), BF)],
        scratch_shapes=[
            pltpu.VMEM((N_SLOT * SLOT, BLK), BF),
            pltpu.VMEM((n_blk, tok, BLK), BF), pltpu.VMEM((n_blk, tok, BLK), BF), pltpu.VMEM((n_blk, tok, BLK), BF),
            pltpu.VMEM((tok, width), BF), pltpu.VMEM((HALF, ff), BF),
            pltpu.VMEM((4, n_kv, tok, 2 * HEAD_DIM), BF), pltpu.VMEM((tok, qcols), BF), pltpu.VMEM((CHUNK, qcols), BF),
            pltpu.VMEM((stacked, HEAD_DIM), F32), pltpu.VMEM((stacked, HEAD_DIM), F32), pltpu.VMEM((stacked, HEAD_DIM), F32),
            dma((n_blk,)), dma((n_kv, 2)), dma((N_SLOT,)), dma((3, n_kv)), dma((3, n_kv)), dma((n_kv,)),
            dma((n_chunk, n_blk)), dma((n_chunk, n_blk)), dma((halves, n_blk)), dma((halves, n_blk)), dma((halves, n_blk)),
            pltpu.SemaphoreType.REGULAR((halves,))],
        compiler_params=pltpu.CompilerParams(vmem_limit_bytes=67043328, collective_id=0, has_side_effects=True),
        name='fused_layer',
        cost_estimate=pl.CostEstimate(flops=2 * tok * width * (2 * qcols + 2 * kcols + 3 * ff), transcendentals=0,
                                      bytes_accessed=2 * width * (2 * qcols + 2 * kcols + 6 * ff)),
    )(cos_tab, sin_tab, attn_gain, mlp_gain, x, w_q, w_k, w_v, w_o, w_gate, w_up, w_down)


def emit_kernel(y_ref, kv_ref, x_out_ref, k_ref, v_ref):
    x_out_ref[...] = y_ref[...]
    for g in range(kv_ref.shape[0]):
        k_ref[:, g, :] = kv_ref[g, :, :HEAD_DIM]
        v_ref[:, g, :] = kv_ref[g, :, HEAD_DIM:]


def emit(y, kv):
    tok, width = y.shape
    n_kv = kv.shape[0]
    rows = 128
    cache = pl.BlockSpec((rows, n_kv, HEAD_DIM), lambda i: (i, 0, 0))
    return pl.pallas_call(
        emit_kernel, grid=(tok // rows,),
        in_specs=[pl.BlockSpec((rows, width), lambda i: (i, 0)), pl.BlockSpec((n_kv, rows, 2 * HEAD_DIM), lambda i: (0, i, 0))],
        out_specs=[pl.BlockSpec((rows, width), lambda i: (i, 0)), cache, cache],
        out_shape=[jax.ShapeDtypeStruct((tok, width), BF)] + [jax.ShapeDtypeStruct((tok, n_kv, HEAD_DIM), BF)] * 2,
        name='emit',
    )(y, kv)


def solution(mesh):
    row_spec = P(('dp', 'cp'), None)
    cache_spec = P(('dp', 'cp'), 'tp', None)
    col_spec = P(None, 'tp')
    split_rows = P('tp', None)
    vec_spec = P(None)

    def local_layer(x, attn_gain, w_q, w_k, w_v, w_o, mlp_gain, w_gate, w_up, w_down):
        tok, width = x.shape
        cos_tab, sin_tab = rope_tables(lax.axis_index('cp') * tok + jnp.arange(tok))
        gains = [g.reshape(width // LANES, LANES) for g in (attn_gain, mlp_gain)]
        y, kv = fused_layer(cos_tab, sin_tab, *gains, x, w_q, w_k, w_v, w_o, w_gate, w_up, w_down)
        return tuple(emit(y, kv))

    return jax.shard_map(local_layer, mesh=mesh,
                         in_specs=(row_spec, vec_spec, col_spec, col_spec, col_spec, split_rows, vec_spec, col_spec, col_spec, split_rows),
                         out_specs=(row_spec, cache_spec, cache_spec), check_vma=False)
```

time: 570 us -> 232 us (0.41); the launches traced: 561 us -> 232 us
  waiting for transfers between devices: 236 us -> 0 us
  Pallas kernels: 0 us -> 229 us
  matrix products: 218 us -> 0 us
  other arithmetic: 62.4 us -> 1.84 us
  local copies, waits for them, and re-layouts: 27.5 us -> 0 us
  between operations: 14.8 us -> 0.65 us
    pallas_call x0 -> x2, Pallas kernels: none -> 229 us  [the longest x1 223 us: fused_layer(): pl.pallas_call(layer_kernel, in_specs=[VMEM] * 4 + [ANY] * 8, out_specs=[...]
    dot_general x15 -> x0, matrix products: 218 us -> none  [the longest x4 42.8 us: tile_step(): jnp.einsum('kgqs,skd->kgqd', exp_scores.astype(jnp.bfloat16), v_tile, pre...]
    psum x2 -> x0, waiting for transfers between devices: 203 us -> none  [the longest x1 103 us: local_layer(): attn_total = lax.psum(attn_part, 'tp')]
    reduce_sum x6 -> x0, other arithmetic: 45.2 us -> none  [the longest x4 36.7 us: tile_step(): new_sum = run_sum * rescale + jnp.sum(exp_scores, axis=-1)]
    ppermute x6 -> x0, waiting for transfers between devices: 32.7 us -> none  [shift_step(): held = lax.ppermute(held, 'cp', shift_pairs)]
    convert_element_type x4 -> x1, other arithmetic: 10.7 us -> 0.01 us  [rope_tables(): angles = positions.astype(F32)[:, None] * inv_freq[None, :]]
    while x7 -> x0, local copies, waits for them, and re-layouts: 10 us -> none  [the longest x1 5.24 us: local_layer(): state = lax.fori_loop(1, cp_size, shift_step, ((keys, values), state))[1]]
    slice x2 -> x0, local copies, waits for them, and re-layouts: 6.44 us -> none  [the longest x1 6.32 us: apply_rope(): first = wide[..., :half]]
  transfers between devices with their start and end apart: 8 -> 0, of which waited for: 8 -> 0; matrix products, arithmetic and copies ran while one was open for 0% -> 0% of each run, Pallas kernels for 0% -> 0%
where the time goes in v3:
time: 232 us
  Pallas kernels  229 us (99%)
    pallas_call x1, Pallas kernels, fused_layer(): pl.pallas_call(layer_kernel, in_specs=[VMEM] * 4 + [ANY] * 8, out_specs=[...  223 us
    pallas_call x1, Pallas kernels, emit(): pl.pallas_call(emit_kernel, grid=(tok // rows,), in_specs=[pl.BlockSpec((...  6.58 us

profile of v3, /device:TPU:3, one launch (start us, length us, event | category | flops | bytes accessed | tf_op | source)
XLA Modules:
  0.0 231.6 jit_solution(8032149397694291706)
XLA Ops:
  0.7 1.8 multiply_sine_fusion
  2.5 222.5 %fused_layer.1 = (bf16[512,4096]{1,0:T(8,128)(2,1)}, bf16[4,512,256]{2,1,0:T(8,128)(2,1)}) custom-call(f32[512,64]{1,0:T(8,128)} %get-tuple-element.8.cos_ref, f32[512,64]{1,0:T(8,128)} %get-tuple-element.7.sin_ref, bf16[32,128]{1,0:T(8,128)(2,1)} %bitcast.2, bf16[32,128]{1,0:T(8,128)(2,1)} %bitcast.3, bf16[512,4096]{1,0:T(8,128)(2,1)} %x_ref.1, ...), custom_call_target="tpu_custom_call" | custom-call | flops 98784247808 | bytes 343932928 | tf_op jit(solution)/shard_map/fused_layer/pallas_call | solution.py:354
  225.0 6.6 %emit.1 = (bf16[512,4096]{1,0:T(8,128)(2,1)}, bf16[512,4,128]{2,1,0:T(4,128)(2,1)}, bf16[512,4,128]{2,1,0:T(4,128)(2,1)}) custom-call(bf16[512,4096]{1,0:T(8,128)(2,1)} %get-tuple-element.5.y_ref, bf16[4,512,256]{2,1,0:T(8,128)(2,1)} %get-tuple-element.6.kv_ref), custom_call_target="tpu_custom_call" | custom-call | tf_op jit(solution)/shard_map/emit/pallas_call | solution.py:387
  (2 shorter events, 0.0 us)

commit v4 on v3

v4 whole, which is shorter than its diff:
```python
import jax
import jax.numpy as jnp
import numpy as np
from jax import lax
from jax.experimental import pallas as pl
from jax.experimental.pallas import tpu as pltpu
from jax.sharding import PartitionSpec as P

HEAD_DIM = 128
ROPE_THETA = 1000000.0
NORM_EPS = 1e-5
MASK_VALUE = -1e30
EXP2_SCALE = HEAD_DIM ** -0.5 * 1.4426950408889634
BF = jnp.bfloat16
F32 = jnp.float32
ANY = pl.BlockSpec(memory_space=pl.ANY)
VMEM = pl.BlockSpec(memory_space=pltpu.VMEM)
MESH = pl.DeviceIdType.MESH
LANES = 128
CHUNK = 128
HALF = 256
BLK = 512
SLOT = 2048
X_ROWS = 64
KV_ROWS = 128
N_SLOT = 12
VMEM_LIMIT = 60000000


def at(i, size):
    return pl.ds(pl.multiple_of(i * size, size), size)


def loop(n, body):
    def step(i, c):
        body(i)
        return c
    lax.fori_loop(0, n, step, 0)


def rope_table(n_pos):
    inv_freq = np.float32(ROPE_THETA) ** (-np.arange(0, HEAD_DIM, 2, dtype=np.float32) / np.float32(HEAD_DIM))
    angles = np.arange(n_pos, dtype=np.float32)[:, None] * inv_freq[None, :]
    return np.concatenate([np.cos(angles), np.sin(angles)], axis=1).astype(np.float32)


def layer_kernel(tab_ref, again_ref, mgain_ref, x_ref, wq_ref, wk_ref, wv_ref, wo_ref, wg_ref, wu_ref, wd_ref,
                 h_buf, k_out, v_out,
                 ring, send_buf, recv_buf, n_buf, act_buf, kv_buf, q_buf, o_buf, again_buf, mgain_buf, tab_buf, cos_buf, sin_buf, m_sc, l_sc, acc_sc,
                 tab_sem, x_sem, wkv_sem, w_sem, kvs_sem, kvr_sem, ps_sem, pr_sem, ds_sem, dr_sem, free_sem):
    cp = lax.axis_index('cp')
    peer = {'tp': 1 - lax.axis_index('tp')}
    pair = {'cp': cp + 1 - 2 * lax.rem(cp, 2)}
    across = {'cp': lax.rem(cp + 2, 4)}
    tok, width = n_buf.shape
    n_blk = width // BLK
    n_gu = wg_ref.shape[1] // BLK
    n_q = wq_ref.shape[1] // BLK
    n_kv = wk_ref.shape[1] // HEAD_DIM
    groups = wq_ref.shape[1] // wk_ref.shape[1]
    n_chunk = tok // CHUNK
    stacked = groups * CHUNK
    gu_slots, d_slots = width // SLOT, wd_ref.shape[0] // SLOT
    gu_deep, d_deep = N_SLOT // (2 * gu_slots), N_SLOT // d_slots
    kv_slots = n_kv // 2 * gu_slots

    def ring_rows(slot, n):
        return pl.ds(pl.multiple_of(slot * SLOT, SLOT), n * SLOT)

    def load(src, slot, n):
        return pltpu.make_async_copy(src, ring.at[ring_rows(slot, n), :], w_sem.at[slot])

    def load_q(u):
        return load(wq_ref.at[:, at(u, BLK)], kv_slots + gu_slots * u, gu_slots)

    def load_wo(t):
        return load(wo_ref.at[:, at(lax.rem(t, n_blk), BLK)], lax.rem(t, N_SLOT), 1)

    def gate_slot(j):
        return lax.rem(j, gu_deep) * 2 * gu_slots

    def load_gate(j):
        return load(wg_ref.at[:, at(j, BLK)], gate_slot(j), gu_slots)

    def load_up(j):
        return load(wu_ref.at[:, at(j, BLK)], gate_slot(j) + gu_slots, gu_slots)

    def load_down(j):
        return load(wd_ref.at[:, at(j, BLK)], lax.rem(j, d_deep) * d_slots, d_slots)

    def load_kv(g, which):
        src = (wk_ref, wv_ref)[which]
        cols = at(lax.rem(g, 2) * 2 + which, HEAD_DIM)
        return pltpu.make_async_copy(src.at[:, at(g, HEAD_DIM)], ring.at[ring_rows(g // 2 * gu_slots, gu_slots), cols], wkv_sem.at[g, which])

    def load_x(i):
        return pltpu.make_async_copy(x_ref.at[at(i, X_ROWS), :], h_buf.at[at(i, X_ROWS), :], x_sem.at[i])

    def kv_copy(kind, g, r=0, n_rows=None):
        n_rows = n_rows or tok
        src_block = 2 if kind == 2 else 0
        rows = at(r, n_rows) if n_rows < tok else slice(None)
        return pltpu.make_async_remote_copy(kv_buf.at[src_block, g, rows, :], kv_buf.at[kind + 1, g, rows, :],
                                            kvs_sem.at[kind], kvr_sem.at[kind, g],
                                            device_id=across if kind == 1 else pair, device_id_type=MESH)

    def part_copy(i, j):
        piece = (j, at(i, CHUNK), slice(None))
        return pltpu.make_async_remote_copy(send_buf.at[piece], recv_buf.at[piece], ps_sem.at[i * CHUNK // HALF], pr_sem.at[i * CHUNK // HALF],
                                            device_id=peer, device_id_type=MESH)

    def down_copy(s, j):
        piece = (j, at(s, HALF), slice(None))
        return pltpu.make_async_remote_copy(send_buf.at[piece], recv_buf.at[piece], ds_sem.at[s], dr_sem.at[s, j],
                                            device_id=peer, device_id_type=MESH)

    def half_copy(s, sent_sem, got_sem):
        piece = (slice(None), at(s, HALF), slice(None))
        return pltpu.make_async_remote_copy(send_buf.at[piece], recv_buf.at[piece], sent_sem.at[s], got_sem,
                                            device_id=peer, device_id_type=MESH)

    def scale_rows(src_rows, dst_rows, total, gain_ref):
        inv = lax.rsqrt(jnp.sum(total, axis=-1, keepdims=True) / width + NORM_EPS)
        for r in range(width // LANES):
            cols = slice(r * LANES, (r + 1) * LANES)
            wide = h_buf[src_rows, cols].astype(F32)
            n_buf[dst_rows, cols] = (wide * inv * gain_ref[r:r + 1, :].astype(F32)).astype(BF)

    def rope(prod, rows):
        u = prod.astype(BF).astype(F32)
        return (u * cos_buf[rows, :] + pltpu.roll(u, HEAD_DIM // 2, 1) * sin_buf[rows, :]).astype(BF)

    small = [pltpu.make_async_copy(again_ref, again_buf, tab_sem.at[0]), pltpu.make_async_copy(mgain_ref, mgain_buf, tab_sem.at[1]),
             pltpu.make_async_copy(tab_ref.at[at(cp, tok), :], tab_buf, tab_sem.at[2])]
    for c in small:
        c.start()
    first_rows = 2 * KV_ROWS // X_ROWS
    loop(first_rows, lambda i: load_x(i).start())
    for g in range(2):
        for which in range(2):
            load_kv(g, which).start()
    lax.fori_loop(first_rows, tok // X_ROWS, lambda i, c: (load_x(i).start(), c)[1], 0)
    barrier = pltpu.get_barrier_semaphore()
    for other in (peer, pair, across):
        pl.semaphore_signal(barrier, inc=1, device_id=other, device_id_type=MESH)
    for c in small:
        c.wait()
    cos, sin = tab_buf[:, :HEAD_DIM // 2], tab_buf[:, HEAD_DIM // 2:]
    cos_buf[...] = jnp.concatenate([cos, cos], axis=1)
    sin_buf[...] = jnp.concatenate([-sin, sin], axis=1)

    def norm_step(i):
        load_x(i).wait()
        for part in range(X_ROWS // 32):
            rows = at(i * (X_ROWS // 32) + part, 32)
            total = jnp.zeros((32, BLK), F32)
            for j in range(n_blk):
                wide = h_buf[rows, j * BLK:(j + 1) * BLK].astype(F32)
                total += wide * wide
            scale_rows(rows, rows, total, again_buf)

    n_quarter = tok // KV_ROWS

    def kv_step(t):
        pair_heads, r = t // n_quarter, lax.rem(t, n_quarter)
        rows = at(r, KV_ROWS)

        @pl.when(t < n_quarter)
        def _():
            lax.fori_loop(r * (KV_ROWS // X_ROWS), (r + 1) * (KV_ROWS // X_ROWS), lambda i, c: (norm_step(i), c)[1], 0)

        @pl.when(t == 0)
        def _():
            pl.semaphore_wait(barrier, 3)

        @pl.when(t == 1)
        def _():
            for g in range(2, n_kv):
                for which in range(2):
                    load_kv(g, which).start()
            for u in range(n_q):
                load_q(u).start()

        @pl.when(r == 0)
        def _():
            for e in range(2):
                for which in range(2):
                    load_kv(2 * pair_heads + e, which).wait()
        prod = jnp.dot(n_buf[rows, :], ring[ring_rows(pair_heads * gu_slots, gu_slots), :], preferred_element_type=F32)
        for e in range(2):
            g = 2 * pair_heads + e
            col = e * 2 * HEAD_DIM
            kv_buf[0, g, rows, :HEAD_DIM] = rope(prod[:, col:col + HEAD_DIM], rows)
            kv_buf[0, g, rows, HEAD_DIM:] = prod[:, col + HEAD_DIM:col + 2 * HEAD_DIM].astype(BF)


        def send_kv(*piece):
            @pl.when(cp < 2)
            def _():
                kv_copy(1, *piece).start()

            @pl.when(lax.rem(cp, 2) == 0)
            def _():
                kv_copy(0, *piece).start()
        send_kv(2 * pair_heads, r, KV_ROWS)

        @pl.when(r == n_quarter - 1)
        def _():
            send_kv(2 * pair_heads + 1)
    loop(n_kv // 2 * n_quarter, kv_step)
    for t in range(kv_slots):
        load_wo(t).start()

    def q_step(u):
        load_q(u).wait()
        w = ring[ring_rows(kv_slots + gu_slots * u, gu_slots), :]
        prod = jnp.dot(n_buf[...], w, preferred_element_type=F32)
        for j in range(BLK // HEAD_DIM):
            q_buf[:, pl.ds(pl.multiple_of(u * BLK + j * HEAD_DIM, HEAD_DIM), HEAD_DIM)] = rope(prod[:, j * HEAD_DIM:(j + 1) * HEAD_DIM], slice(None))
        for t in range(gu_slots):
            load_wo(kv_slots + gu_slots * u + t).start()
    loop(n_q, q_step)

    lo = jnp.where(cp == 2, 2, 1)
    hi = jnp.where(cp == 0, 1, jnp.where(cp == 1, 2, 4))
    for i in range(n_chunk):
        row0 = i * CHUNK
        n_keys = row0 + CHUNK

        n_heads = 2

        def scores(g, b, n):
            q = jnp.concatenate([q_buf[row0:row0 + CHUNK, at(g * groups + j, HEAD_DIM)] for j in range(groups)], axis=0)
            return lax.dot_general(kv_buf[b, g, :n, :HEAD_DIM], q, (((1,), (1,)), ((), ())), preferred_element_type=F32)

        def weigh(g, b, n, p):
            return lax.dot_general(kv_buf[b, g, :n, HEAD_DIM:], p.astype(BF), (((0,), (0,)), ((), ())), preferred_element_type=F32)

        def pass_on(g):
            kv_copy(1, g).wait_recv()
            kv_copy(2, g).start()

        def head_step(step):
            heads = [step * n_heads + e for e in range(n_heads)]
            kpos = lax.broadcasted_iota(jnp.int32, (n_keys, stacked), 0)
            qpos = row0 + lax.rem(lax.broadcasted_iota(jnp.int32, (n_keys, stacked), 1), CHUNK)
            if i == 0:
                @pl.when(cp >= 2)
                def _():
                    pass_on(heads[0])
            all_s = [scores(g, 0, n_keys) for g in heads]
            for e, g in enumerate(heads):
                s = jnp.where(kpos <= qpos, all_s[e], MASK_VALUE)
                m0 = jnp.max(s, axis=0, keepdims=True)
                p = jnp.exp2(s * EXP2_SCALE - m0 * EXP2_SCALE)
                m_sc[e] = m0
                l_sc[e] = jnp.sum(p, axis=0, keepdims=True)
                acc_sc[e] = weigh(g, 0, n_keys, p)

            def block_step(b, c):
                if i == 0:
                    @pl.when(b == 1)
                    def _():
                        for g in heads:
                            kv_copy(0, g).wait_recv()

                    @pl.when(b == 2)
                    def _():
                        pass_on(heads[1])

                    @pl.when(b == 3)
                    def _():
                        for g in heads:
                            kv_copy(2, g).wait_recv()
                all_s = [scores(g, b, tok) for g in heads]
                for e, g in enumerate(heads):
                    s = all_s[e]
                    m_old = m_sc[e]
                    m_new = jnp.maximum(m_old, jnp.max(s, axis=0, keepdims=True))
                    alpha = jnp.exp2((m_old - m_new) * EXP2_SCALE)
                    p = jnp.exp2(s * EXP2_SCALE - m_new * EXP2_SCALE)
                    l_sc[e] = l_sc[e] * alpha + jnp.sum(p, axis=0, keepdims=True)
                    acc_sc[e] = acc_sc[e] * alpha + weigh(g, b, tok, p)
                    m_sc[e] = m_new
                return c
            lax.fori_loop(lo, hi, block_step, 0)
            for e, g in enumerate(heads):
                out = acc_sc[e] / l_sc[e]
                for j in range(groups):
                    o_buf[:, at(g * groups + j, HEAD_DIM)] = out[:, j * CHUNK:(j + 1) * CHUNK].T.astype(BF)
        loop(n_kv // n_heads, head_step)

        def wo_step(j):
            t = i * n_blk + j
            load_wo(t).wait()
            w = ring[ring_rows(lax.rem(t, N_SLOT), 1), :]
            send_buf[j, row0:row0 + CHUNK, :] = jnp.dot(o_buf[...], w, preferred_element_type=F32).astype(BF)
            part_copy(i, j).start()
            if (i + 1) * n_blk - 1 + N_SLOT < n_chunk * n_blk:
                load_wo(t + N_SLOT).start()
            else:
                @pl.when(t + N_SLOT < n_chunk * n_blk)
                def _():
                    load_wo(t + N_SLOT).start()

                first = n_chunk * n_blk - N_SLOT
                for b in range(gu_deep):
                    end = 2 * gu_slots * b
                    for which in range(2):
                        last_slot = end + which * gu_slots + gu_slots - 1
                        when = first + (last_slot - first) % N_SLOT

                        @pl.when(t == when)
                        def _():
                            (load_gate, load_up)[which](b).start()
        loop(n_blk, wo_step)

    def half_step(s):
        parts = half_copy(s, ps_sem, pr_sem.at[s])
        parts.wait_recv()
        parts.wait_send()

        def h_step(r):
            rows = at(s * (HALF // 32) + r, 32)
            total = jnp.zeros((32, BLK), F32)
            for j in range(n_blk):
                cols = slice(j * BLK, (j + 1) * BLK)
                add = send_buf[j, rows, :].astype(F32) + recv_buf[j, rows, :].astype(F32)
                h = (h_buf[rows, cols].astype(F32) + add).astype(BF)
                h_buf[rows, cols] = h
                wide = h.astype(F32)
                total += wide * wide
            scale_rows(rows, at(r, 32), total, mgain_buf)
        loop(HALF // 32, h_step)
        pl.semaphore_signal(free_sem.at[s], inc=1, device_id=peer, device_id_type=MESH)

        def gu_step(j):
            slot = gate_slot(j)
            load_gate(j).wait()
            gate = jnp.dot(n_buf[:HALF, :], ring[ring_rows(slot, gu_slots), :], preferred_element_type=F32)
            load_up(j).wait()
            up = jnp.dot(n_buf[:HALF, :], ring[ring_rows(slot + gu_slots, gu_slots), :], preferred_element_type=F32)
            act_buf[:, at(j, BLK)] = (gate / (1.0 + jnp.exp(-gate)) * up).astype(BF)

            @pl.when(j + gu_deep < n_gu)
            def _():
                load_gate(j + gu_deep).start()
                load_up(j + gu_deep).start()
            freed = 0
            for back in range(gu_deep, 0, -1):
                now = (2 * gu_slots * (gu_deep - back + 1)) // d_slots

                @pl.when(j == n_gu - back)
                def _():
                    for d in range(freed, now):
                        load_down(d).start()
                freed = now
        loop(n_gu, gu_step)
        pl.semaphore_wait(free_sem.at[s], 1)

        def down_step(j):
            load_down(j).wait()
            w = ring[ring_rows(lax.rem(j, d_deep) * d_slots, d_slots), :]
            send_buf[j, at(s, HALF), :] = jnp.dot(act_buf[...], w, preferred_element_type=F32).astype(BF)
            down_copy(s, j).start()

            @pl.when(j + d_deep < n_blk)
            def _():
                load_down(j + d_deep).start()
            freed = 0
            for back in range(d_deep, 0, -1):
                now = d_slots * (d_deep - back + 1) // gu_slots

                @pl.when((j == n_blk - back) & (s == 0))
                def _():
                    for d in range(freed, now):
                        (load_gate, load_up)[d % 2](d // 2).start()
                freed = now
        loop(n_blk, down_step)
    loop(tok // HALF, half_step)

    for g in range(n_kv):
        k_out[:, g, :] = kv_buf[0, g, :, :HEAD_DIM]
        v_out[:, g, :] = kv_buf[0, g, :, HEAD_DIM:]

    def final_step(t):
        s, j = t // n_blk, lax.rem(t, n_blk)
        down_copy(s, j).wait_recv()
        rows, cols = at(s, HALF), at(j, BLK)
        add = send_buf[j, rows, :].astype(F32) + recv_buf[j, rows, :].astype(F32)
        h_buf[rows, cols] = (h_buf[rows, cols].astype(F32) + add).astype(BF)
    loop(tok // HALF * n_blk, final_step)

    loop(tok // HALF, lambda s: half_copy(s, ds_sem, pr_sem.at[s]).wait_send())
    def kv_sent(kind):
        pltpu.make_async_remote_copy(kv_buf.at[0], kv_buf.at[kind + 1], kvs_sem.at[kind], kvr_sem.at[kind, 0],
                                     device_id=pair, device_id_type=MESH).wait_send()

    @pl.when(cp < 2)
    def _():
        kv_sent(1)

    @pl.when(lax.rem(cp, 2) == 0)
    def _():
        kv_sent(0)

    @pl.when(cp >= 2)
    def _():
        kv_sent(2)


def fused_layer(tab, attn_gain, mlp_gain, x, w_q, w_k, w_v, w_o, w_gate, w_up, w_down):
    tok, width = x.shape
    qcols, kcols, ff = w_q.shape[1], w_k.shape[1], w_gate.shape[1]
    n_blk, n_kv, halves = width // BLK, kcols // HEAD_DIM, tok // HALF
    stacked = CHUNK * (qcols // kcols)
    dma = pltpu.SemaphoreType.DMA
    return pl.pallas_call(
        layer_kernel,
        in_specs=[ANY] * 11,
        out_specs=[VMEM] * 3,
        out_shape=[pltpu.VMEM((tok, width), BF)] + [pltpu.VMEM((tok, n_kv, HEAD_DIM), BF)] * 2,
        scratch_shapes=[
            pltpu.VMEM((N_SLOT * SLOT, BLK), BF),
            pltpu.VMEM((n_blk, tok, BLK), BF), pltpu.VMEM((n_blk, tok, BLK), BF),
            pltpu.VMEM((tok, width), BF), pltpu.VMEM((HALF, ff), BF),
            pltpu.VMEM((4, n_kv, tok, 2 * HEAD_DIM), BF), pltpu.VMEM((tok, qcols), BF), pltpu.VMEM((CHUNK, qcols), BF),
            pltpu.VMEM((width // LANES, LANES), BF), pltpu.VMEM((width // LANES, LANES), BF),
            pltpu.VMEM((tok, HEAD_DIM), F32), pltpu.VMEM((tok, HEAD_DIM), F32), pltpu.VMEM((tok, HEAD_DIM), F32),
            pltpu.VMEM((2, 1, stacked), F32), pltpu.VMEM((2, 1, stacked), F32), pltpu.VMEM((2, HEAD_DIM, stacked), F32),
            dma((3,)), dma((tok // X_ROWS,)), dma((n_kv, 2)), dma((N_SLOT,)), dma((3,)), dma((3, n_kv)),
            dma((halves,)), dma((halves,)), dma((halves,)), dma((halves, n_blk)),
            pltpu.SemaphoreType.REGULAR((halves,))],
        compiler_params=pltpu.CompilerParams(vmem_limit_bytes=VMEM_LIMIT, collective_id=0, has_side_effects=True),
        name='fused_layer',
        cost_estimate=pl.CostEstimate(flops=2 * tok * width * (2 * qcols + 2 * kcols + 3 * ff), transcendentals=0,
                                      bytes_accessed=2 * width * (2 * qcols + 2 * kcols + 6 * ff)),
    )(tab, attn_gain, mlp_gain, x, w_q, w_k, w_v, w_o, w_gate, w_up, w_down)


def emit_kernel(y_ref, k_ref, v_ref, x_out, k_out, v_out, sem):
    copies = [pltpu.make_async_copy(y_ref.at[at(i, CHUNK), :], x_out.at[at(i, CHUNK), :], sem.at[i]) for i in range(y_ref.shape[0] // CHUNK)]
    copies += [pltpu.make_async_copy(k_ref, k_out, sem.at[len(copies)]), pltpu.make_async_copy(v_ref, v_out, sem.at[len(copies) + 1])]
    for c in copies:
        c.start()
    for c in copies:
        c.wait()


def emit(*results):
    here = [pltpu.with_memory_space_constraint(r, pltpu.VMEM) for r in results]
    return pl.pallas_call(
        emit_kernel, in_specs=[VMEM] * 3, out_specs=[ANY] * 3,
        out_shape=[jax.ShapeDtypeStruct(r.shape, r.dtype) for r in results],
        scratch_shapes=[pltpu.SemaphoreType.DMA((results[0].shape[0] // CHUNK + 2,))],
        compiler_params=pltpu.CompilerParams(vmem_limit_bytes=1 << 20), name='emit',
    )(*here)


def solution(mesh):
    row_spec = P(('dp', 'cp'), None)
    cache_spec = P(('dp', 'cp'), 'tp', None)
    col_spec = P(None, 'tp')
    split_rows = P('tp', None)
    vec_spec = P(None)

    def local_layer(x, attn_gain, w_q, w_k, w_v, w_o, mlp_gain, w_gate, w_up, w_down):
        tok, width = x.shape
        tab = jnp.asarray(rope_table(tok * mesh.shape['cp']))
        gains = [g.reshape(width // LANES, LANES) for g in (attn_gain, mlp_gain)]
        return tuple(emit(*fused_layer(tab, *gains, x, w_q, w_k, w_v, w_o, w_gate, w_up, w_down)))

    return jax.shard_map(local_layer, mesh=mesh,
                         in_specs=(row_spec, vec_spec, col_spec, col_spec, col_spec, split_rows, vec_spec, col_spec, col_spec, split_rows),
                         out_specs=(row_spec, cache_spec, cache_spec), check_vma=False)
```

time: 232 us -> 217 us (0.935)
  Pallas kernels: 229 us -> 216 us
    pallas_call x2, Pallas kernels: 229 us -> 216 us  [the longest x1 214 us: fused_layer(): pl.pallas_call(layer_kernel, in_specs=[ANY] * 11, out_specs=[VMEM] * 3, o...]
where the time goes in v4:
time: 217 us
  Pallas kernels  216 us (100%)
    pallas_call x1, Pallas kernels, fused_layer(): pl.pallas_call(layer_kernel, in_specs=[ANY] * 11, out_specs=[VMEM] * 3, o...  214 us

profile of v4, /device:TPU:3, one launch (start us, length us, event | category | flops | bytes accessed | tf_op | source)
XLA Modules:
  0.0 216.9 jit_solution(13500818535056084265)
XLA Ops:
  0.6 213.7 %fused_layer.1 = (bf16[512,4096]{1,0:T(8,128)(2,1)S(1)}, bf16[512,4,128]{2,1,0:T(4,128)(2,1)S(1)}, bf16[512,4,128]{2,1,0:T(4,128)(2,1)S(1)}) custom-call(f32[2048,128]{1,0:T(8,128)} %constant.2.clone.tab_ref, bf16[32,128]{1,0:T(8,128)(2,1)} %bitcast.2, bf16[32,128]{1,0:T(8,128)(2,1)} %bitcast.3, bf16[512,4096]{1,0:T(8,128)(2,1)} %x_ref.1, ...), custom_call_target="tpu_custom_call" | custom-call | flops 98784247808 | bytes 343932928 | tf_op jit(solution)/shard_map/fused_layer/pallas_call | solution.py:418
  214.4 2.4 %emit.1 = (bf16[512,4096]{1,0:T(8,128)(2,1)}, bf16[512,4,128]{2,1,0:T(4,128)(2,1)}, bf16[512,4,128]{2,1,0:T(4,128)(2,1)}) custom-call(bf16[512,4096]{1,0:T(8,128)(2,1)S(1)} %get-tuple-element.6.y_ref, bf16[512,4,128]{2,1,0:T(4,128)(2,1)S(1)} %get-tuple-element.7.k_ref, bf16[512,4,128]{2,1,0:T(4,128)(2,1)S(1)} %get-tuple-element.8.v_ref), custom_call_target="tpu_custom_call" | custom-call | tf_op jit(solution)/shard_map/emit/pallas_call | solution.py:452

commit v5 on v4

--- a/solution.py
+++ b/solution.py
@@ -23,6 +23,7 @@
 SLOT = 2048
 X_ROWS = 64
 KV_ROWS = 128
+N_RELAY = 2
 N_SLOT = 12
 VMEM_LIMIT = 60000000
 
@@ -46,12 +47,13 @@
 
 def layer_kernel(tab_ref, again_ref, mgain_ref, x_ref, wq_ref, wk_ref, wv_ref, wo_ref, wg_ref, wu_ref, wd_ref,
                  h_buf, k_out, v_out,
-                 ring, send_buf, recv_buf, n_buf, act_buf, kv_buf, q_buf, o_buf, again_buf, mgain_buf, tab_buf, cos_buf, sin_buf, m_sc, l_sc, acc_sc,
-                 tab_sem, x_sem, wkv_sem, w_sem, kvs_sem, kvr_sem, ps_sem, pr_sem, ds_sem, dr_sem, free_sem):
+                 ring, send_buf, recv_buf, relay_buf, n_buf, act_buf, kv_buf, q_buf, o_buf, again_buf, mgain_buf, tab_buf, cos_buf, sin_buf, m_sc, l_sc, acc_sc,
+                 tab_sem, x_sem, wkv_sem, w_sem, kvs_sem, kvr_sem, ps_sem, pr_sem, ds_sem, dr_sem, relay_sem, free_sem):
     cp = lax.axis_index('cp')
     peer = {'tp': 1 - lax.axis_index('tp')}
     pair = {'cp': cp + 1 - 2 * lax.rem(cp, 2)}
     across = {'cp': lax.rem(cp + 2, 4)}
+    diagonal = {'tp': 1 - lax.axis_index('tp'), 'cp': lax.rem(cp + 2, 4)}
     tok, width = n_buf.shape
     n_blk = width // BLK
     n_gu = wg_ref.shape[1] // BLK
@@ -73,8 +75,11 @@
     def load_q(u):
         return load(wq_ref.at[:, at(u, BLK)], kv_slots + gu_slots * u, gu_slots)
 
+    def wo_slot(t):
+        return jnp.where(t < n_blk, lax.rem(t, kv_slots), lax.rem(t, N_SLOT))
+
     def load_wo(t):
-        return load(wo_ref.at[:, at(lax.rem(t, n_blk), BLK)], lax.rem(t, N_SLOT), 1)
+        return load(wo_ref.at[:, at(lax.rem(t, n_blk), BLK)], wo_slot(t), 1)
 
     def gate_slot(j):
         return lax.rem(j, gu_deep) * 2 * gu_slots
@@ -88,10 +93,14 @@
     def load_down(j):
         return load(wd_ref.at[:, at(j, BLK)], lax.rem(j, d_deep) * d_slots, d_slots)
 
-    def load_kv(g, which):
+    def load_kv(u, which, part):
         src = (wk_ref, wv_ref)[which]
-        cols = at(lax.rem(g, 2) * 2 + which, HEAD_DIM)
-        return pltpu.make_async_copy(src.at[:, at(g, HEAD_DIM)], ring.at[ring_rows(g // 2 * gu_slots, gu_slots), cols], wkv_sem.at[g, which])
+        rows = pl.ds(part * (width // 2), width // 2)
+        dst = ring.at[pl.ds(u * gu_slots * SLOT + part * (width // 2), width // 2), pl.ds(which * 2 * HEAD_DIM, 2 * HEAD_DIM)]
+        return pltpu.make_async_copy(src.at[rows, pl.ds(u * 2 * HEAD_DIM, 2 * HEAD_DIM)], dst, wkv_sem.at[u, which, part])
+
+    def all_kv(u):
+        return [load_kv(u, which, part) for part in range(2) for which in range(2)]
 
     def load_x(i):
         return pltpu.make_async_copy(x_ref.at[at(i, X_ROWS), :], h_buf.at[at(i, X_ROWS), :], x_sem.at[i])
@@ -109,6 +118,17 @@
         return pltpu.make_async_remote_copy(send_buf.at[piece], recv_buf.at[piece], ps_sem.at[i * CHUNK // HALF], pr_sem.at[i * CHUNK // HALF],
                                             device_id=peer, device_id_type=MESH)
 
+    def relay_piece(j):
+        return (n_blk - N_RELAY + j, slice(0, CHUNK), slice(None))
+
+    def relay_copy(j):
+        return pltpu.make_async_remote_copy(send_buf.at[relay_piece(j)], relay_buf.at[j], ps_sem.at[0], relay_sem.at[0],
+                                            device_id=diagonal, device_id_type=MESH)
+
+    def forward_copy(j):
+        return pltpu.make_async_remote_copy(relay_buf.at[j], recv_buf.at[relay_piece(j)], relay_sem.at[1], pr_sem.at[0],
+                                            device_id=across, device_id_type=MESH)
+
     def down_copy(s, j):
         piece = (j, at(s, HALF), slice(None))
         return pltpu.make_async_remote_copy(send_buf.at[piece], recv_buf.at[piece], ds_sem.at[s], dr_sem.at[s, j],
@@ -130,24 +150,19 @@
         u = prod.astype(BF).astype(F32)
         return (u * cos_buf[rows, :] + pltpu.roll(u, HEAD_DIM // 2, 1) * sin_buf[rows, :]).astype(BF)
 
-    small = [pltpu.make_async_copy(again_ref, again_buf, tab_sem.at[0]), pltpu.make_async_copy(mgain_ref, mgain_buf, tab_sem.at[1]),
-             pltpu.make_async_copy(tab_ref.at[at(cp, tok), :], tab_buf, tab_sem.at[2])]
-    for c in small:
+    barrier = pltpu.get_barrier_semaphore()
+    for other in (peer, pair, across, diagonal):
+        pl.semaphore_signal(barrier, inc=1, device_id=other, device_id_type=MESH)
+
+    gain_copy = pltpu.make_async_copy(again_ref, again_buf, tab_sem.at[0])
+    small = [pltpu.make_async_copy(mgain_ref, mgain_buf, tab_sem.at[1]), pltpu.make_async_copy(tab_ref.at[at(cp, tok), :], tab_buf, tab_sem.at[2])]
+    gain_copy.start()
+    first_rows = KV_ROWS // X_ROWS
+    loop(first_rows, lambda i: load_x(i).start())
+    for c in small + all_kv(0):
         c.start()
-    first_rows = 2 * KV_ROWS // X_ROWS
-    loop(first_rows, lambda i: load_x(i).start())
-    for g in range(2):
-        for which in range(2):
-            load_kv(g, which).start()
     lax.fori_loop(first_rows, tok // X_ROWS, lambda i, c: (load_x(i).start(), c)[1], 0)
-    barrier = pltpu.get_barrier_semaphore()
-    for other in (peer, pair, across):
-        pl.semaphore_signal(barrier, inc=1, device_id=other, device_id_type=MESH)
-    for c in small:
-        c.wait()
-    cos, sin = tab_buf[:, :HEAD_DIM // 2], tab_buf[:, HEAD_DIM // 2:]
-    cos_buf[...] = jnp.concatenate([cos, cos], axis=1)
-    sin_buf[...] = jnp.concatenate([-sin, sin], axis=1)
+    gain_copy.wait()
 
     def norm_step(i):
         load_x(i).wait()
@@ -171,28 +186,38 @@
 
         @pl.when(t == 0)
         def _():
-            pl.semaphore_wait(barrier, 3)
+            for c in small:
+                c.wait()
+            cos, sin = tab_buf[:, :HEAD_DIM // 2], tab_buf[:, HEAD_DIM // 2:]
+            cos_buf[...] = jnp.concatenate([cos, cos], axis=1)
+            sin_buf[...] = jnp.concatenate([-sin, sin], axis=1)
 
         @pl.when(t == 1)
         def _():
-            for g in range(2, n_kv):
-                for which in range(2):
-                    load_kv(g, which).start()
+            for u in range(1, n_kv // 2):
+                for c in all_kv(u):
+                    c.start()
             for u in range(n_q):
                 load_q(u).start()
 
         @pl.when(r == 0)
         def _():
-            for e in range(2):
-                for which in range(2):
-                    load_kv(2 * pair_heads + e, which).wait()
+            for u in range(n_kv // 2):
+                @pl.when(pair_heads == u)
+                def _():
+                    for c in all_kv(u):
+                        c.wait()
         prod = jnp.dot(n_buf[rows, :], ring[ring_rows(pair_heads * gu_slots, gu_slots), :], preferred_element_type=F32)
         for e in range(2):
             g = 2 * pair_heads + e
-            col = e * 2 * HEAD_DIM
+            col = e * HEAD_DIM
             kv_buf[0, g, rows, :HEAD_DIM] = rope(prod[:, col:col + HEAD_DIM], rows)
-            kv_buf[0, g, rows, HEAD_DIM:] = prod[:, col + HEAD_DIM:col + 2 * HEAD_DIM].astype(BF)
-
+            kv_buf[0, g, rows, HEAD_DIM:] = prod[:, col + 2 * HEAD_DIM:col + 3 * HEAD_DIM].astype(BF)
+
+
+        @pl.when(t == 0)
+        def _():
+            pl.semaphore_wait(barrier, 4)
 
         def send_kv(*piece):
             @pl.when(cp < 2)
@@ -211,15 +236,25 @@
     for t in range(kv_slots):
         load_wo(t).start()
 
-    def q_step(u):
+    def q_rows(u, row, n):
+        w = ring[ring_rows(kv_slots + gu_slots * u, gu_slots), :]
+        prod = jnp.dot(n_buf[row:row + n, :], w, preferred_element_type=F32)
+        for j in range(BLK // HEAD_DIM):
+            cols = pl.ds(pl.multiple_of(u * BLK + j * HEAD_DIM, HEAD_DIM), HEAD_DIM)
+            q_buf[row:row + n, cols] = rope(prod[:, j * HEAD_DIM:(j + 1) * HEAD_DIM], slice(row, row + n))
+
+    def q_first(u):
         load_q(u).wait()
-        w = ring[ring_rows(kv_slots + gu_slots * u, gu_slots), :]
-        prod = jnp.dot(n_buf[...], w, preferred_element_type=F32)
-        for j in range(BLK // HEAD_DIM):
-            q_buf[:, pl.ds(pl.multiple_of(u * BLK + j * HEAD_DIM, HEAD_DIM), HEAD_DIM)] = rope(prod[:, j * HEAD_DIM:(j + 1) * HEAD_DIM], slice(None))
-        for t in range(gu_slots):
-            load_wo(kv_slots + gu_slots * u + t).start()
-    loop(n_q, q_step)
+        q_rows(u, 0, CHUNK)
+    loop(n_q, q_first)
+
+    def q_rest(u, c):
+        q_rows(u, CHUNK, tok - CHUNK)
+        for e in range(gu_slots):
+            t = kv_slots + gu_slots * u + e
+            load_wo(jnp.where(t < n_blk, t + N_SLOT, t)).start()
+        return c
+    q_early = jnp.where(cp >= 2, n_q - 1, 0)
 
     lo = jnp.where(cp == 2, 2, 1)
     hi = jnp.where(cp == 0, 1, jnp.where(cp == 1, 2, 4))
@@ -288,15 +323,30 @@
                 out = acc_sc[e] / l_sc[e]
                 for j in range(groups):
                     o_buf[:, at(g * groups + j, HEAD_DIM)] = out[:, j * CHUNK:(j + 1) * CHUNK].T.astype(BF)
+            if i == 0:
+                lax.fori_loop(jnp.where(step == 0, 0, q_early), q_early, q_rest, 0)
         loop(n_kv // n_heads, head_step)
 
         def wo_step(j):
             t = i * n_blk + j
             load_wo(t).wait()
-            w = ring[ring_rows(lax.rem(t, N_SLOT), 1), :]
+            w = ring[ring_rows(wo_slot(t), 1), :]
             send_buf[j, row0:row0 + CHUNK, :] = jnp.dot(o_buf[...], w, preferred_element_type=F32).astype(BF)
-            part_copy(i, j).start()
-            if (i + 1) * n_blk - 1 + N_SLOT < n_chunk * n_blk:
+            if i > 0:
+                part_copy(i, j).start()
+            else:
+                relayed = (cp >= 2) & (j >= n_blk - N_RELAY)
+
+                @pl.when(relayed)
+                def _():
+                    relay_copy(j - (n_blk - N_RELAY)).start()
+
+                @pl.when(jnp.logical_not(relayed))
+                def _():
+                    part_copy(i, j).start()
+            if i == 0:
+                load_wo(jnp.where(j < kv_slots, t + kv_slots, t + n_blk)).start()
+            elif (i + 1) * n_blk - 1 + N_SLOT < n_chunk * n_blk:
                 load_wo(t + N_SLOT).start()
             else:
                 @pl.when(t + N_SLOT < n_chunk * n_blk)
@@ -314,8 +364,15 @@
                         def _():
                             (load_gate, load_up)[which](b).start()
         loop(n_blk, wo_step)
+        if i == 0:
+            lax.fori_loop(q_early, n_q, q_rest, 0)
 
     def half_step(s):
+        @pl.when((s == 0) & (cp < 2))
+        def _():
+            pltpu.make_async_remote_copy(relay_buf, relay_buf, relay_sem.at[1], relay_sem.at[0], device_id=across, device_id_type=MESH).wait_recv()
+            for j in range(N_RELAY):
+                forward_copy(j).start()
         parts = half_copy(s, ps_sem, pr_sem.at[s])
         parts.wait_recv()
         parts.wait_send()
@@ -399,6 +456,7 @@
     @pl.when(cp < 2)
     def _():
         kv_sent(1)
+        pltpu.make_async_remote_copy(relay_buf, relay_buf, relay_sem.at[1], relay_sem.at[0], device_id=across, device_id_type=MESH).wait_send()
 
     @pl.when(lax.rem(cp, 2) == 0)
     def _():
@@ -422,14 +480,14 @@
         out_shape=[pltpu.VMEM((tok, width), BF)] + [pltpu.VMEM((tok, n_kv, HEAD_DIM), BF)] * 2,
         scratch_shapes=[
             pltpu.VMEM((N_SLOT * SLOT, BLK), BF),
-            pltpu.VMEM((n_blk, tok, BLK), BF), pltpu.VMEM((n_blk, tok, BLK), BF),
+            pltpu.VMEM((n_blk, tok, BLK), BF), pltpu.VMEM((n_blk, tok, BLK), BF), pltpu.VMEM((N_RELAY, CHUNK, BLK), BF),
             pltpu.VMEM((tok, width), BF), pltpu.VMEM((HALF, ff), BF),
             pltpu.VMEM((4, n_kv, tok, 2 * HEAD_DIM), BF), pltpu.VMEM((tok, qcols), BF), pltpu.VMEM((CHUNK, qcols), BF),
             pltpu.VMEM((width // LANES, LANES), BF), pltpu.VMEM((width // LANES, LANES), BF),
             pltpu.VMEM((tok, HEAD_DIM), F32), pltpu.VMEM((tok, HEAD_DIM), F32), pltpu.VMEM((tok, HEAD_DIM), F32),
             pltpu.VMEM((2, 1, stacked), F32), pltpu.VMEM((2, 1, stacked), F32), pltpu.VMEM((2, HEAD_DIM, stacked), F32),
-            dma((3,)), dma((tok // X_ROWS,)), dma((n_kv, 2)), dma((N_SLOT,)), dma((3,)), dma((3, n_kv)),
-            dma((halves,)), dma((halves,)), dma((halves,)), dma((halves, n_blk)),
+            dma((3,)), dma((tok // X_ROWS,)), dma((n_kv // 2, 2, 2)), dma((N_SLOT,)), dma((3,)), dma((3, n_kv)),
+            dma((halves,)), dma((halves,)), dma((halves,)), dma((halves, n_blk)), dma((2,)),
             pltpu.SemaphoreType.REGULAR((halves,))],
         compiler_params=pltpu.CompilerParams(vmem_limit_bytes=VMEM_LIMIT, collective_id=0, has_side_effects=True),
         name='fused_layer',

time: 217 us -> 211 us (0.972)
  Pallas kernels: 216 us -> 210 us
    pallas_call x1, Pallas kernels: 214 us -> 208 us  [fused_layer(): pl.pallas_call(layer_kernel, in_specs=[ANY] * 11, out_specs=[VMEM] * 3, o...]
where the time goes in v5:
time: 211 us
  Pallas kernels  210 us (100%)
    pallas_call x1, Pallas kernels, fused_layer(): pl.pallas_call(layer_kernel, in_specs=[ANY] * 11, out_specs=[VMEM] * 3, o...  208 us

profile of v5, /device:TPU:3, one launch (start us, length us, event | category | flops | bytes accessed | tf_op | source)
XLA Modules:
  0.0 211.0 jit_solution(6366390526294197336)
XLA Ops:
  0.6 207.8 %fused_layer.1 = (bf16[512,4096]{1,0:T(8,128)(2,1)S(1)}, bf16[512,4,128]{2,1,0:T(4,128)(2,1)S(1)}, bf16[512,4,128]{2,1,0:T(4,128)(2,1)S(1)}) custom-call(f32[2048,128]{1,0:T(8,128)} %constant.2.clone.tab_ref, bf16[32,128]{1,0:T(8,128)(2,1)} %bitcast.2, bf16[32,128]{1,0:T(8,128)(2,1)} %bitcast.3, bf16[512,4096]{1,0:T(8,128)(2,1)} %x_ref.1, ...), custom_call_target="tpu_custom_call" | custom-call | flops 98784247808 | bytes 343932928 | tf_op jit(solution)/shard_map/fused_layer/pallas_call | solution.py:476
  208.5 2.4 %emit.1 = (bf16[512,4096]{1,0:T(8,128)(2,1)}, bf16[512,4,128]{2,1,0:T(4,128)(2,1)}, bf16[512,4,128]{2,1,0:T(4,128)(2,1)}) custom-call(bf16[512,4096]{1,0:T(8,128)(2,1)S(1)} %get-tuple-element.6.y_ref, bf16[512,4,128]{2,1,0:T(4,128)(2,1)S(1)} %get-tuple-element.7.k_ref, bf16[512,4,128]{2,1,0:T(4,128)(2,1)S(1)} %get-tuple-element.8.v_ref), custom_call_target="tpu_custom_call" | custom-call | tf_op jit(solution)/shard_map/emit/pallas_call | solution.py:510

commit v6 on v5

--- a/solution.py
+++ b/solution.py
@@ -23,7 +23,9 @@
 SLOT = 2048
 X_ROWS = 64
 KV_ROWS = 128
-N_RELAY = 2
+N_RELAY = 5
+UNIT = 64
+KV_PARTS = 2
 N_SLOT = 12
 VMEM_LIMIT = 60000000
 
@@ -95,12 +97,13 @@
 
     def load_kv(u, which, part):
         src = (wk_ref, wv_ref)[which]
-        rows = pl.ds(part * (width // 2), width // 2)
-        dst = ring.at[pl.ds(u * gu_slots * SLOT + part * (width // 2), width // 2), pl.ds(which * 2 * HEAD_DIM, 2 * HEAD_DIM)]
+        n = width // KV_PARTS
+        rows = pl.ds(part * n, n)
+        dst = ring.at[pl.ds(u * gu_slots * SLOT + part * n, n), pl.ds(which * 2 * HEAD_DIM, 2 * HEAD_DIM)]
         return pltpu.make_async_copy(src.at[rows, pl.ds(u * 2 * HEAD_DIM, 2 * HEAD_DIM)], dst, wkv_sem.at[u, which, part])
 
     def all_kv(u):
-        return [load_kv(u, which, part) for part in range(2) for which in range(2)]
+        return [load_kv(u, which, part) for part in range(KV_PARTS) for which in range(2)]
 
     def load_x(i):
         return pltpu.make_async_copy(x_ref.at[at(i, X_ROWS), :], h_buf.at[at(i, X_ROWS), :], x_sem.at[i])
@@ -118,15 +121,22 @@
         return pltpu.make_async_remote_copy(send_buf.at[piece], recv_buf.at[piece], ps_sem.at[i * CHUNK // HALF], pr_sem.at[i * CHUNK // HALF],
                                             device_id=peer, device_id_type=MESH)
 
-    def relay_piece(j):
-        return (n_blk - N_RELAY + j, slice(0, CHUNK), slice(None))
-
-    def relay_copy(j):
-        return pltpu.make_async_remote_copy(send_buf.at[relay_piece(j)], relay_buf.at[j], ps_sem.at[0], relay_sem.at[0],
+    per_piece = CHUNK // UNIT
+    first_relay = n_blk * per_piece - N_RELAY
+
+    def unit(g):
+        return (g // per_piece, at(lax.rem(g, per_piece), UNIT), slice(None))
+
+    def unit_copy(g):
+        return pltpu.make_async_remote_copy(send_buf.at[unit(g)], recv_buf.at[unit(g)], ps_sem.at[0], pr_sem.at[0],
+                                            device_id=peer, device_id_type=MESH)
+
+    def relay_copy(g):
+        return pltpu.make_async_remote_copy(send_buf.at[unit(g)], relay_buf.at[g - first_relay], ps_sem.at[0], relay_sem.at[0],
                                             device_id=diagonal, device_id_type=MESH)
 
-    def forward_copy(j):
-        return pltpu.make_async_remote_copy(relay_buf.at[j], recv_buf.at[relay_piece(j)], relay_sem.at[1], pr_sem.at[0],
+    def forward_copy(g):
+        return pltpu.make_async_remote_copy(relay_buf.at[g - first_relay], recv_buf.at[unit(g)], relay_sem.at[1], pr_sem.at[0],
                                             device_id=across, device_id_type=MESH)
 
     def down_copy(s, j):
@@ -176,63 +186,55 @@
 
     n_quarter = tok // KV_ROWS
 
-    def kv_step(t):
-        pair_heads, r = t // n_quarter, lax.rem(t, n_quarter)
-        rows = at(r, KV_ROWS)
-
-        @pl.when(t < n_quarter)
+    def send_kv(*piece):
+        @pl.when(cp < 2)
         def _():
-            lax.fori_loop(r * (KV_ROWS // X_ROWS), (r + 1) * (KV_ROWS // X_ROWS), lambda i, c: (norm_step(i), c)[1], 0)
-
-        @pl.when(t == 0)
+            kv_copy(1, *piece).start()
+
+        @pl.when(lax.rem(cp, 2) == 0)
+        def _():
+            kv_copy(0, *piece).start()
+
+    def kv_rows(u, rows):
+        prod = jnp.dot(n_buf[rows, :], ring[ring_rows(u * gu_slots, gu_slots), :], preferred_element_type=F32)
+        for e in range(2):
+            kv_buf[0, 2 * u + e, rows, :HEAD_DIM] = rope(prod[:, e * HEAD_DIM:(e + 1) * HEAD_DIM], rows)
+            kv_buf[0, 2 * u + e, rows, HEAD_DIM:] = prod[:, (e + 2) * HEAD_DIM:(e + 3) * HEAD_DIM].astype(BF)
+
+    def kv_step(r):
+        lax.fori_loop(r * (KV_ROWS // X_ROWS), (r + 1) * (KV_ROWS // X_ROWS), lambda i, c: (norm_step(i), c)[1], 0)
+
+        @pl.when(r == 0)
         def _():
             for c in small:
                 c.wait()
             cos, sin = tab_buf[:, :HEAD_DIM // 2], tab_buf[:, HEAD_DIM // 2:]
             cos_buf[...] = jnp.concatenate([cos, cos], axis=1)
             sin_buf[...] = jnp.concatenate([-sin, sin], axis=1)
-
-        @pl.when(t == 1)
+            for c in all_kv(0):
+                c.wait()
+
+        @pl.when(r == 1)
         def _():
             for u in range(1, n_kv // 2):
                 for c in all_kv(u):
                     c.start()
             for u in range(n_q):
                 load_q(u).start()
+        kv_rows(0, at(r, KV_ROWS))
 
         @pl.when(r == 0)
         def _():
-            for u in range(n_kv // 2):
-                @pl.when(pair_heads == u)
-                def _():
-                    for c in all_kv(u):
-                        c.wait()
-        prod = jnp.dot(n_buf[rows, :], ring[ring_rows(pair_heads * gu_slots, gu_slots), :], preferred_element_type=F32)
-        for e in range(2):
-            g = 2 * pair_heads + e
-            col = e * HEAD_DIM
-            kv_buf[0, g, rows, :HEAD_DIM] = rope(prod[:, col:col + HEAD_DIM], rows)
-            kv_buf[0, g, rows, HEAD_DIM:] = prod[:, col + 2 * HEAD_DIM:col + 3 * HEAD_DIM].astype(BF)
-
-
-        @pl.when(t == 0)
-        def _():
             pl.semaphore_wait(barrier, 4)
-
-        def send_kv(*piece):
-            @pl.when(cp < 2)
-            def _():
-                kv_copy(1, *piece).start()
-
-            @pl.when(lax.rem(cp, 2) == 0)
-            def _():
-                kv_copy(0, *piece).start()
-        send_kv(2 * pair_heads, r, KV_ROWS)
-
-        @pl.when(r == n_quarter - 1)
-        def _():
-            send_kv(2 * pair_heads + 1)
-    loop(n_kv // 2 * n_quarter, kv_step)
+        send_kv(0, r, KV_ROWS)
+    loop(n_quarter, kv_step)
+    send_kv(1)
+    for u in range(1, n_kv // 2):
+        for c in all_kv(u):
+            c.wait()
+        kv_rows(u, slice(None))
+        send_kv(2 * u)
+        send_kv(2 * u + 1)
     for t in range(kv_slots):
         load_wo(t).start()
 
@@ -335,15 +337,20 @@
             if i > 0:
                 part_copy(i, j).start()
             else:
-                relayed = (cp >= 2) & (j >= n_blk - N_RELAY)
-
-                @pl.when(relayed)
-                def _():
-                    relay_copy(j - (n_blk - N_RELAY)).start()
-
-                @pl.when(jnp.logical_not(relayed))
+                @pl.when(cp < 2)
                 def _():
                     part_copy(i, j).start()
+
+                for e in range(per_piece):
+                    g = j * per_piece + e
+
+                    @pl.when((cp >= 2) & (g < first_relay))
+                    def _():
+                        unit_copy(g).start()
+
+                    @pl.when((cp >= 2) & (g >= first_relay))
+                    def _():
+                        relay_copy(g).start()
             if i == 0:
                 load_wo(jnp.where(j < kv_slots, t + kv_slots, t + n_blk)).start()
             elif (i + 1) * n_blk - 1 + N_SLOT < n_chunk * n_blk:
@@ -371,8 +378,7 @@
         @pl.when((s == 0) & (cp < 2))
         def _():
             pltpu.make_async_remote_copy(relay_buf, relay_buf, relay_sem.at[1], relay_sem.at[0], device_id=across, device_id_type=MESH).wait_recv()
-            for j in range(N_RELAY):
-                forward_copy(j).start()
+            loop(N_RELAY, lambda k: forward_copy(first_relay + k).start())
         parts = half_copy(s, ps_sem, pr_sem.at[s])
         parts.wait_recv()
         parts.wait_send()
@@ -480,13 +486,13 @@
         out_shape=[pltpu.VMEM((tok, width), BF)] + [pltpu.VMEM((tok, n_kv, HEAD_DIM), BF)] * 2,
         scratch_shapes=[
             pltpu.VMEM((N_SLOT * SLOT, BLK), BF),
-            pltpu.VMEM((n_blk, tok, BLK), BF), pltpu.VMEM((n_blk, tok, BLK), BF), pltpu.VMEM((N_RELAY, CHUNK, BLK), BF),
+            pltpu.VMEM((n_blk, tok, BLK), BF), pltpu.VMEM((n_blk, tok, BLK), BF), pltpu.VMEM((N_RELAY, UNIT, BLK), BF),
             pltpu.VMEM((tok, width), BF), pltpu.VMEM((HALF, ff), BF),
             pltpu.VMEM((4, n_kv, tok, 2 * HEAD_DIM), BF), pltpu.VMEM((tok, qcols), BF), pltpu.VMEM((CHUNK, qcols), BF),
             pltpu.VMEM((width // LANES, LANES), BF), pltpu.VMEM((width // LANES, LANES), BF),
             pltpu.VMEM((tok, HEAD_DIM), F32), pltpu.VMEM((tok, HEAD_DIM), F32), pltpu.VMEM((tok, HEAD_DIM), F32),
             pltpu.VMEM((2, 1, stacked), F32), pltpu.VMEM((2, 1, stacked), F32), pltpu.VMEM((2, HEAD_DIM, stacked), F32),
-            dma((3,)), dma((tok // X_ROWS,)), dma((n_kv // 2, 2, 2)), dma((N_SLOT,)), dma((3,)), dma((3, n_kv)),
+            dma((3,)), dma((tok // X_ROWS,)), dma((n_kv // 2, 2, KV_PARTS)), dma((N_SLOT,)), dma((3,)), dma((3, n_kv)),
             dma((halves,)), dma((halves,)), dma((halves,)), dma((halves, n_blk)), dma((2,)),
             pltpu.SemaphoreType.REGULAR((halves,))],
         compiler_params=pltpu.CompilerParams(vmem_limit_bytes=VMEM_LIMIT, collective_id=0, has_side_effects=True),

time: 211 us -> 210 us (level)
  no operation moved by 1% of the time
where the time goes in v6:
time: 210 us
  Pallas kernels  209 us (100%)
    pallas_call x1, Pallas kernels, fused_layer(): pl.pallas_call(layer_kernel, in_specs=[ANY] * 11, out_specs=[VMEM] * 3, o...  207 us

profile of v6, /device:TPU:3, one launch (start us, length us, event | category | flops | bytes accessed | tf_op | source)
XLA Modules:
  0.0 209.9 jit_solution(2778616075046005738)
XLA Ops:
  0.6 206.7 %fused_layer.1 = (bf16[512,4096]{1,0:T(8,128)(2,1)S(1)}, bf16[512,4,128]{2,1,0:T(4,128)(2,1)S(1)}, bf16[512,4,128]{2,1,0:T(4,128)(2,1)S(1)}) custom-call(f32[2048,128]{1,0:T(8,128)} %constant.2.clone.tab_ref, bf16[32,128]{1,0:T(8,128)(2,1)} %bitcast.2, bf16[32,128]{1,0:T(8,128)(2,1)} %bitcast.3, bf16[512,4096]{1,0:T(8,128)(2,1)} %x_ref.1, ...), custom_call_target="tpu_custom_call" | custom-call | flops 98784247808 | bytes 343932928 | tf_op jit(solution)/shard_map/fused_layer/pallas_call | solution.py:482
  207.3 2.4 %emit.1 = (bf16[512,4096]{1,0:T(8,128)(2,1)}, bf16[512,4,128]{2,1,0:T(4,128)(2,1)}, bf16[512,4,128]{2,1,0:T(4,128)(2,1)}) custom-call(bf16[512,4096]{1,0:T(8,128)(2,1)S(1)} %get-tuple-element.6.y_ref, bf16[512,4,128]{2,1,0:T(4,128)(2,1)S(1)} %get-tuple-element.7.k_ref, bf16[512,4,128]{2,1,0:T(4,128)(2,1)S(1)} %get-tuple-element.8.v_ref), custom_call_target="tpu_custom_call" | custom-call | tf_op jit(solution)/shard_map/emit/pallas_call | solution.py:516

commit v7 on v6

--- a/solution.py
+++ b/solution.py
@@ -28,6 +28,7 @@
 KV_PARTS = 2
 N_SLOT = 12
 VMEM_LIMIT = 60000000
+EMIT_ROWS = 512
 
 
 def at(i, size):
@@ -116,6 +117,13 @@
                                             kvs_sem.at[kind], kvr_sem.at[kind, g],
                                             device_id=across if kind == 1 else pair, device_id_type=MESH)
 
+    def kv_half(kind, g, r):
+        src_block = 2 if kind == 2 else 0
+        rows = pl.ds(r * HALF, HALF)
+        return pltpu.make_async_remote_copy(kv_buf.at[src_block, g, rows, :], kv_buf.at[kind + 1, g, rows, :],
+                                            kvs_sem.at[kind], kvr_sem.at[kind if kind == 2 or r == 0 else 3, g],
+                                            device_id=across if kind == 1 else pair, device_id_type=MESH)
+
     def part_copy(i, j):
         piece = (j, at(i, CHUNK), slice(None))
         return pltpu.make_async_remote_copy(send_buf.at[piece], recv_buf.at[piece], ps_sem.at[i * CHUNK // HALF], pr_sem.at[i * CHUNK // HALF],
@@ -189,7 +197,11 @@
     def send_kv(*piece):
         @pl.when(cp < 2)
         def _():
-            kv_copy(1, *piece).start()
+            if len(piece) == 1 and piece[0] % 2:
+                for r in range(tok // HALF):
+                    kv_half(1, piece[0], r).start()
+            else:
+                kv_copy(1, *piece).start()
 
         @pl.when(lax.rem(cp, 2) == 0)
         def _():
@@ -256,7 +268,7 @@
             t = kv_slots + gu_slots * u + e
             load_wo(jnp.where(t < n_blk, t + N_SLOT, t)).start()
         return c
-    q_early = jnp.where(cp >= 2, n_q - 1, 0)
+    q_early = jnp.where(cp >= 2, n_q - 2, 0)
 
     lo = jnp.where(cp == 2, 2, 1)
     hi = jnp.where(cp == 0, 1, jnp.where(cp == 1, 2, 4))
@@ -303,7 +315,9 @@
 
                     @pl.when(b == 2)
                     def _():
-                        pass_on(heads[1])
+                        for r in range(tok // HALF):
+                            kv_half(1, heads[1], r).wait_recv()
+                            kv_half(2, heads[1], r).start()
 
                     @pl.when(b == 3)
                     def _():
@@ -492,7 +506,7 @@
             pltpu.VMEM((width // LANES, LANES), BF), pltpu.VMEM((width // LANES, LANES), BF),
             pltpu.VMEM((tok, HEAD_DIM), F32), pltpu.VMEM((tok, HEAD_DIM), F32), pltpu.VMEM((tok, HEAD_DIM), F32),
             pltpu.VMEM((2, 1, stacked), F32), pltpu.VMEM((2, 1, stacked), F32), pltpu.VMEM((2, HEAD_DIM, stacked), F32),
-            dma((3,)), dma((tok // X_ROWS,)), dma((n_kv // 2, 2, KV_PARTS)), dma((N_SLOT,)), dma((3,)), dma((3, n_kv)),
+            dma((3,)), dma((tok // X_ROWS,)), dma((n_kv // 2, 2, KV_PARTS)), dma((N_SLOT,)), dma((3,)), dma((4, n_kv)),
             dma((halves,)), dma((halves,)), dma((halves,)), dma((halves, n_blk)), dma((2,)),
             pltpu.SemaphoreType.REGULAR((halves,))],
         compiler_params=pltpu.CompilerParams(vmem_limit_bytes=VMEM_LIMIT, collective_id=0, has_side_effects=True),
@@ -503,7 +517,7 @@
 
 
 def emit_kernel(y_ref, k_ref, v_ref, x_out, k_out, v_out, sem):
-    copies = [pltpu.make_async_copy(y_ref.at[at(i, CHUNK), :], x_out.at[at(i, CHUNK), :], sem.at[i]) for i in range(y_ref.shape[0] // CHUNK)]
+    copies = [pltpu.make_async_copy(y_ref.at[at(i, EMIT_ROWS), :], x_out.at[at(i, EMIT_ROWS), :], sem.at[i]) for i in range(y_ref.shape[0] // EMIT_ROWS)]
     copies += [pltpu.make_async_copy(k_ref, k_out, sem.at[len(copies)]), pltpu.make_async_copy(v_ref, v_out, sem.at[len(copies) + 1])]
     for c in copies:
         c.start()
@@ -516,7 +530,7 @@
     return pl.pallas_call(
         emit_kernel, in_specs=[VMEM] * 3, out_specs=[ANY] * 3,
         out_shape=[jax.ShapeDtypeStruct(r.shape, r.dtype) for r in results],
-        scratch_shapes=[pltpu.SemaphoreType.DMA((results[0].shape[0] // CHUNK + 2,))],
+        scratch_shapes=[pltpu.SemaphoreType.DMA((results[0].shape[0] // EMIT_ROWS + 2,))],
         compiler_params=pltpu.CompilerParams(vmem_limit_bytes=1 << 20), name='emit',
     )(*here)
 

time: 210 us -> 210 us (level)
  no operation moved by 1% of the time
where the time goes in v7:
time: 210 us
  Pallas kernels  209 us (100%)
    pallas_call x1, Pallas kernels, fused_layer(): pl.pallas_call(layer_kernel, in_specs=[ANY] * 11, out_specs=[VMEM] * 3, o...  207 us

profile of v7, /device:TPU:3, one launch (start us, length us, event | category | flops | bytes accessed | tf_op | source)
XLA Modules:
  0.0 209.7 jit_solution(3702116825828771421)
XLA Ops:
  0.6 206.5 %fused_layer.1 = (bf16[512,4096]{1,0:T(8,128)(2,1)S(1)}, bf16[512,4,128]{2,1,0:T(4,128)(2,1)S(1)}, bf16[512,4,128]{2,1,0:T(4,128)(2,1)S(1)}) custom-call(f32[2048,128]{1,0:T(8,128)} %constant.2.clone.tab_ref, bf16[32,128]{1,0:T(8,128)(2,1)} %bitcast.2, bf16[32,128]{1,0:T(8,128)(2,1)} %bitcast.3, bf16[512,4096]{1,0:T(8,128)(2,1)} %x_ref.1, ...), custom_call_target="tpu_custom_call" | custom-call | flops 98784247808 | bytes 343932928 | tf_op jit(solution)/shard_map/fused_layer/pallas_call | solution.py:496
  207.1 2.4 %emit.1 = (bf16[512,4096]{1,0:T(8,128)(2,1)}, bf16[512,4,128]{2,1,0:T(4,128)(2,1)}, bf16[512,4,128]{2,1,0:T(4,128)(2,1)}) custom-call(bf16[512,4096]{1,0:T(8,128)(2,1)S(1)} %get-tuple-element.6.y_ref, bf16[512,4,128]{2,1,0:T(4,128)(2,1)S(1)} %get-tuple-element.7.k_ref, bf16[512,4,128]{2,1,0:T(4,128)(2,1)S(1)} %get-tuple-element.8.v_ref), custom_call_target="tpu_custom_call" | custom-call | tf_op jit(solution)/shard_map/emit/pallas_call | solution.py:530

commit v8 on v7

--- a/solution.py
+++ b/solution.py
@@ -177,7 +177,7 @@
     gain_copy.start()
     first_rows = KV_ROWS // X_ROWS
     loop(first_rows, lambda i: load_x(i).start())
-    for c in small + all_kv(0):
+    for c in all_kv(0) + small:
         c.start()
     lax.fori_loop(first_rows, tok // X_ROWS, lambda i, c: (load_x(i).start(), c)[1], 0)
     gain_copy.wait()
@@ -207,15 +207,15 @@
         def _():
             kv_copy(0, *piece).start()
 
-    def kv_rows(u, rows):
+    def kv_rows(u, rows, before_rope=None):
         prod = jnp.dot(n_buf[rows, :], ring[ring_rows(u * gu_slots, gu_slots), :], preferred_element_type=F32)
+        if before_rope is not None:
+            before_rope()
         for e in range(2):
             kv_buf[0, 2 * u + e, rows, :HEAD_DIM] = rope(prod[:, e * HEAD_DIM:(e + 1) * HEAD_DIM], rows)
             kv_buf[0, 2 * u + e, rows, HEAD_DIM:] = prod[:, (e + 2) * HEAD_DIM:(e + 3) * HEAD_DIM].astype(BF)
 
-    def kv_step(r):
-        lax.fori_loop(r * (KV_ROWS // X_ROWS), (r + 1) * (KV_ROWS // X_ROWS), lambda i, c: (norm_step(i), c)[1], 0)
-
+    def build_tables(r):
         @pl.when(r == 0)
         def _():
             for c in small:
@@ -223,6 +223,12 @@
             cos, sin = tab_buf[:, :HEAD_DIM // 2], tab_buf[:, HEAD_DIM // 2:]
             cos_buf[...] = jnp.concatenate([cos, cos], axis=1)
             sin_buf[...] = jnp.concatenate([-sin, sin], axis=1)
+
+    def kv_step(r):
+        lax.fori_loop(r * (KV_ROWS // X_ROWS), (r + 1) * (KV_ROWS // X_ROWS), lambda i, c: (norm_step(i), c)[1], 0)
+
+        @pl.when(r == 0)
+        def _():
             for c in all_kv(0):
                 c.wait()
 
@@ -233,7 +239,7 @@
                     c.start()
             for u in range(n_q):
                 load_q(u).start()
-        kv_rows(0, at(r, KV_ROWS))
+        kv_rows(0, at(r, KV_ROWS), lambda: build_tables(r))
 
         @pl.when(r == 0)
         def _():

time: 210 us -> 210 us (level)
  no operation moved by 1% of the time
where the time goes in v8:
time: 210 us
  Pallas kernels  209 us (100%)
    pallas_call x1, Pallas kernels, fused_layer(): pl.pallas_call(layer_kernel, in_specs=[ANY] * 11, out_specs=[VMEM] * 3, o...  207 us

profile of v8, /device:TPU:3, one launch (start us, length us, event | category | flops | bytes accessed | tf_op | source)
XLA Modules:
  0.0 209.8 jit_solution(8526274674661430553)
XLA Ops:
  0.6 206.6 %fused_layer.1 = (bf16[512,4096]{1,0:T(8,128)(2,1)S(1)}, bf16[512,4,128]{2,1,0:T(4,128)(2,1)S(1)}, bf16[512,4,128]{2,1,0:T(4,128)(2,1)S(1)}) custom-call(f32[2048,128]{1,0:T(8,128)} %constant.2.clone.tab_ref, bf16[32,128]{1,0:T(8,128)(2,1)} %bitcast.2, bf16[32,128]{1,0:T(8,128)(2,1)} %bitcast.3, bf16[512,4096]{1,0:T(8,128)(2,1)} %x_ref.1, ...), custom_call_target="tpu_custom_call" | custom-call | flops 98784247808 | bytes 343932928 | tf_op jit(solution)/shard_map/fused_layer/pallas_call | solution.py:502
  207.3 2.4 %emit.1 = (bf16[512,4096]{1,0:T(8,128)(2,1)}, bf16[512,4,128]{2,1,0:T(4,128)(2,1)}, bf16[512,4,128]{2,1,0:T(4,128)(2,1)}) custom-call(bf16[512,4096]{1,0:T(8,128)(2,1)S(1)} %get-tuple-element.6.y_ref, bf16[512,4,128]{2,1,0:T(4,128)(2,1)S(1)} %get-tuple-element.7.k_ref, bf16[512,4,128]{2,1,0:T(4,128)(2,1)S(1)} %get-tuple-element.8.v_ref), custom_call_target="tpu_custom_call" | custom-call | tf_op jit(solution)/shard_map/emit/pallas_call | solution.py:536
